TPU v7x, 32 devices: a 4x4x1 block of a 4x4x8 slice. The times are simulated.
32 devices in a mesh: dp: 1 (over z), ch: 4 (over y), wd: 8 (over x, core).
Axes of the slice: x: 4, y: 4, z: 1, core: 2. Of those that a mesh axis runs over, the one named last changes fastest.
The devices are a block of a 4x4x8 slice.
Arguments:
- resid_in: bfloat16 [4096, 4096], P('dp', 'wd')
- seg_pos: int32 [1, 4096], P('dp')
- gain_temporal: bfloat16 [4096], P('wd')
- w_x: bfloat16 [4096, 4096], P('wd', 'ch')
- bias_x: bfloat16 [4096], P('ch')
- w_y: bfloat16 [4096, 4096], P('wd', 'ch')
- bias_y: bfloat16 [4096], P('ch')
- conv_w: bfloat16 [4, 4096], P(None, 'ch')
- conv_bias: bfloat16 [4096], P('ch')
- lam_param: float32 [4096], P('ch')
- rgate_w: bfloat16 [16, 256, 256], P('ch')
- rgate_b: bfloat16 [4096], P('ch')
- igate_w: bfloat16 [16, 256, 256], P('ch')
- igate_b: bfloat16 [4096], P('ch')
- w_o: bfloat16 [4096, 4096], P('ch', 'wd')
- bias_o: bfloat16 [4096], P('wd')
- gain_mlp: bfloat16 [4096], P('wd')
- w_g: bfloat16 [4096, 12288], P('wd', 'ch')
- bias_g: bfloat16 [12288], P('ch')
- w_u: bfloat16 [4096, 12288], P('wd', 'ch')
- bias_u: bfloat16 [12288], P('ch')
- w_d: bfloat16 [12288, 4096], P('ch', 'wd')
- bias_d: bfloat16 [4096], P('wd')
Outputs:
- output: bfloat16 [4096, 4096], P('dp', 'wd')
All inputs are finite; a program needn't handle non-finite values.
Results may differ from a plain program's by a relative error of at most 0.0128771.
Values are sent between devices in bfloat16 or wider.
A program may use at most 768 MiB of HBM per device.

v0:
```python
import jax
import jax.numpy as jnp
from jax import lax
from jax.sharding import PartitionSpec as P, NamedSharding

EPS = 1e-6


def rms_apply(vals, sum_sq, width, gain):
    return (vals * lax.rsqrt(sum_sq / width + EPS) * (1.0 + gain.astype(jnp.float32))).astype(jnp.bfloat16)


def token_sum(part_sum, axis_name, count):
    tokens, width = part_sum.shape
    pieces = part_sum.astype(jnp.bfloat16).reshape(count, tokens // count, width)
    received = lax.all_to_all(pieces, axis_name, 0, 0)
    return jnp.sum(received.astype(jnp.float32), axis=0)


def conv_mix(vals, positions, conv_w, conv_bias):
    vals32 = vals.astype(jnp.float32)
    taps = conv_w.astype(jnp.float32)
    total = conv_bias.astype(jnp.float32) + vals32 * taps[0]
    for shift in range(1, conv_w.shape[0]):
        moved = jnp.pad(vals32[:-shift], ((shift, 0), (0, 0)))
        total = total + jnp.where((positions >= shift)[:, None], moved, 0.0) * taps[shift]
    return total.astype(jnp.bfloat16)


def combine(left, right):
    return left[0] * right[0], right[0] * left[1] + right[1]


def rg_lru(conv_out, positions, seqs, lam_param, rgate_w, rgate_b, igate_w, igate_b):
    tokens, width = conv_out.shape
    blocks = rgate_w.shape[0]
    grouped = conv_out.reshape(tokens, blocks, width // blocks)
    rate = jax.nn.sigmoid(jnp.einsum('nbi,bij->nbj', grouped, rgate_w, preferred_element_type=jnp.float32).reshape(tokens, width) + rgate_b.astype(jnp.float32))
    inflow = jax.nn.sigmoid(jnp.einsum('nbi,bij->nbj', grouped, igate_w, preferred_element_type=jnp.float32).reshape(tokens, width) + igate_b.astype(jnp.float32))
    log_a = -8.0 * rate * jax.nn.softplus(-lam_param)
    reset = (positions == 0)[:, None]
    decay = jnp.where(reset, 0.0, jnp.exp(log_a))
    scale = jnp.where(reset, 1.0, jnp.sqrt(-jnp.expm1(2.0 * log_a)))
    drive = scale * inflow * conv_out.astype(jnp.float32)
    steps = tokens // seqs
    hidden = lax.associative_scan(combine, (decay.reshape(seqs, steps, width), drive.reshape(seqs, steps, width)), axis=1)[1]
    return hidden.reshape(tokens, width)


def solution(mesh):
    wd_count = mesh.shape['wd']
    ch_count = mesh.shape['ch']
    row_spec = P('dp', 'wd')
    specs = (row_spec, P('dp', None), P('wd'), P('wd', 'ch'), P('ch'), P('wd', 'ch'), P('ch'), P(None, 'ch'), P('ch'), P('ch'), P('ch', None, None), P('ch'), P('ch', None, None), P('ch'), P('ch', 'wd'), P('wd'), P('wd'), P('wd', 'ch'), P('ch'), P('wd', 'ch'), P('ch'), P('ch', 'wd'), P('wd'))

    def local_layer(resid_in, seg_pos, gain_temporal, w_x, bias_x, w_y, bias_y, conv_w, conv_bias, lam_param, rgate_w, rgate_b, igate_w, igate_b, w_o, bias_o, gain_mlp, w_g, bias_g, w_u, bias_u, w_d, bias_d):
        tokens, local_width = resid_in.shape
        model_width = local_width * wd_count
        share = tokens // ch_count
        positions = seg_pos.reshape(tokens)
        resid32 = resid_in.astype(jnp.float32)
        sum_sq = lax.psum(jnp.sum(resid32 * resid32, axis=1, keepdims=True), 'wd')
        normed = rms_apply(resid32, sum_sq, model_width, gain_temporal)
        y_sum = token_sum(jnp.dot(normed, w_y, preferred_element_type=jnp.float32), 'wd', wd_count)
        y_rows = jax.nn.gelu(y_sum + bias_y.astype(jnp.float32), approximate=True).astype(jnp.bfloat16)
        y_branch = lax.all_gather(y_rows, 'wd', axis=0, tiled=True)
        u_sum = token_sum(jnp.dot(normed, w_x, preferred_element_type=jnp.float32), 'wd', wd_count)
        u_rows = (u_sum + bias_x.astype(jnp.float32)).astype(jnp.bfloat16)
        u_branch = lax.all_gather(u_rows, 'wd', axis=0, tiled=True)
        conv_out = conv_mix(u_branch, positions, conv_w, conv_bias)
        hidden = rg_lru(conv_out, positions, seg_pos.shape[0], lam_param, rgate_w, rgate_b, igate_w, igate_b)
        mixed = (hidden * y_branch.astype(jnp.float32)).astype(jnp.bfloat16)
        mix_sum = token_sum(jnp.dot(mixed, w_o, preferred_element_type=jnp.float32), 'ch', ch_count)
        resid_rows = lax.dynamic_slice_in_dim(resid32, lax.axis_index('ch') * share, share, axis=0)
        resid = resid_rows + mix_sum + bias_o.astype(jnp.float32)
        sum_sq2 = lax.psum(jnp.sum(resid * resid, axis=1, keepdims=True), 'wd')
        normed2 = lax.all_gather(rms_apply(resid, sum_sq2, model_width, gain_mlp), 'ch', axis=0, tiled=True)
        gate_sum = token_sum(jnp.dot(normed2, w_g, preferred_element_type=jnp.float32), 'wd', wd_count)
        up_sum = token_sum(jnp.dot(normed2, w_u, preferred_element_type=jnp.float32), 'wd', wd_count)
        inner_rows = (jax.nn.gelu(gate_sum + bias_g.astype(jnp.float32), approximate=True) * (up_sum + bias_u.astype(jnp.float32))).astype(jnp.bfloat16)
        inner = lax.all_gather(inner_rows, 'wd', axis=0, tiled=True)
        down_sum = token_sum(jnp.dot(inner, w_d, preferred_element_type=jnp.float32), 'ch', ch_count)
        out_rows = (resid + down_sum + bias_d.astype(jnp.float32)).astype(jnp.bfloat16)
        return lax.all_gather(out_rows, 'ch', axis=0, tiled=True)

    return jax.shard_map(local_layer, mesh=mesh, in_specs=specs, out_specs=row_spec, check_vma=False)
```

profile of v0, /device:TPU:97, one launch (start us, length us, event | category | flops | bytes accessed | tf_op | source)
XLA Modules:
  0.0 2366.4 jit_solution(15899565636020944906)
XLA Ops:
  10.6 24.0 %psum.14 = f32[4096,1]{0,1:T(1,128)S(1)} all-reduce(f32[4096,1]{0,1:T(1,128)S(1)} %bitcast.56), channel_id=1, replica_groups=mesh['dp'=1,'ch'=4,'wd'=8] {'wd'}, use_global_device_ids=true, to_apply=%region_1.0 | all-reduce | flops 4096 | bytes 32768 | tf_op jit(solution)/shard_map/psum | solution.py:62
  53.7 93.4 %all-to-all-done = bf16[8,512,1024]{2,1,0:T(8,128)(2,1)} async-done(((bf16[8,512,1024]{2,1,0:T(8,128)(2,1)}), bf16[8,512,1024]{2,1,0:T(8,128)(2,1)}, u32[]{:S(2)}, u32[]{:S(2)}) %all-to-all-start) | async-done | bytes 8388640 | tf_op jit(solution)/shard_map/all_to_all | solution.py:16
  171.1 120.1 %all-to-all-done.1 = bf16[8,512,1024]{2,1,0:T(8,128)(2,1)} async-done(((bf16[8,512,1024]{2,1,0:T(8,128)(2,1)}), bf16[8,512,1024]{2,1,0:T(8,128)(2,1)}, u32[]{:S(2)}, u32[]{:S(2)}) %all-to-all-start.1) | async-done | bytes 8388640 | tf_op jit(solution)/shard_map/all_to_all | solution.py:16
  332.5 24.7 %add_convert_fusion = bf16[4096,1024]{1,0:T(8,128)(2,1)} fusion(f32[4093,1024]{1,0:T(8,128)} %slice.403, f32[4094,1024]{1,0:T(8,128)} %slice.401, f32[4095,1024]{1,0:T(8,128)} %slice.399, f32[1024]{0:T(1024)S(1)} %bitcast.64, f32[1024]{0:T(1024)S(1)} %bitcast.63, f32[1024]{0:T(1024)S(1)} %bitcast.62, f32[1024]{0:T(1024)S(1)} %bitcast.61, ...), kind=kLoop, calls=%fused_computation.9 | loop fusion | flops 54525952 | bytes 67117056 | tf_op jit(solution)/shard_map/convert_element_type | solution.py:27
  357.2 11.4 copy.30
  368.6 11.5 fusion.50
  380.2 17.5 copy.37
  397.6 14.2 exponential_select_fusion
  411.8 36.5 %slice.308 = f32[1,2047,1024]{2,1,0:T(8,128)} slice(f32[1,4096,1024]{2,1,0:T(8,128)} %exponential_select_fusion), slice={[0:1:1], [2:4096:2], [0:1024:1]} | slice | bytes 16769024 | tf_op jit(solution)/shard_map/slice | solution.py:46
  448.4 35.9 %slice.313 = f32[1,2048,1024]{2,1,0:T(8,128)} slice(f32[1,4096,1024]{2,1,0:T(8,128)} %exponential_select_fusion), slice={[0:1:1], [0:4095:2], [0:1024:1]} | slice | bytes 16777216 | tf_op jit(solution)/shard_map/slice | solution.py:46
  484.3 35.9 %slice.309 = f32[1,2048,1024]{2,1,0:T(8,128)} slice(f32[1,4096,1024]{2,1,0:T(8,128)} %exponential_select_fusion), slice={[0:1:1], [1:4096:2], [0:1024:1]} | slice | bytes 16777216 | tf_op jit(solution)/shard_map/slice | solution.py:46
  520.2 11.6 fusion.51
  531.7 17.5 copy.36
  549.2 17.5 copy.33
  566.6 25.8 %multiply_bitcast_fusion = f32[1,4096,1024]{2,1,0:T(8,128)} fusion(bf16[4096,1024]{1,0:T(8,128)(2,1)} %add_convert_fusion, f32[4096,1024]{1,0:T(8,128)} %copy.36, f32[4096,1024]{1,0:T(8,128)} %copy.33, f32[1024]{0:T(1024)S(1)} %convert_element_type.126, f32[1024]{0:T(1024)S(1)} %fusion.35, f32[1024]{0:T(1024)S(1)} %convert_element_type.125, ...), kind=kLoop, calls=%fused_computation.8 | loop fusion | flops 62914560 | bytes 58736640 | tf_op jit(solution)/shard_map/reshape | solution.py:46
  592.4 36.5 %slice.397 = f32[1,2047,1024]{2,1,0:T(8,128)} slice(f32[1,4096,1024]{2,1,0:T(8,128)} %multiply_bitcast_fusion), slice={[0:1:1], [2:4096:2], [0:1024:1]} | slice | bytes 16769024 | tf_op jit(solution)/shard_map/slice | solution.py:46
  628.9 35.9 %slice.311 = f32[1,2048,1024]{2,1,0:T(8,128)} slice(f32[1,4096,1024]{2,1,0:T(8,128)} %multiply_bitcast_fusion), slice={[0:1:1], [1:4096:2], [0:1024:1]} | slice | bytes 16777216 | tf_op jit(solution)/shard_map/slice | solution.py:46
  664.9 35.9 %slice.310 = f32[1,2048,1024]{2,1,0:T(8,128)} slice(f32[1,4096,1024]{2,1,0:T(8,128)} %multiply_bitcast_fusion), slice={[0:1:1], [0:4095:2], [0:1024:1]} | slice | bytes 16777216 | tf_op jit(solution)/shard_map/slice | solution.py:46
  700.7 18.7 fusion.37
  719.4 18.5 slice.319
  737.9 18.5 slice.315
  756.4 18.4 slice.317
  774.8 18.4 slice.316
  793.3 12.2 fusion.38
  992.3 18.9 slice.395
  1011.2 18.8 slice.314
  1099.6 16.5 pad.106
  1116.0 16.5 pad.107
  1139.4 32.4 %pad.109 = f32[1,2048,1024]{2,1,0:T(8,128)} pad(f32[1,1024,1024]{2,1,0:T(8,128)} %add.370, f32[]{:T(128)} %constant.21.clone.1), padding=0_0_0x1_0_1x0_0_0 | pad | bytes 12582916 | tf_op jit(solution)/shard_map/pad | solution.py:46
  1182.2 32.3 %pad.108 = f32[1,2048,1024]{2,1,0:T(8,128)} pad(f32[1,1024,1024]{2,1,0:T(8,128)} %pad_maximum_fusion.1, f32[]{:T(128)} %constant.21.clone.1), padding=0_0_0x0_1_1x0_0_0 | pad | bytes 12582916 | tf_op jit(solution)/shard_map/pad | solution.py:46
  1214.5 12.0 add.372
  1226.5 12.7 fusion.3
  1243.5 64.1 %pad.110 = f32[1,4096,1024]{2,1,0:T(8,128)} pad(f32[1,2048,1024]{2,1,0:T(8,128)} %pad_maximum_fusion, f32[]{:T(128)} %constant.21.clone.1), padding=0_0_0x0_1_1x0_0_0 | pad | bytes 25165828 | tf_op jit(solution)/shard_map/pad | solution.py:46
  1307.5 64.1 %pad.111 = f32[1,4096,1024]{2,1,0:T(8,128)} pad(f32[1,2048,1024]{2,1,0:T(8,128)} %add.372, f32[]{:T(128)} %constant.21.clone.1), padding=0_0_0x1_0_1x0_0_0 | pad | bytes 25165828 | tf_op jit(solution)/shard_map/pad | solution.py:46
  1371.7 17.4 fusion.13
  1400.9 41.2 %all-to-all-done.2 = bf16[4,1024,512]{2,1,0:T(8,128)(2,1)} async-done(((bf16[4,1024,512]{2,1,0:T(8,128)(2,1)}), bf16[4,1024,512]{2,1,0:T(8,128)(2,1)}, u32[]{:S(2)}, u32[]{:S(2)}) %all-to-all-start.2) | async-done | bytes 4194336 | tf_op jit(solution)/shard_map/all_to_all | solution.py:16
  1448.5 13.4 psum.15
  1464.8 42.7 %all-gather.10.cloned.1.call-done = bf16[4096,512]{1,0:T(8,128)(2,1)} async-done(((bf16[1024,512]{1,0:T(8,128)(2,1)}), bf16[4096,512]{1,0:T(8,128)(2,1)}) %all-gather.10.cloned.1.call-update) | async-done | bytes 4194320 | tf_op jit(solution)/shard_map/all_gather | solution.py:77
  1507.5 19.6 convolution_convert_fusion
  1534.3 20.7 convolution_convert_fusion.1
  1555.0 252.7 %all-to-all-done.4 = bf16[8,512,3072]{2,1,0:T(8,128)(2,1)} async-done(((bf16[8,512,3072]{2,1,0:T(8,128)(2,1)}), bf16[8,512,3072]{2,1,0:T(8,128)(2,1)}, u32[]{:S(2)}, u32[]{:S(2)}) %all-to-all-start.4) | async-done | bytes 25165856 | tf_op jit(solution)/shard_map/all_to_all | solution.py:16
  1815.2 16.8 convert_reduce_fusion
  1832.0 256.5 %all-to-all-done.3 = bf16[8,512,3072]{2,1,0:T(8,128)(2,1)} async-done(((bf16[8,512,3072]{2,1,0:T(8,128)(2,1)}), bf16[8,512,3072]{2,1,0:T(8,128)(2,1)}, u32[]{:S(2)}, u32[]{:S(2)}) %all-to-all-start.3) | async-done | bytes 25165856 | tf_op jit(solution)/shard_map/all_to_all | solution.py:16
  2088.5 16.4 convert_reduce_fusion.1
  2112.1 117.7 %all-gather.12.cloned.1.call-done = bf16[4096,3072]{1,0:T(8,128)(2,1)} async-done(((bf16[512,3072]{1,0:T(8,128)(2,1)}), bf16[4096,3072]{1,0:T(8,128)(2,1)}) %all-gather.12.cloned.1.call-update) | async-done | bytes 25165840 | tf_op jit(solution)/shard_map/all_gather | solution.py:81
  2229.8 20.2 convolution_convert_fusion.4
  2255.2 48.3 %all-to-all-done.5 = bf16[4,1024,512]{2,1,0:T(8,128)(2,1)} async-done(((bf16[4,1024,512]{2,1,0:T(8,128)(2,1)}), bf16[4,1024,512]{2,1,0:T(8,128)(2,1)}, u32[]{:S(2)}, u32[]{:S(2)}) %all-to-all-start.5) | async-done | bytes 4194336 | tf_op jit(solution)/shard_map/all_to_all | solution.py:16
  2309.9 45.0 %all-gather.14.cloned.1.call-done = bf16[4096,512]{1,0:T(8,128)(2,1)} async-done(((bf16[1024,512]{1,0:T(8,128)(2,1)}), bf16[4096,512]{1,0:T(8,128)(2,1)}) %all-gather.14.cloned.1.call-update) | async-done | bytes 4194320 | tf_op jit(solution)/shard_map/all_gather | solution.py:84
  (229 shorter events, 424.6 us)
Async XLA Ops:
  6.5 1501.0 %copy-start = (bf16[512,3072]{1,0:T(8,128)(2,1)S(1)}, bf16[512,3072]{1,0:T(8,128)(2,1)}, u32[]{:S(2)}) copy-start(bf16[512,3072]{1,0:T(8,128)(2,1)} %param.42) | copy-start | bytes 9437188
  44.9 8.7 copy-start.21
  44.9 102.1 %all-to-all-start = ((bf16[8,512,1024]{2,1,0:T(8,128)(2,1)}), bf16[8,512,1024]{2,1,0:T(8,128)(2,1)}, u32[]{:S(2)}, u32[]{:S(2)}) async-start(bf16[8,512,1024]{2,1,0:T(8,128)(2,1)} %bitcast.54), calls=%async_computation | async-start | bytes 16777216 | tf_op jit(solution)/shard_map/all_to_all | solution.py:16
  53.5 245.2 %all-gather.6.cloned.1.call-start = ((), (), s32[]{:S(2)}) async-start(), calls=%async_computation.6 | async-start | bytes 9437184 | tf_op jit(solution)/shard_map/all_gather | solution.py:69
  164.3 6.4 copy-start.22
  164.3 6.4 copy-start.23
  164.3 6.4 copy-start.24
  164.3 6.4 copy-start.25
  164.3 6.5 copy-start.17
  164.4 6.6 copy-start.20
  164.4 6.7 copy-start.7
  164.4 126.8 %all-to-all-start.1 = ((bf16[8,512,1024]{2,1,0:T(8,128)(2,1)}), bf16[8,512,1024]{2,1,0:T(8,128)(2,1)}, u32[]{:S(2)}, u32[]{:S(2)}) async-start(bf16[8,512,1024]{2,1,0:T(8,128)(2,1)} %bitcast.53), calls=%async_computation.1 | async-start | bytes 16777216 | tf_op jit(solution)/shard_map/all_to_all | solution.py:16
  170.5 1201.2 %all-gather.8.cloned.1.call-start = ((), (), s32[]{:S(2)}) async-start(), calls=%async_computation.7 | async-start | bytes 9437184 | tf_op jit(solution)/shard_map/all_gather | solution.py:66
  992.2 40.4 %copy-start.6 = (f32[1,2,1024]{2,1,0:T(2,128)S(1)}, f32[1,2,1024]{2,1,0:T(2,128)}, u32[]{:S(2)}) copy-start(f32[1,2,1024]{2,1,0:T(2,128)} %slice.369) | copy-start | bytes 24580
  992.2 40.4 %copy-start.8 = (f32[1,2,1024]{2,1,0:T(2,128)S(1)}, f32[1,2,1024]{2,1,0:T(2,128)}, u32[]{:S(2)}) copy-start(f32[1,2,1024]{2,1,0:T(2,128)} %slice.371) | copy-start | bytes 24580
  992.2 40.4 %copy-start.9 = (f32[1,2,1024]{2,1,0:T(2,128)S(1)}, f32[1,2,1024]{2,1,0:T(2,128)}, u32[]{:S(2)}) copy-start(f32[1,2,1024]{2,1,0:T(2,128)} %slice.370) | copy-start | bytes 24580
  992.2 40.4 %copy-start.10 = (f32[1,2,1024]{2,1,0:T(2,128)S(1)}, f32[1,2,1024]{2,1,0:T(2,128)}, u32[]{:S(2)}) copy-start(f32[1,2,1024]{2,1,0:T(2,128)} %slice.373) | copy-start | bytes 24580
  992.2 41.3 %copy-start.4 = (f32[1,3,1024]{2,1,0:T(4,128)S(1)}, f32[1,3,1024]{2,1,0:T(4,128)}, u32[]{:S(2)}) copy-start(f32[1,3,1024]{2,1,0:T(4,128)} %slice.379) | copy-start | bytes 36868
  992.2 41.3 %copy-start.5 = (f32[1,3,1024]{2,1,0:T(4,128)S(1)}, f32[1,3,1024]{2,1,0:T(4,128)}, u32[]{:S(2)}) copy-start(f32[1,3,1024]{2,1,0:T(4,128)} %slice.362) | copy-start | bytes 36868
  992.3 41.4 %copy-start.16 = (f32[1,1,1024]{2,1,0:T(1,128)S(1)}, f32[1,1,1024]{2,1,0:T(1,128)}, u32[]{:S(2)}) copy-start(f32[1,1,1024]{2,1,0:T(1,128)} %slice.414) | copy-start | bytes 12292
  992.3 41.4 %copy-start.2 = (f32[1,7,1024]{2,1,0:T(8,128)S(1)}, f32[1,7,1024]{2,1,0:T(8,128)}, u32[]{:S(2)}) copy-start(f32[1,7,1024]{2,1,0:T(8,128)} %slice.356) | copy-start | bytes 86020
  992.3 41.4 %copy-start.3 = (f32[1,7,1024]{2,1,0:T(8,128)S(1)}, f32[1,7,1024]{2,1,0:T(8,128)}, u32[]{:S(2)}) copy-start(f32[1,7,1024]{2,1,0:T(8,128)} %slice.381) | copy-start | bytes 86020
  992.3 41.4 %copy-start.15 = (f32[1,1,1024]{2,1,0:T(1,128)S(1)}, f32[1,1,1024]{2,1,0:T(1,128)}, u32[]{:S(2)}) copy-start(f32[1,1,1024]{2,1,0:T(1,128)} %slice.413) | copy-start | bytes 12292
  992.3 46.7 %copy-start.1 = (f32[1,31,1024]{2,1,0:T(8,128)S(1)}, f32[1,31,1024]{2,1,0:T(8,128)}, u32[]{:S(2)}) copy-start(f32[1,31,1024]{2,1,0:T(8,128)} %slice.344) | copy-start | bytes 380932
  1054.8 24.9 %copy-start.14 = (f32[1,1,1024]{2,1,0:T(1,128)S(1)}, f32[1,1,1024]{2,1,0:T(1,128)}, u32[]{:S(2)}) copy-start(f32[1,1,1024]{2,1,0:T(1,128)} %slice.408) | copy-start | bytes 12292
  1089.3 8.5 copy-start.13
  1171.8 7.9 copy-start.12
  1226.5 12.7 copy-start.11
  1389.1 53.1 %all-to-all-start.2 = ((bf16[4,1024,512]{2,1,0:T(8,128)(2,1)}), bf16[4,1024,512]{2,1,0:T(8,128)(2,1)}, u32[]{:S(2)}, u32[]{:S(2)}) async-start(bf16[4,1024,512]{2,1,0:T(8,128)(2,1)} %bitcast.50), calls=%async_computation.2 | async-start | bytes 8388608 | tf_op jit(solution)/shard_map/all_to_all | solution.py:16
  1394.1 6.8 copy-start.26
  1394.1 6.8 copy-start.27
  1394.1 113.4 %all-gather.10.cloned.1.call-start = ((), (), s32[]{:S(2)}) async-start(), calls=%async_computation.8 | async-start | bytes 5242880 | tf_op jit(solution)/shard_map/all_gather | solution.py:77
  1527.1 280.6 %all-to-all-start.4 = ((bf16[8,512,3072]{2,1,0:T(8,128)(2,1)}), bf16[8,512,3072]{2,1,0:T(8,128)(2,1)}, u32[]{:S(2)}, u32[]{:S(2)}) async-start(bf16[8,512,3072]{2,1,0:T(8,128)(2,1)} %bitcast.52), calls=%async_computation.4 | async-start | bytes 50331648 | tf_op jit(solution)/shard_map/all_to_all | solution.py:16
  1807.7 7.5 copy-start.18
  1807.7 7.5 copy-start.19
  1807.7 280.9 %all-to-all-start.3 = ((bf16[8,512,3072]{2,1,0:T(8,128)(2,1)}), bf16[8,512,3072]{2,1,0:T(8,128)(2,1)}, u32[]{:S(2)}, u32[]{:S(2)}) async-start(bf16[8,512,3072]{2,1,0:T(8,128)(2,1)} %bitcast.51), calls=%async_computation.3 | async-start | bytes 50331648 | tf_op jit(solution)/shard_map/all_to_all | solution.py:16
  1815.2 414.7 %all-gather.12.cloned.1.call-start = ((), (), s32[]{:S(2)}) async-start(), calls=%async_computation.9 | async-start | bytes 28311552 | tf_op jit(solution)/shard_map/all_gather | solution.py:81
  2250.0 5.2 copy-start.28
  2250.1 53.5 %all-to-all-start.5 = ((bf16[4,1024,512]{2,1,0:T(8,128)(2,1)}), bf16[4,1024,512]{2,1,0:T(8,128)(2,1)}, u32[]{:S(2)}, u32[]{:S(2)}) async-start(bf16[4,1024,512]{2,1,0:T(8,128)(2,1)} %bitcast.55), calls=%async_computation.5 | async-start | bytes 8388608 | tf_op jit(solution)/shard_map/all_to_all | solution.py:16
  2255.1 99.8 %all-gather.14.cloned.1.call-start = ((), (), s32[]{:S(2)}) async-start(), calls=%async_computation.10 | async-start | bytes 5242880 | tf_op jit(solution)/shard_map/all_gather | solution.py:84
Sparse Core Ops, SparseCore 0:
  154.2 87.0 all-gather.5
  298.8 47.4 all-gather.7
  1464.9 42.5 all-gather.9
  2112.3 117.5 all-gather.11
  2310.0 44.8 all-gather.13
where the time goes:
time: 2390 us; the launch traced here: 2370 us
  waiting for transfers between devices  1020 us (43%)
  local copies, waits for them, and re-layouts  859 us (36%)
  other arithmetic  276 us (12%)
  matrix products  122 us (5%)
  starting transfers between devices  40 us (2%)
  blocking collectives  37.4 us (2%)
    all_to_all x6, waiting for transfers between devices, token_sum(): received = lax.all_to_all(pieces, axis_name, 0, 0)  812 us
    slice x74, local copies, waits for them, and re-layouts, rg_lru(): lax.associative_scan(combine, (decay.reshape(seqs, steps, width), drive.r...  496 us
    pad x22, local copies, waits for them, and re-layouts, rg_lru(): lax.associative_scan(combine, (decay.reshape(seqs, steps, width), drive.r...  261 us
    all_gather x1, waiting for transfers between devices, local_layer(): inner = lax.all_gather(inner_rows, 'wd', axis=0, tiled=True)  118 us
    mul x10, other arithmetic, combine(): return (left[0] * right[0], right[0] * left[1] + right[1])  52.7 us
    reduce_sum x6, other arithmetic, token_sum(): return jnp.sum(received.astype(jnp.float32), axis=0)  50.9 us
  transfers between devices with their start and end apart: 11, of which 9 were waited for; matrix products, arithmetic and copies ran while one was open for 48% of the time, Pallas kernels for 0%

commit v1 on v0

v1 whole, which is shorter than its diff:
```python
import functools

import jax
import jax.numpy as jnp
from jax import lax
from jax.experimental import pallas as pl
from jax.experimental.pallas import tpu as pltpu
from jax.sharding import PartitionSpec as P

EPS = 1e-6
CORES = 2
SEGS = 8
PAD = 8


def rms_apply(vals, sum_sq, width, gain):
    return (vals * lax.rsqrt(sum_sq / width + EPS) * (1.0 + gain.astype(jnp.float32))).astype(jnp.bfloat16)


def neg_expm1(z):
    series = -z * (1.0 + z * (0.5 + z * (1.0 / 6.0 + z * (1.0 / 24.0))))
    return jnp.where(z > -0.03, series, 1.0 - jnp.exp(z))


def lru_kernel(u_ref, y_ref, pos_ref, taps_ref, cbias_ref, gate_w_ref, gate_b_ref, lam_ref, out_ref, u32, a_s, b_s):
    tokens, wide = u_ref.shape
    width = y_ref.shape[1]
    tile = tokens // SEGS
    pitch = tile + PAD
    taps = taps_ref[...].astype(jnp.float32)
    n_taps = taps_ref.shape[0]
    cbias = cbias_ref[...].astype(jnp.float32)
    gate_b = gate_b_ref[...].astype(jnp.float32)
    lam = -lam_ref[...]
    soft = -8.0 * (jnp.maximum(lam, 0.0) + jnp.log(1.0 + jnp.exp(-jnp.abs(lam))))
    u32[0:PAD, :] = jnp.zeros((PAD, wide), jnp.float32)

    def widen(i, carry):
        rows = pl.multiple_of(i * tile, tile)
        u32[pl.ds(rows + PAD, tile), :] = u_ref[pl.ds(rows, tile), :].astype(jnp.float32)
        return carry
    lax.fori_loop(0, SEGS, widen, 0)

    sub = tile // 4

    def gates(i, carry):
        rows = pl.multiple_of(i * sub, sub)
        window = u32[pl.ds(rows, sub + PAD), :]
        pos = pos_ref[pl.ds(rows, sub), :]
        total = cbias + window[PAD:] * taps[0:1]
        for k in range(1, n_taps):
            total = total + jnp.where(pos >= k, window[PAD - k:PAD - k + sub], 0.0) * taps[k:k + 1]
        conv = total.astype(jnp.bfloat16)
        pre = jnp.dot(conv, gate_w_ref[...], preferred_element_type=jnp.float32) + gate_b
        both = jax.nn.sigmoid(pre)
        log_a = both[:, :width] * soft
        reset = pos == 0
        decay = jnp.where(reset, 0.0, jnp.exp(log_a))
        scale = jnp.where(reset, 1.0, jnp.sqrt(neg_expm1(2.0 * log_a)))
        drive = scale * both[:, width:] * conv[:, :width].astype(jnp.float32)
        seg = i // 4
        at = pl.multiple_of(seg * pitch + (i - seg * 4) * sub, 8)
        a_s[pl.ds(at, sub), :] = decay
        b_s[pl.ds(at, sub), :] = drive
        return carry
    lax.fori_loop(0, SEGS * 4, gates, 0)

    def steps(i, carry):
        hid, acc = carry
        for j in range(8):
            t = i * 8 + j
            a = a_s[pl.ds(t, SEGS, stride=pitch), :]
            hid = a * hid + b_s[pl.ds(t, SEGS, stride=pitch), :]
            acc = a * acc
            b_s[pl.ds(t, SEGS, stride=pitch), :] = hid
            a_s[pl.ds(t, SEGS, stride=pitch), :] = acc
        return hid, acc
    hid, acc = lax.fori_loop(0, tile // 8, steps, (jnp.zeros((SEGS, width), jnp.float32), jnp.ones((SEGS, width), jnp.float32)))

    entry = jnp.zeros((1, width), jnp.float32)
    for seg in range(SEGS):
        for q in range(4):
            at = seg * pitch + q * sub
            hidden = b_s[at:at + sub, :] + a_s[at:at + sub, :] * entry
            rows = slice(seg * tile + q * sub, seg * tile + (q + 1) * sub)
            out_ref[rows, :] = (hidden * y_ref[rows, :].astype(jnp.float32)).astype(jnp.bfloat16)
        entry = hid[seg:seg + 1] + acc[seg:seg + 1] * entry


def lru(u_pair, y_rows, pos, taps, cbias, gate_w, gate_b, lam):
    tokens, wide = u_pair.shape
    width = y_rows.shape[1]
    rows = SEGS * (tokens // SEGS + PAD)
    return pl.pallas_call(
        lru_kernel,
        out_shape=jax.ShapeDtypeStruct((tokens, width), jnp.bfloat16),
        in_specs=[pl.BlockSpec(memory_space=pltpu.VMEM)] * 8,
        out_specs=pl.BlockSpec(memory_space=pltpu.VMEM),
        scratch_shapes=[pltpu.VMEM((tokens + PAD, wide), jnp.float32), pltpu.VMEM((rows, width), jnp.float32), pltpu.VMEM((rows, width), jnp.float32)],
        compiler_params=pltpu.CompilerParams(vmem_limit_bytes=48 << 20),
        name='lru',
    )(u_pair, y_rows, pos, taps, cbias, gate_w, gate_b, lam)


def gate_up_kernel(n_ref, w_ref, bias_ref, out_ref, acc):
    step = pl.program_id(2)
    half = out_ref.shape[1]
    part = jnp.dot(n_ref[0, 0], w_ref[0], preferred_element_type=jnp.float32)

    @pl.when(step == 0)
    def _():
        acc[...] = part

    @pl.when(step > 0)
    def _():
        acc[...] += part

    @pl.when(step == pl.num_programs(2) - 1)
    def _():
        bias = bias_ref[...].astype(jnp.float32)
        total = acc[...] + bias
        out_ref[...] = (jax.nn.gelu(total[:, :half], approximate=True) * total[:, half:]).astype(jnp.bfloat16)


def gate_up(normed, weight, bias):
    ch, wd, share, depth = normed.shape
    cols = weight.shape[2]
    tile = 512
    return pl.pallas_call(
        gate_up_kernel,
        grid=(ch, share // tile, wd),
        out_shape=jax.ShapeDtypeStruct((ch * share, cols // 2), jnp.bfloat16),
        in_specs=[pl.BlockSpec((1, 1, tile, depth), lambda c, t, i: (c, i, t, 0)),
                  pl.BlockSpec((1, depth, cols), lambda c, t, i: (i, 0, 0)),
                  pl.BlockSpec((1, cols), lambda c, t, i: (0, 0))],
        out_specs=pl.BlockSpec((tile, cols // 2), lambda c, t, i: (c * (share // tile) + t, 0)),
        scratch_shapes=[pltpu.VMEM((tile, cols), jnp.float32)],
        compiler_params=pltpu.CompilerParams(vmem_limit_bytes=40 << 20),
        name='gate_up',
    )(normed, weight, bias)


def down_kernel(h_ref, w_ref, out_ref, acc):
    step = pl.program_id(1)
    depth = h_ref.shape[2]
    part = jnp.dot(h_ref[0], w_ref[pl.ds(pl.multiple_of(step * depth, depth), depth), :], preferred_element_type=jnp.float32)

    @pl.when(step == 0)
    def _():
        acc[...] = part

    @pl.when(step > 0)
    def _():
        acc[...] += part

    @pl.when(step == pl.num_programs(1) - 1)
    def _():
        out_ref[...] = acc[...].astype(jnp.bfloat16)


def down(parts, weight):
    count, tokens, depth = parts.shape
    cols = weight.shape[1]
    tile = 1024
    return pl.pallas_call(
        down_kernel,
        grid=(tokens // tile, count),
        out_shape=jax.ShapeDtypeStruct((tokens, cols), jnp.bfloat16),
        in_specs=[pl.BlockSpec((1, tile, depth), lambda t, i: (i, t, 0)),
                  pl.BlockSpec(weight.shape, lambda t, i: (0, 0))],
        out_specs=pl.BlockSpec((tile, cols), lambda t, i: (t, 0)),
        scratch_shapes=[pltpu.VMEM((tile, cols), jnp.float32)],
        compiler_params=pltpu.CompilerParams(vmem_limit_bytes=40 << 20),
        name='down',
    )(parts, weight)


def solution(mesh):
    wd_count = mesh.shape['wd']
    ch_count = mesh.shape['ch']
    chips = wd_count // CORES
    row_spec = P('dp', 'wd')
    specs = (row_spec, P('dp', None), P('wd'), P('wd', 'ch'), P('ch'), P('wd', 'ch'), P('ch'), P(None, 'ch'), P('ch'), P('ch'), P('ch', None, None), P('ch'), P('ch', None, None), P('ch'), P('ch', 'wd'), P('wd'), P('wd'), P('wd', 'ch'), P('ch'), P('wd', 'ch'), P('ch'), P('ch', 'wd'), P('wd'))
    swap = [(i, i + 1 - 2 * (i % CORES)) for i in range(wd_count)]
    same_core = [[x * CORES + c for x in range(chips)] for c in range(CORES)]

    def local_layer(resid_in, seg_pos, gain_temporal, w_x, bias_x, w_y, bias_y, conv_w, conv_bias, lam_param, rgate_w, rgate_b, igate_w, igate_b, w_o, bias_o, gain_mlp, w_g, bias_g, w_u, bias_u, w_d, bias_d):
        tokens, local_width = resid_in.shape
        model_width = local_width * wd_count
        share = tokens // ch_count
        rnn = w_x.shape[1]
        mine = rnn // wd_count
        wd_i = lax.axis_index('wd')
        core = wd_i % CORES
        block = wd_i // CORES
        positions = seg_pos.reshape(tokens)

        def own(vec):
            return lax.dynamic_slice_in_dim(vec, wd_i * mine, mine, axis=vec.ndim - 1)

        def both(vec):
            pair = lax.dynamic_slice_in_dim(vec, block * CORES * mine, CORES * mine, axis=vec.ndim - 1)
            return jnp.where(core == 0, pair, jnp.concatenate([pair[..., mine:], pair[..., :mine]], axis=-1))

        ff = w_g.shape[1] // wd_count
        pieces = jnp.concatenate([w_g.reshape(local_width, wd_count, ff), w_u.reshape(local_width, wd_count, ff)], axis=2)
        mlp_w = lax.all_to_all(pieces.transpose(1, 0, 2), 'wd', 0, 0)

        resid32 = resid_in.astype(jnp.float32)
        sum_sq = lax.psum(jnp.sum(resid32 * resid32, axis=1, keepdims=True), 'wd')
        normed = rms_apply(resid32, sum_sq, model_width, gain_temporal)
        normed_pair = lax.ppermute(normed, 'wd', swap)
        w_xy = jnp.concatenate([w_x.reshape(local_width, chips, CORES, mine), w_y.reshape(local_width, chips, CORES, mine)], axis=3)
        w_keep = lax.dynamic_index_in_dim(w_xy, core, 2, keepdims=False).reshape(local_width, rnn)
        w_send = lax.dynamic_index_in_dim(w_xy, 1 - core, 2, keepdims=False).reshape(local_width, rnn)
        w_pair = lax.ppermute(w_send, 'wd', swap)
        part = (jnp.dot(normed, w_keep, preferred_element_type=jnp.float32) + jnp.dot(normed_pair, w_pair, preferred_element_type=jnp.float32)).astype(jnp.bfloat16)
        got = lax.all_to_all(part.reshape(tokens, chips, CORES * mine).transpose(1, 0, 2), 'wd', 0, 0, axis_index_groups=same_core)
        uy = jnp.sum(got.astype(jnp.float32), axis=0)
        u_own = (uy[:, :mine] + own(bias_x).astype(jnp.float32)).astype(jnp.bfloat16)
        y_own = jax.nn.gelu(uy[:, mine:] + own(bias_y).astype(jnp.float32), approximate=True).astype(jnp.bfloat16)
        u_pair = jnp.concatenate([u_own, lax.ppermute(u_own, 'wd', swap)], axis=1)
        gate_w = jnp.concatenate([lax.dynamic_index_in_dim(w, block, 0, keepdims=False) for w in (rgate_w, igate_w)], axis=1)
        gate_w = gate_w.reshape(CORES, mine, 2, CORES, mine)
        gate_w = lax.dynamic_index_in_dim(gate_w, core, 3, keepdims=False).reshape(CORES, mine, 2 * mine)
        gate_w = jnp.where(core == 0, gate_w, gate_w[::-1]).reshape(CORES * mine, 2 * mine)
        gate_b = jnp.concatenate([own(rgate_b), own(igate_b)])[None]
        mixed = lru(u_pair, y_own, positions[:, None], both(conv_w), both(conv_bias)[None], gate_w, gate_b, own(lam_param)[None])
        mixed_all = lax.all_gather(mixed, 'wd', axis=0)
        mix_part = jnp.dot(mixed_all.transpose(1, 0, 2).reshape(tokens, rnn), w_o, preferred_element_type=jnp.float32).astype(jnp.bfloat16)
        mix_sum = jnp.sum(lax.all_to_all(mix_part.reshape(ch_count, share, local_width), 'ch', 0, 0).astype(jnp.float32), axis=0)
        resid_rows = lax.dynamic_slice_in_dim(resid32, lax.axis_index('ch') * share, share, axis=0)
        resid = resid_rows + mix_sum + bias_o.astype(jnp.float32)
        sum_sq2 = lax.psum(jnp.sum(resid * resid, axis=1, keepdims=True), 'wd')
        normed2 = rms_apply(resid, sum_sq2, model_width, gain_mlp)
        all2 = lax.all_gather(normed2, ('ch', 'wd'), axis=0).reshape(ch_count, wd_count, share, local_width)
        mlp_b = jnp.concatenate([lax.dynamic_slice_in_dim(b, wd_i * ff, ff) for b in (bias_g, bias_u)])[None]
        inner = gate_up(all2, mlp_w, mlp_b)
        inner_all = lax.all_gather(inner, 'wd', axis=0)
        down_part = down(inner_all, w_d)
        down_sum = jnp.sum(lax.all_to_all(down_part.reshape(ch_count, share, local_width), 'ch', 0, 0).astype(jnp.float32), axis=0)
        out_rows = (resid + down_sum + bias_d.astype(jnp.float32)).astype(jnp.bfloat16)
        return lax.all_gather(out_rows, 'ch', axis=0, tiled=True)

    return jax.shard_map(local_layer, mesh=mesh, in_specs=specs, out_specs=row_spec, check_vma=False)
```

time: 2390 us -> 853 us (0.36)
  local copies, waits for them, and re-layouts: 859 us -> 55.8 us
  waiting for transfers between devices: 1020 us -> 524 us
  other arithmetic: 276 us -> 42.6 us
  Pallas kernels: 0 us -> 118 us
  matrix products: 122 us -> 31.4 us
    slice x78 -> x3, local copies, waits for them, and re-layouts: 530 us -> 2.33 us  [the longest x1 2.31 us: local_layer(): uy[:, mine:] + own(bias_y).astype(jnp.float32)]
    all_to_all x6 -> x4, waiting for transfers between devices: 812 us -> 311 us  [the longest x1 135 us: local_layer(): mlp_w = lax.all_to_all(pieces.transpose(1, 0, 2), 'wd', 0, 0)]
    pad x22 -> x0, local copies, waits for them, and re-layouts: 261 us -> none  [rg_lru(): lax.associative_scan(combine, (decay.reshape(seqs, steps, width), drive.r...]
    pallas_call x0 -> x3, Pallas kernels: none -> 118 us  [the longest x1 69.4 us: gate_up(): pl.pallas_call(gate_up_kernel, grid=(ch, share // tile, wd), out_shape=ja...]
    dot_general x8 -> x3, matrix products: 122 us -> 31.4 us  [the longest x1 11.3 us: local_layer(): jnp.dot(normed_pair, w_pair, preferred_element_type=jnp.float32)]
    add x22 -> x0, other arithmetic: 63 us -> none  [the longest x11 32.2 us: combine(): return (left[0] * right[0], right[0] * left[1] + right[1])]
    mul x11 -> x0, other arithmetic: 52.7 us -> none  [the longest x10 52.7 us: combine(): return (left[0] * right[0], right[0] * left[1] + right[1])]
    reshape x3, local copies, waits for them, and re-layouts: 52.4 us -> 9.41 us  [the longest x1 4.69 us: local_layer(): w_g.reshape(local_width, wd_count, ff)]
  transfers between devices with their start and end apart: 11 -> 11, of which waited for: 9 -> 8; matrix products, arithmetic and copies ran while one was open for 48% -> 7% of each run, Pallas kernels for 0% -> 0%
where the time goes in v1:
time: 853 us; the launch traced here: 850 us
  waiting for transfers between devices  524 us (61%)
  Pallas kernels  118 us (14%)
  local copies, waits for them, and re-layouts  55.8 us (7%)
  other arithmetic  42.6 us (5%)
  blocking collectives  37.3 us (4%)
  matrix products  31.4 us (4%)
  starting transfers between devices  26.8 us (3%)
  between operations  13.5 us (2%)
    all_to_all x1, waiting for transfers between devices, local_layer(): mlp_w = lax.all_to_all(pieces.transpose(1, 0, 2), 'wd', 0, 0)  135 us
    all_gather x1, waiting for transfers between devices, local_layer(): inner_all = lax.all_gather(inner, 'wd', axis=0)  116 us
    all_to_all x1, waiting for transfers between devices, local_layer(): lax.all_to_all(part.reshape(tokens, chips, CORES * mine).transpose(1, 0,...  85.9 us
    pallas_call x1, Pallas kernels, gate_up(): pl.pallas_call(gate_up_kernel, grid=(ch, share // tile, wd), out_shape=ja...  69.4 us
    all_to_all x1, waiting for transfers between devices, local_layer(): lax.all_to_all(down_part.reshape(ch_count, share, local_width), 'ch', 0, 0)  48.4 us
    all_gather x1, waiting for transfers between devices, local_layer(): mixed_all = lax.all_gather(mixed, 'wd', axis=0)  48 us
    all_gather x1, waiting for transfers between devices, local_layer(): return lax.all_gather(out_rows, 'ch', axis=0, tiled=True)  45 us
    all_to_all x1, waiting for transfers between devices, local_layer(): lax.all_to_all(mix_part.reshape(ch_count, share, local_width), 'ch', 0, 0)  41.7 us
  transfers between devices with their start and end apart: 11, of which 8 were waited for; matrix products, arithmetic and copies ran while one was open for 7% of the time, Pallas kernels for 0%

profile of v1, /device:TPU:97, one launch (start us, length us, event | category | flops | bytes accessed | tf_op | source)
XLA Modules:
  0.0 849.6 jit_solution(4598362496229296354)
XLA Ops:
  7.3 3.1 multiply_reduce_fusion
  10.4 24.0 %psum.14 = f32[4096,1]{0,1:T(1,128)S(1)} all-reduce(f32[4096,1]{0,1:T(1,128)S(1)} %bitcast.54), channel_id=1, replica_groups=mesh['dp'=1,'ch'=4,'wd'=8] {'wd'}, use_global_device_ids=true, to_apply=%region_1.2 | all-reduce | flops 4096 | bytes 32768 | tf_op jit(solution)/shard_map/psum | solution.py:210
  34.5 4.2 multiply_convert_fusion
  38.7 3.5 collective-permute-start
  42.8 1.5 copy.41
  44.7 10.3 %fusion.13 = f32[4096,1024]{0,1:T(8,128)} fusion(bf16[4096,512]{1,0:T(8,128)(2,1)} %multiply_convert_fusion, bf16[512,1024]{0,1:T(8,128)(2,1)S(1)} %bitcast.50), kind=kOutput, calls=%fused_computation.50 | convolution fusion | flops 4294967296 | bytes 22020096 | tf_op jit(solution)/shard_map/dot_general | solution.py:217
  55.0 11.3 %add_convert_fusion = bf16[4096,1024]{0,1:T(8,128)(2,1)} fusion(f32[4096,1024]{0,1:T(8,128)} %fusion.13, bf16[4096,512]{1,0:T(8,128)(2,1)} %collective-permute-done, bf16[512,1024]{0,1:T(8,128)(2,1)S(1)} %collective-permute-done.1), kind=kOutput, calls=%fused_computation.1 | convolution fusion | flops 4303355904 | bytes 30408704 | tf_op jit(solution)/shard_map/dot_general | solution.py:217
  66.3 5.9 all-to-all-start
  75.9 2.0 copy.46.pos_ref
  79.5 85.9 %all-to-all-done = bf16[4,4096,256]{1,2,0:T(8,128)(2,1)} async-done(((bf16[4,4096,256]{1,2,0:T(8,128)(2,1)}), bf16[4,4096,256]{1,2,0:T(8,128)(2,1)}, u32[]{:S(2)}, u32[]{:S(2)}) %all-to-all-start) | async-done | bytes 8388640 | tf_op jit(solution)/shard_map/all_to_all | solution.py:218
  165.4 5.4 convert_reduce_fusion
  170.8 2.3 fusion.11
  173.1 1.9 copy.52
  175.0 1.1 add_convert_fusion.2
  176.1 1.4 collective-permute-start.2
  178.3 1.9 copy.53
  181.0 1.8 pad_maximum_fusion.u_ref
  182.7 14.1 %lru.1 = bf16[4096,128]{1,0:T(8,128)(2,1)} custom-call(bf16[4096,256]{1,0:T(8,128)(2,1)S(1)} %pad_maximum_fusion.u_ref, bf16[4096,128]{1,0:T(8,128)(2,1)S(1)} %fusion.7.y_ref, s32[4096,1]{1,0:T(8,128)} %copy.46.pos_ref, bf16[4,256]{1,0:T(4,128)(2,1)S(1)} %fusion.10.taps_ref, bf16[1,256]{1,0:T(2,128)(2,1)S(1)} %broadcast_in_dim.25.cbias_ref, ...), custom_call_target="tpu_custom_call" | custom-call | tf_op jit(solution)/shard_map/lru/pallas_call | solution.py:94
  196.9 48.0 %all-gather.10.cloned.1.call-done = bf16[32768,128]{1,0:T(8,128)(2,1)} async-done(((bf16[4096,128]{1,0:T(8,128)(2,1)}), bf16[32768,128]{1,0:T(8,128)(2,1)}) %all-gather.10.cloned.1.call-update) | async-done | bytes 8388624 | tf_op jit(solution)/shard_map/all_gather | solution.py:229
  244.9 11.4 %copy.47 = bf16[8,4096,128]{1,2,0:T(8,128)(2,1)} copy(bf16[8,4096,128]{2,1,0:T(8,128)(2,1)} %bitcast.45) | data formatting | bytes 16777216 | tf_op jit(solution)/shard_map/all_gather | solution.py:229
  256.3 9.7 %convolution_convert_fusion = bf16[4096,512]{1,0:T(8,128)(2,1)} fusion(bf16[4096,1024]{0,1:T(8,128)(2,1)} %bitcast.46, bf16[1024,512]{1,0:T(8,128)(2,1)S(1)} %copy-done), kind=kOutput, calls=%fused_computation.7 | convolution fusion | flops 4297064448 | bytes 13631488 | tf_op jit(solution)/shard_map/dot_general | solution.py:230
  266.0 5.0 all-to-all-start.1
  271.1 6.6 convert_element_type.51
  277.8 41.7 %all-to-all-done.1 = bf16[4,1024,512]{2,1,0:T(8,128)(2,1)} async-done(((bf16[4,1024,512]{2,1,0:T(8,128)(2,1)}), bf16[4,1024,512]{2,1,0:T(8,128)(2,1)}, u32[]{:S(2)}, u32[]{:S(2)}) %all-to-all-start.1) | async-done | bytes 4194336 | tf_op jit(solution)/shard_map/all_to_all | solution.py:231
  319.5 3.1 convert_reduce_fusion.2
  322.6 2.0 multiply_reduce_fusion.1
  324.6 13.3 %psum.15 = f32[1024,1]{0,1:T(1,128)S(1)} all-reduce(f32[1024,1]{0,1:T(1,128)S(1)} %bitcast.57), channel_id=1, replica_groups=mesh['dp'=1,'ch'=4,'wd'=8] {'wd'}, use_global_device_ids=true, to_apply=%region_5.6 | all-reduce | flops 1024 | bytes 8192 | tf_op jit(solution)/shard_map/psum | solution.py:234
  337.9 1.2 multiply_convert_fusion.1
  339.2 4.6 copy.48
  343.9 4.7 copy.50
  348.6 4.6 copy.49
  353.2 4.7 copy.51
  357.9 5.9 maximum_bitcast_fusion
  363.8 5.3 all-to-all-start.2
  370.6 134.8 %all-to-all-done.2.w_ref = bf16[8,512,768]{2,1,0:T(8,128)(2,1)} async-done(((bf16[8,512,768]{2,1,0:T(8,128)(2,1)}), bf16[8,512,768]{2,1,0:T(8,128)(2,1)}, u32[]{:S(2)}, u32[]{:S(2)}) %all-to-all-start.2) | async-done | bytes 6291488 | tf_op jit(solution)/shard_map/all_to_all | solution.py:207
  505.5 4.3 all-gather.12.cloned.1.call-done
  509.7 69.4 %gate_up.1 = bf16[4096,384]{1,0:T(8,128)(2,1)S(1)} custom-call(bf16[4,8,1024,512]{3,2,1,0:T(8,128)(2,1)} %bitcast.40, bf16[8,512,768]{2,1,0:T(8,128)(2,1)} %all-to-all-done.2.w_ref, bf16[1,768]{1,0:T(2,128)(2,1)S(1)} %broadcast_in_dim.29.bias_ref), custom_call_target="tpu_custom_call" | custom-call | tf_op jit(solution)/shard_map/gate_up/pallas_call | solution.py:129
  579.2 1.7 copy-done.3
  580.9 116.2 %all-gather.14.cloned.1.call-done = bf16[32768,384]{1,0:T(8,128)(2,1)} async-done(((bf16[4096,384]{1,0:T(8,128)(2,1)}), bf16[32768,384]{1,0:T(8,128)(2,1)}) %all-gather.14.cloned.1.call-update) | async-done | bytes 25165840 | tf_op jit(solution)/shard_map/all_gather | solution.py:239
  697.1 1.9 copy-done.4
  699.0 34.3 %down.1 = bf16[4096,512]{1,0:T(8,128)(2,1)S(1)} custom-call(bf16[8,4096,384]{2,1,0:T(8,128)(2,1)} %bitcast.41, bf16[3072,512]{1,0:T(8,128)(2,1)S(1)} %copy-done.4), custom_call_target="tpu_custom_call" | custom-call | tf_op jit(solution)/shard_map/down/pallas_call | solution.py:165
  733.3 2.0 copy-done.2
  735.3 5.1 all-to-all-start.3
  740.4 48.4 %all-to-all-done.3 = bf16[4,1024,512]{2,1,0:T(8,128)(2,1)} async-done(((bf16[4,1024,512]{2,1,0:T(8,128)(2,1)}), bf16[4,1024,512]{2,1,0:T(8,128)(2,1)}, u32[]{:S(2)}, u32[]{:S(2)}) %all-to-all-start.3) | async-done | bytes 4194336 | tf_op jit(solution)/shard_map/all_to_all | solution.py:241
  788.8 3.1 convert_reduce_fusion.1
  791.9 1.5 add_convert_fusion.1
  793.5 45.0 %all-gather.8.cloned.1.call-done = bf16[4096,512]{1,0:T(8,128)(2,1)} async-done(((bf16[1024,512]{1,0:T(8,128)(2,1)}), bf16[4096,512]{1,0:T(8,128)(2,1)}) %all-gather.8.cloned.1.call-update) | async-done | bytes 4194320 | tf_op jit(solution)/shard_map/all_gather | solution.py:243
  838.5 4.5 copy.55
  (66 shorter events, 10.3 us)
Async XLA Ops:
  6.5 249.8 %copy-start = (bf16[1024,512]{1,0:T(8,128)(2,1)S(1)}, bf16[1024,512]{1,0:T(8,128)(2,1)}, u32[]{:S(2)}) copy-start(bf16[1024,512]{1,0:T(8,128)(2,1)} %param.37) | copy-start | bytes 3145732
  34.5 7.8 copy-start.5
  38.7 16.3 %collective-permute-start = (bf16[4096,512]{1,0:T(8,128)(2,1)}, bf16[4096,512]{1,0:T(8,128)(2,1)}, u32[]{:S(2)}, u32[]{:S(2)}) collective-permute-start(bf16[4096,512]{1,0:T(8,128)(2,1)} %multiply_convert_fusion), channel_id=1, source_target_pairs={{0,1},{1,0},{2,3},{3,2},{4,5},{5,4},{6,7},{7,6},{8,9},{9,8},{10,11... | collective-permute-start | bytes 12582920 | tf_op jit(solution)/shard_map/ppermute | solution.py:212
  44.5 10.4 %collective-permute-start.1 = (bf16[512,1024]{0,1:T(8,128)(2,1)S(1)}, bf16[512,1024]{0,1:T(8,128)(2,1)S(1)}, u32[]{:S(2)}, u32[]{:S(2)}) collective-permute-start(bf16[512,1024]{0,1:T(8,128)(2,1)S(1)} %bitcast.51), channel_id=1, source_target_pairs={{0,1},{1,0},{2,3},{3,2},{4,5},{5,4},{6,7},{7,6},{8,9},{9,8},{10,11... | collective-permute-start | bytes 3145736 | tf_op jit(solution)/shard_map/ppermute | solution.py:216
  66.3 7.7 copy-start.11
  66.3 9.6 %copy-start.6 = (s32[1,4096]{1,0:T(1,128)S(1)}, s32[1,4096]{1,0:T(1,128)}, u32[]{:S(2)}) copy-start(s32[1,4096]{1,0:T(1,128)} %param.24) | copy-start | bytes 49156
  66.3 99.0 %all-to-all-start = ((bf16[4,4096,256]{1,2,0:T(8,128)(2,1)}), bf16[4,4096,256]{1,2,0:T(8,128)(2,1)}, u32[]{:S(2)}, u32[]{:S(2)}) async-start(bf16[4,4096,256]{1,2,0:T(8,128)(2,1)} %bitcast.44), calls=%async_computation | async-start | bytes 16777216 | tf_op jit(solution)/shard_map/all_to_all | solution.py:218
  72.2 7.3 copy-start.7
  72.2 172.7 %all-gather.10.cloned.1.call-start = ((), (), s32[]{:S(2)}) async-start(), calls=%async_computation.5 | async-start | bytes 9437184 | tf_op jit(solution)/shard_map/all_gather | solution.py:229
  176.1 4.9 collective-permute-start.2
  266.0 53.5 %all-to-all-start.1 = ((bf16[4,1024,512]{2,1,0:T(8,128)(2,1)}), bf16[4,1024,512]{2,1,0:T(8,128)(2,1)}, u32[]{:S(2)}, u32[]{:S(2)}) async-start(bf16[4,1024,512]{2,1,0:T(8,128)(2,1)} %bitcast.49), calls=%async_computation.1 | async-start | bytes 8388608 | tf_op jit(solution)/shard_map/all_to_all | solution.py:231
  271.1 6.7 copy-start.8
  271.1 6.7 copy-start.9
  271.1 238.7 %all-gather.12.cloned.1.call-start = ((), (), s32[]{:S(2)}) async-start(), calls=%async_computation.6 | async-start | bytes 34603008 | tf_op jit(solution)/shard_map/all_gather | solution.py:236
  363.8 141.7 %all-to-all-start.2 = ((bf16[8,512,768]{2,1,0:T(8,128)(2,1)}), bf16[8,512,768]{2,1,0:T(8,128)(2,1)}, u32[]{:S(2)}, u32[]{:S(2)}) async-start(bf16[8,512,768]{2,1,0:T(8,128)(2,1)} %maximum_bitcast_fusion), calls=%async_computation.2 | async-start | bytes 12582912 | tf_op jit(solution)/shard_map/all_to_all | solution.py:207
  369.1 328.0 %all-gather.14.cloned.1.call-start = ((), (), s32[]{:S(2)}) async-start(), calls=%async_computation.7 | async-start | bytes 28311552 | tf_op jit(solution)/shard_map/all_gather | solution.py:239
  579.2 1.7 copy-start.3
  697.1 1.9 copy-start.4
  733.2 2.0 copy-start.2
  735.3 5.2 copy-start.10
  735.3 53.5 %all-to-all-start.3 = ((bf16[4,1024,512]{2,1,0:T(8,128)(2,1)}), bf16[4,1024,512]{2,1,0:T(8,128)(2,1)}, u32[]{:S(2)}, u32[]{:S(2)}) async-start(bf16[4,1024,512]{2,1,0:T(8,128)(2,1)} %bitcast.38), calls=%async_computation.3 | async-start | bytes 8388608 | tf_op jit(solution)/shard_map/all_to_all | solution.py:241
  740.4 98.2 %all-gather.8.cloned.1.call-start = ((), (), s32[]{:S(2)}) async-start(), calls=%async_computation.4 | async-start | bytes 5242880 | tf_op jit(solution)/shard_map/all_gather | solution.py:243
  793.5 49.5 %copy-start.1 = (bf16[1024,512]{1,0:T(8,128)(2,1)S(1)}, bf16[1024,512]{1,0:T(8,128)(2,1)}, u32[]{:S(2)}) copy-start(bf16[1024,512]{1,0:T(8,128)(2,1)} %param.37) | copy-start | bytes 3145732
Sparse Core Ops, SparseCore 0:
  197.1 47.8 all-gather.9
  339.3 170.3 all-gather.11
  581.0 116.0 all-gather.13
  793.6 44.8 all-gather.7

commit v2 on v1

--- a/solution.py
+++ b/solution.py
@@ -140,39 +140,195 @@
     )(normed, weight, bias)
 
 
-def down_kernel(h_ref, w_ref, out_ref, acc):
-    step = pl.program_id(1)
-    depth = h_ref.shape[2]
-    part = jnp.dot(h_ref[0], w_ref[pl.ds(pl.multiple_of(step * depth, depth), depth), :], preferred_element_type=jnp.float32)
-
-    @pl.when(step == 0)
-    def _():
-        acc[...] = part
-
-    @pl.when(step > 0)
-    def _():
-        acc[...] += part
-
-    @pl.when(step == pl.num_programs(1) - 1)
-    def _():
-        out_ref[...] = acc[...].astype(jnp.bfloat16)
-
-
-def down(parts, weight):
-    count, tokens, depth = parts.shape
-    cols = weight.shape[1]
-    tile = 1024
-    return pl.pallas_call(
-        down_kernel,
-        grid=(tokens // tile, count),
-        out_shape=jax.ShapeDtypeStruct((tokens, cols), jnp.bfloat16),
-        in_specs=[pl.BlockSpec((1, tile, depth), lambda t, i: (i, t, 0)),
-                  pl.BlockSpec(weight.shape, lambda t, i: (0, 0))],
-        out_specs=pl.BlockSpec((tile, cols), lambda t, i: (t, 0)),
-        scratch_shapes=[pltpu.VMEM((tile, cols), jnp.float32)],
-        compiler_params=pltpu.CompilerParams(vmem_limit_bytes=40 << 20),
-        name='down',
-    )(parts, weight)
+MESH = pl.DeviceIdType.MESH
+ROUNDS = 4
+
+
+def ring_kernel(regather, h_ref, w_ref, resid_ref, bias_ref, out_ref, hbuf, pbuf, opp_buf, side, xs, xr, ys, yr, own_sem):
+    share, depth = h_ref.shape[1:]
+    rr = share // ROUNDS
+    half = rr // 2
+    ring_x = lax.axis_size('wd') // CORES
+    ring_y = lax.axis_size('ch')
+    ch = lax.axis_index('ch')
+    wd = lax.axis_index('wd')
+    core = lax.rem(wd, CORES)
+    chip = wd // CORES
+    other = 1 - 2 * core
+
+    def along_x(step):
+        return lax.rem(chip + step, ring_x) * CORES + core
+
+    x_right, x_opp, x_left = along_x(1), along_x(2), along_x(3)
+    y_right, y_opp, y_left = (lax.rem(ch + step, ring_y) for step in (1, 2, 3))
+    partner = wd + other
+
+    def span(r, part):
+        if part is None:
+            return pl.ds(r * rr, rr)
+        return pl.ds(r * rr + part * half, half)
+
+    def cols(owner, r, part=None):
+        return hbuf.at[:, span(r, part), pl.ds(pl.multiple_of(owner * depth, depth), depth)]
+
+    def x_send(k, r):
+        if k in (0, 1, 4):
+            src, dst = h_ref.at[:, span(r, None)], cols(wd, r)
+        else:
+            owner, part = {2: (x_left, 0), 3: (x_right, 1), 5: (x_left, None), 6: (x_right, None), 7: (x_opp, 0), 8: (x_opp, 1)}[k]
+            src = dst = cols(owner, r, part)
+        to = {0: x_right, 1: x_left, 2: x_right, 3: x_left}.get(k, partner)
+        return pltpu.make_async_remote_copy(src_ref=src, dst_ref=dst, send_sem=xs.at[r, k], recv_sem=xr.at[r, k], device_id={'wd': to}, device_id_type=MESH)
+
+    def x_recv(k, r):
+        owner, part = {0: (x_left, None), 1: (x_right, None), 2: (x_opp, 0), 3: (x_opp, 1), 4: (partner, None), 5: (x_left + other, None),
+                       6: (x_right + other, None), 7: (x_opp + other, 0), 8: (x_opp + other, 1)}[k]
+        ref = cols(owner, r, part)
+        pltpu.make_async_remote_copy(src_ref=ref, dst_ref=ref, send_sem=xs.at[r, k], recv_sem=xr.at[r, k], device_id={'wd': partner}, device_id_type=MESH).wait_recv()
+
+    def y_refs(k, r):
+        opp_rows = pl.ds(r * half, half)
+        a, b, full = span(r, 0), span(r, 1), span(r, None)
+        if k < 6:
+            src, dst, to = {
+                0: (pbuf.at[0, a], opp_buf.at[0, opp_rows], y_right),
+                1: (pbuf.at[0, b], opp_buf.at[1, opp_rows], y_left),
+                2: (pbuf.at[3, b], side.at[0, b], y_right),
+                3: (pbuf.at[1, a], side.at[1, a], y_left),
+                4: (pbuf.at[3, a], side.at[0, a], y_right),
+                5: (pbuf.at[1, b], side.at[1, b], y_left),
+            }[k]
+            return src, dst, to, dst
+        owner, part, to, got = {
+            6: (ch, full, y_right, y_left),
+            7: (ch, full, y_left, y_right),
+            8: (y_left, a, y_right, y_opp),
+            9: (y_right, b, y_left, y_opp),
+        }[k]
+        return out_ref.at[owner, part], out_ref.at[owner, part], to, out_ref.at[got, part]
+
+    def y_send(k, r):
+        src, dst, to, _ = y_refs(k, r)
+        return pltpu.make_async_remote_copy(src_ref=src, dst_ref=dst, send_sem=ys.at[r, k], recv_sem=yr.at[r, k], device_id={'ch': to}, device_id_type=MESH)
+
+    def y_recv(k, r):
+        ref = y_refs(k, r)[3]
+        pltpu.make_async_remote_copy(src_ref=ref, dst_ref=ref, send_sem=ys.at[r, k], recv_sem=yr.at[r, k], device_id={'ch': y_right}, device_id_type=MESH).wait_recv()
+
+    def start_own(r):
+        for k in (0, 1, 4):
+            x_send(k, r).start()
+
+    def dots(r):
+        def one(slot, carry):
+            rows_of = lax.rem(ch + 2 + slot, ring_y)
+            block = hbuf[rows_of, pl.ds(r * rr, rr), :]
+            pbuf[slot, pl.ds(r * rr, rr), :] = jnp.dot(block, w_ref[...], preferred_element_type=jnp.float32).astype(jnp.bfloat16)
+            return carry
+        lax.fori_loop(0, ring_y, one, 0)
+        for k in range(4):
+            y_send(k, r).start()
+
+    def combine(r):
+        opp_rows = pl.ds(r * half, half)
+        y_recv(0, r)
+        pbuf[3, span(r, 0), :] = (pbuf[3, span(r, 0), :].astype(jnp.float32) + opp_buf[0, opp_rows, :].astype(jnp.float32)).astype(jnp.bfloat16)
+        y_send(4, r).start()
+        y_recv(1, r)
+        pbuf[1, span(r, 1), :] = (pbuf[1, span(r, 1), :].astype(jnp.float32) + opp_buf[1, opp_rows, :].astype(jnp.float32)).astype(jnp.bfloat16)
+        y_send(5, r).start()
+
+    def final(r):
+        for k in range(2, 6):
+            y_recv(k, r)
+        rows = span(r, None)
+        total = pbuf[2, rows, :].astype(jnp.float32) + side[0, rows, :].astype(jnp.float32) + side[1, rows, :].astype(jnp.float32)
+        total = resid_ref[rows, :].astype(jnp.float32) + total + bias_ref[...].astype(jnp.float32)
+        if regather:
+            out_ref[ch, rows, :] = total.astype(out_ref.dtype)
+            y_send(6, r).start()
+            y_send(7, r).start()
+        else:
+            out_ref[rows, :] = total.astype(out_ref.dtype)
+
+    def relay(r):
+        if regather:
+            y_recv(6, r)
+            y_recv(7, r)
+            y_send(8, r).start()
+            y_send(9, r).start()
+
+    barrier = pltpu.get_barrier_semaphore()
+    for to in ({'wd': partner}, {'wd': x_left}, {'wd': x_right}, {'ch': y_left}, {'ch': y_right}):
+        pl.semaphore_signal(barrier, inc=1, device_id=to, device_id_type=MESH)
+    own = pltpu.make_async_copy(h_ref, hbuf.at[:, :, pl.ds(pl.multiple_of(wd * depth, depth), depth)], own_sem)
+    own.start()
+    pl.semaphore_wait(barrier, 5)
+    start_own(0)
+    start_own(1)
+    for r in range(ROUNDS):
+        x_recv(0, r)
+        x_send(2, r).start()
+        x_recv(1, r)
+        x_send(3, r).start()
+        x_send(5, r).start()
+        x_send(6, r).start()
+        if r + 2 < ROUNDS:
+            start_own(r + 2)
+        if r >= 1:
+            combine(r - 1)
+        x_recv(2, r)
+        x_send(7, r).start()
+        x_recv(3, r)
+        x_send(8, r).start()
+        for k in range(4, 9):
+            x_recv(k, r)
+        if r == 0:
+            own.wait()
+        dots(r)
+        if r >= 1:
+            final(r - 1)
+        if r >= 2:
+            relay(r - 2)
+    combine(ROUNDS - 1)
+    relay(ROUNDS - 2)
+    final(ROUNDS - 1)
+    relay(ROUNDS - 1)
+    for r in range(ROUNDS):
+        if regather:
+            y_recv(8, r)
+            y_recv(9, r)
+        for k in range(9):
+            x_send(k, r).wait_send()
+        for k in range(10 if regather else 6):
+            y_send(k, r).wait_send()
+
+
+def ring_layer(h, w, resid, bias, ring_y, regather, cid):
+    tokens, depth = h.shape
+    share = tokens // ring_y
+    wide, cols = w.shape
+    dtype = jnp.bfloat16 if regather else jnp.float32
+    out = jax.ShapeDtypeStruct((ring_y, share, cols) if regather else (share, cols), dtype)
+    vmem = pl.BlockSpec(memory_space=pltpu.VMEM)
+    res = pl.pallas_call(
+        functools.partial(ring_kernel, regather),
+        out_shape=out,
+        in_specs=[pl.BlockSpec(memory_space=pl.ANY), vmem, vmem, vmem],
+        out_specs=vmem,
+        scratch_shapes=[
+            pltpu.VMEM((ring_y, share, wide), jnp.bfloat16),
+            pltpu.VMEM((ring_y, share, cols), jnp.bfloat16),
+            pltpu.VMEM((2, share // 2, cols), jnp.bfloat16),
+            pltpu.VMEM((2, share, cols), jnp.bfloat16),
+            pltpu.SemaphoreType.DMA((ROUNDS, 9)), pltpu.SemaphoreType.DMA((ROUNDS, 9)),
+            pltpu.SemaphoreType.DMA((ROUNDS, 10)), pltpu.SemaphoreType.DMA((ROUNDS, 10)),
+            pltpu.SemaphoreType.DMA,
+        ],
+        compiler_params=pltpu.CompilerParams(collective_id=cid, has_side_effects=True, vmem_limit_bytes=60 << 20),
+        name='ring_layer',
+    )(h.reshape(ring_y, share, depth), w, resid, bias)
+    return res.reshape(tokens, cols) if regather else res
 
 
 def solution(mesh):
@@ -226,20 +382,13 @@
         gate_w = jnp.where(core == 0, gate_w, gate_w[::-1]).reshape(CORES * mine, 2 * mine)
         gate_b = jnp.concatenate([own(rgate_b), own(igate_b)])[None]
         mixed = lru(u_pair, y_own, positions[:, None], both(conv_w), both(conv_bias)[None], gate_w, gate_b, own(lam_param)[None])
-        mixed_all = lax.all_gather(mixed, 'wd', axis=0)
-        mix_part = jnp.dot(mixed_all.transpose(1, 0, 2).reshape(tokens, rnn), w_o, preferred_element_type=jnp.float32).astype(jnp.bfloat16)
-        mix_sum = jnp.sum(lax.all_to_all(mix_part.reshape(ch_count, share, local_width), 'ch', 0, 0).astype(jnp.float32), axis=0)
-        resid_rows = lax.dynamic_slice_in_dim(resid32, lax.axis_index('ch') * share, share, axis=0)
-        resid = resid_rows + mix_sum + bias_o.astype(jnp.float32)
+        resid_rows = lax.dynamic_slice_in_dim(resid_in, lax.axis_index('ch') * share, share, axis=0)
+        resid = ring_layer(mixed, w_o, resid_rows, bias_o[None], ch_count, False, 1)
         sum_sq2 = lax.psum(jnp.sum(resid * resid, axis=1, keepdims=True), 'wd')
         normed2 = rms_apply(resid, sum_sq2, model_width, gain_mlp)
         all2 = lax.all_gather(normed2, ('ch', 'wd'), axis=0).reshape(ch_count, wd_count, share, local_width)
         mlp_b = jnp.concatenate([lax.dynamic_slice_in_dim(b, wd_i * ff, ff) for b in (bias_g, bias_u)])[None]
         inner = gate_up(all2, mlp_w, mlp_b)
-        inner_all = lax.all_gather(inner, 'wd', axis=0)
-        down_part = down(inner_all, w_d)
-        down_sum = jnp.sum(lax.all_to_all(down_part.reshape(ch_count, share, local_width), 'ch', 0, 0).astype(jnp.float32), axis=0)
-        out_rows = (resid + down_sum + bias_d.astype(jnp.float32)).astype(jnp.bfloat16)
-        return lax.all_gather(out_rows, 'ch', axis=0, tiled=True)
+        return ring_layer(inner, w_d, resid, bias_d[None], ch_count, True, 2)
 
     return jax.shard_map(local_layer, mesh=mesh, in_specs=specs, out_specs=row_spec, check_vma=False)

time: 853 us -> 684 us (0.80)
  waiting for transfers between devices: 524 us -> 222 us
  Pallas kernels: 118 us -> 306 us
  local copies, waits for them, and re-layouts: 55.8 us -> 36.6 us
  other arithmetic: 42.6 us -> 27.1 us
  matrix products: 31.4 us -> 21.9 us
    all_gather x3 -> x0, waiting for transfers between devices: 209 us -> none  [the longest x1 116 us: local_layer(): inner_all = lax.all_gather(inner, 'wd', axis=0)]
    pallas_call x1 -> x2, Pallas kernels: 34.3 us -> 223 us  [ring_layer(): pl.pallas_call(functools.partial(ring_kernel, regather), out_shape=out, i...]
    all_to_all x2 -> x0, waiting for transfers between devices: 90 us -> none  [the longest x1 48.4 us: local_layer(): lax.all_to_all(down_part.reshape(ch_count, share, local_width), 'ch', 0, 0)]
    all_gather x1 -> x0, local copies, waits for them, and re-layouts: 11.4 us -> none  [local_layer(): mixed_all = lax.all_gather(mixed, 'wd', axis=0)]
    all_to_all x2 -> x0, starting transfers between devices: 10.1 us -> none  [the longest x1 5.08 us: local_layer(): lax.all_to_all(down_part.reshape(ch_count, share, local_width), 'ch', 0, 0)]
    dot_general x1 -> x0, matrix products: 9.71 us -> none  [local_layer(): jnp.dot(mixed_all.transpose(1, 0, 2).reshape(tokens, rnn), w_o, preferred...]
    all_to_all x1, waiting for transfers between devices: 135 us -> 126 us  [local_layer(): mlp_w = lax.all_to_all(pieces.transpose(1, 0, 2), 'wd', 0, 0)]
    unnamed x31 -> x33, local copies, waits for them, and re-layouts: 25.2 us -> 18.4 us
  transfers between devices with their start and end apart: 11 -> 6, of which waited for: 8 -> 3; matrix products, arithmetic and copies ran while one was open for 7% -> 6% of each run, Pallas kernels for 0% -> 0%
where the time goes in v2:
time: 684 us; the launch traced here: 682 us
  Pallas kernels  306 us (45%)
  waiting for transfers between devices  222 us (32%)
  local copies, waits for them, and re-layouts  36.6 us (5%)
  blocking collectives  36.2 us (5%)
  other arithmetic  27.1 us (4%)
  matrix products  21.9 us (3%)
  starting transfers between devices  18.6 us (3%)
  between operations  13.8 us (2%)
    pallas_call x2, Pallas kernels, ring_layer(): pl.pallas_call(functools.partial(ring_kernel, regather), out_shape=out, i...  223 us
    all_to_all x1, waiting for transfers between devices, local_layer(): mlp_w = lax.all_to_all(pieces.transpose(1, 0, 2), 'wd', 0, 0)  126 us
    all_to_all x1, waiting for transfers between devices, local_layer(): lax.all_to_all(part.reshape(tokens, chips, CORES * mine).transpose(1, 0,...  83 us
    pallas_call x1, Pallas kernels, gate_up(): pl.pallas_call(gate_up_kernel, grid=(ch, share // tile, wd), out_shape=ja...  69.4 us
    psum x1, blocking collectives, local_layer(): sum_sq = lax.psum(jnp.sum(resid32 * resid32, axis=1, keepdims=True), 'wd')  24 us
    unnamed x33, local copies, waits for them, and re-layouts  18.4 us
  transfers between devices with their start and end apart: 6, of which 3 were waited for; matrix products, arithmetic and copies ran while one was open for 6% of the time, Pallas kernels for 0%

profile of v2, /device:TPU:97, one launch (start us, length us, event | category | flops | bytes accessed | tf_op | source)
XLA Modules:
  0.0 681.9 jit_solution(14062136030298502126)
XLA Ops:
  6.6 0.7 convert_add_fusion.1
  7.2 3.1 fusion
  10.3 24.0 %psum.14 = f32[4096,1]{0,1:T(1,128)S(1)} all-reduce(f32[4096,1]{0,1:T(1,128)S(1)} %bitcast.46), channel_id=1, replica_groups=mesh['dp'=1,'ch'=4,'wd'=8] {'wd'}, use_global_device_ids=true, to_apply=%region_1.2 | all-reduce | flops 4096 | bytes 32768 | tf_op jit(solution)/shard_map/psum | solution.py:366
  34.4 4.3 fusion.2
  38.7 3.5 collective-permute-start
  42.3 0.5 copy.38
  42.8 0.5 copy.39
  43.7 10.3 %fusion.16 = f32[4096,1024]{0,1:T(8,128)} fusion(bf16[4096,512]{1,0:T(8,128)(2,1)} %fusion.2, bf16[512,1024]{0,1:T(8,128)(2,1)S(1)} %bitcast.42), kind=kOutput, calls=%fused_computation.49 | convolution fusion | flops 4294967296 | bytes 22020096 | tf_op jit(solution)/shard_map/dot_general | solution.py:373
  54.1 11.5 %add_convert_fusion = bf16[4096,1024]{0,1:T(8,128)(2,1)} fusion(f32[4096,1024]{0,1:T(8,128)} %fusion.16, bf16[4096,512]{1,0:T(8,128)(2,1)} %collective-permute-done, bf16[512,1024]{0,1:T(8,128)(2,1)S(1)} %collective-permute-done.1), kind=kOutput, calls=%fused_computation.1 | convolution fusion | flops 4303355904 | bytes 30408704 | tf_op jit(solution)/shard_map/dot_general | solution.py:373
  65.6 5.9 all-to-all-start
  71.8 0.8 dynamic_slice.57
  72.5 0.8 dynamic_slice.58
  73.5 0.6 broadcast_in_dim.32.bias_ref
  74.1 1.0 dynamic-slice_bitcast_fusion
  75.2 0.3 constant_dynamic-slice_fusion.1
  75.8 2.0 copy.44.pos_ref
  77.8 0.8 dynamic-slice_convert_fusion.1
  78.6 0.8 dynamic-slice_convert_fusion
  79.3 2.3 constant_dynamic-slice_fusion.resid_ref
  81.6 83.0 %all-to-all-done = bf16[4,4096,256]{1,2,0:T(8,128)(2,1)} async-done(((bf16[4,4096,256]{1,2,0:T(8,128)(2,1)}), bf16[4,4096,256]{1,2,0:T(8,128)(2,1)}, u32[]{:S(2)}, u32[]{:S(2)}) %all-to-all-start) | async-done | bytes 8388640 | tf_op jit(solution)/shard_map/all_to_all | solution.py:374
  164.7 5.5 convert_reduce_fusion
  170.2 2.3 fusion.14
  172.5 1.9 copy.49
  174.5 1.5 collective-permute-start.2
  176.1 1.9 copy.50
  178.0 0.8 fusion.10.y_ref
  178.8 1.6 pad_maximum_fusion.u_ref
  180.4 13.2 %lru.1 = bf16[4096,128]{1,0:T(8,128)(2,1)S(1)} custom-call(bf16[4096,256]{1,0:T(8,128)(2,1)S(1)} %pad_maximum_fusion.u_ref, bf16[4096,128]{1,0:T(8,128)(2,1)S(1)} %fusion.10.y_ref, s32[4096,1]{1,0:T(8,128)} %copy.44.pos_ref, bf16[4,256]{1,0:T(4,128)(2,1)S(1)} %fusion.13.taps_ref, bf16[1,256]{1,0:T(2,128)(2,1)S(1)} %broadcast_in_dim.29.cbias_ref, ...), custom_call_target="tpu_custom_call" | custom-call | tf_op jit(solution)/shard_map/lru/pallas_call | solution.py:94
  193.7 1.0 copy-done.3
  194.6 67.0 %ring_layer.2.resid_ref = f32[1024,512]{1,0:T(8,128)} custom-call(bf16[4,1024,128]{2,1,0:T(8,128)(2,1)} %bitcast.33, bf16[1024,512]{1,0:T(8,128)(2,1)} %w_ref.2, bf16[1024,512]{1,0:T(8,128)(2,1)} %constant_dynamic-slice_fusion.resid_ref, bf16[1,512]{1,0:T(2,128)(2,1)} %broadcast_in_dim.32.bias_ref), custom_call_target="tpu_custom_call" | custom-call | tf_op jit(solution)/shard_map/ring_layer/pallas_call | solution.py:314
  261.7 2.0 multiply_reduce_fusion
  263.6 12.2 %psum.15 = f32[1024,1]{0,1:T(1,128)S(1)} all-reduce(f32[1024,1]{0,1:T(1,128)S(1)} %bitcast.49), channel_id=1, replica_groups=mesh['dp'=1,'ch'=4,'wd'=8] {'wd'}, use_global_device_ids=true, to_apply=%region_4.5 | all-reduce | flops 1024 | bytes 8192 | tf_op jit(solution)/shard_map/psum | solution.py:387
  275.9 1.2 multiply_convert_fusion
  277.2 3.2 copy.45
  280.4 2.8 copy.47
  283.2 3.2 copy.46
  286.4 2.8 copy.48
  289.1 5.9 maximum_bitcast_fusion
  295.1 7.3 %all-to-all-start.1 = ((bf16[8,512,768]{2,1,0:T(8,128)(2,1)}), bf16[8,512,768]{2,1,0:T(8,128)(2,1)}, u32[]{:S(2)}, u32[]{:S(2)}) async-start(bf16[8,512,768]{2,1,0:T(8,128)(2,1)} %maximum_bitcast_fusion), calls=%async_computation.1 | async-start | bytes 12582912 | tf_op jit(solution)/shard_map/all_to_all | solution.py:363
  302.3 0.8 dynamic_slice.61
  303.1 0.8 dynamic_slice.62
  303.9 0.6 broadcast_in_dim.35.bias_ref
  304.5 126.0 %all-to-all-done.1.w_ref = bf16[8,512,768]{2,1,0:T(8,128)(2,1)} async-done(((bf16[8,512,768]{2,1,0:T(8,128)(2,1)}), bf16[8,512,768]{2,1,0:T(8,128)(2,1)}, u32[]{:S(2)}, u32[]{:S(2)}) %all-to-all-start.1) | async-done | bytes 6291488 | tf_op jit(solution)/shard_map/all_to_all | solution.py:363
  430.5 12.5 %all-gather.3.cloned.1.call-done = bf16[32768,512]{1,0:T(8,128)(2,1)} async-done(((bf16[1024,512]{1,0:T(8,128)(2,1)}), bf16[32768,512]{1,0:T(8,128)(2,1)}) %all-gather.3.cloned.1.call-update) | async-done | bytes 33554448 | tf_op jit(solution)/shard_map/all_gather | solution.py:389
  443.0 69.4 %gate_up.1 = bf16[4096,384]{1,0:T(8,128)(2,1)S(1)} custom-call(bf16[4,8,1024,512]{3,2,1,0:T(8,128)(2,1)} %bitcast.35, bf16[8,512,768]{2,1,0:T(8,128)(2,1)} %all-to-all-done.1.w_ref, bf16[1,768]{1,0:T(2,128)(2,1)S(1)} %broadcast_in_dim.34.bias_ref), custom_call_target="tpu_custom_call" | custom-call | tf_op jit(solution)/shard_map/gate_up/pallas_call | solution.py:129
  512.5 1.7 copy-done.2
  514.1 156.5 %ring_layer.3 = bf16[4,1024,512]{2,1,0:T(8,128)(2,1)} custom-call(bf16[4,1024,384]{2,1,0:T(8,128)(2,1)} %bitcast.32, bf16[3072,512]{1,0:T(8,128)(2,1)} %w_ref.3, f32[1024,512]{1,0:T(8,128)} %ring_layer.2.resid_ref, bf16[1,512]{1,0:T(2,128)(2,1)} %broadcast_in_dim.35.bias_ref), custom_call_target="tpu_custom_call" | custom-call | tf_op jit(solution)/shard_map/ring_layer/pallas_call | solution.py:314
  670.6 4.5 copy.52
  (51 shorter events, 1.5 us)
Async XLA Ops:
  6.5 169.5 %copy-start = (f32[1024]{0:T(1024)S(1)}, f32[1024]{0:T(1024)}, u32[]{:S(2)}) copy-start(f32[1024]{0:T(1024)} %param.32) | copy-start | bytes 12292
  34.4 7.9 %copy-start.5 = (bf16[512,1024]{1,0:T(8,128)(2,1)S(1)}, bf16[512,1024]{1,0:T(8,128)(2,1)}, u32[]{:S(2)}) copy-start(bf16[512,1024]{1,0:T(8,128)(2,1)} %param.26) | copy-start | bytes 3145732
  34.4 8.4 %copy-start.6 = (bf16[512,1024]{1,0:T(8,128)(2,1)S(1)}, bf16[512,1024]{1,0:T(8,128)(2,1)}, u32[]{:S(2)}) copy-start(bf16[512,1024]{1,0:T(8,128)(2,1)} %param.28) | copy-start | bytes 3145732
  38.7 15.4 %collective-permute-start = (bf16[4096,512]{1,0:T(8,128)(2,1)}, bf16[4096,512]{1,0:T(8,128)(2,1)}, u32[]{:S(2)}, u32[]{:S(2)}) collective-permute-start(bf16[4096,512]{1,0:T(8,128)(2,1)} %fusion.2), channel_id=1, source_target_pairs={{0,1},{1,0},{2,3},{3,2},{4,5},{5,4},{6,7},{7,6},{8,9},{9,8},{10,11... | collective-permute-start | bytes 12582920 | tf_op jit(solution)/shard_map/ppermute | solution.py:368
  43.6 10.5 %collective-permute-start.1 = (bf16[512,1024]{0,1:T(8,128)(2,1)S(1)}, bf16[512,1024]{0,1:T(8,128)(2,1)S(1)}, u32[]{:S(2)}, u32[]{:S(2)}) collective-permute-start(bf16[512,1024]{0,1:T(8,128)(2,1)S(1)} %bitcast.43), channel_id=1, source_target_pairs={{0,1},{1,0},{2,3},{3,2},{4,5},{5,4},{6,7},{7,6},{8,9},{9,8},{10,11... | collective-permute-start | bytes 3145736 | tf_op jit(solution)/shard_map/ppermute | solution.py:372
  65.6 7.7 %copy-start.12 = (bf16[1024]{0:T(1024)(128)(2,1)S(1)}, bf16[1024]{0:T(1024)(128)(2,1)}, u32[]{:S(2)}) copy-start(bf16[1024]{0:T(1024)(128)(2,1)} %param.31) | copy-start | bytes 6148
  65.6 7.9 %copy-start.9 = (bf16[512]{0:T(512)(128)(2,1)S(1)}, bf16[512]{0:T(512)(128)(2,1)}, u32[]{:S(2)}) copy-start(bf16[512]{0:T(512)(128)(2,1)} %param.38) | copy-start | bytes 3076
  65.6 10.2 %copy-start.7 = (s32[1,4096]{1,0:T(1,128)S(1)}, s32[1,4096]{1,0:T(1,128)}, u32[]{:S(2)}) copy-start(s32[1,4096]{1,0:T(1,128)} %param.24) | copy-start | bytes 49156
  65.6 99.0 %all-to-all-start = ((bf16[4,4096,256]{1,2,0:T(8,128)(2,1)}), bf16[4,4096,256]{1,2,0:T(8,128)(2,1)}, u32[]{:S(2)}, u32[]{:S(2)}) async-start(bf16[4,4096,256]{1,2,0:T(8,128)(2,1)} %bitcast.39), calls=%async_computation | async-start | bytes 16777216 | tf_op jit(solution)/shard_map/all_to_all | solution.py:374
  71.5 7.8 %copy-start.8 = (bf16[4,1024]{1,0:T(4,128)(2,1)S(1)}, bf16[4,1024]{1,0:T(4,128)(2,1)}, u32[]{:S(2)}) copy-start(bf16[4,1024]{1,0:T(4,128)(2,1)} %param.30) | copy-start | bytes 24580
  71.5 371.5 %all-gather.3.cloned.1.call-start = ((), (), s32[]{:S(2)}) async-start(), calls=%async_computation.2 | async-start | bytes 34603008 | tf_op jit(solution)/shard_map/all_gather | solution.py:389
  75.1 6.5 copy-start.10
  174.5 4.3 collective-permute-start.2
  193.7 1.0 copy-start.3
  261.7 14.2 %copy-start.4 = (f32[1024,512]{1,0:T(8,128)S(1)}, f32[1024,512]{1,0:T(8,128)}, u32[]{:S(2)}) copy-start(f32[1024,512]{1,0:T(8,128)} %ring_layer.2.resid_ref) | copy-start | bytes 6291460
  295.1 8.8 %copy-start.11 = (bf16[512]{0:T(512)(128)(2,1)S(1)}, bf16[512]{0:T(512)(128)(2,1)}, u32[]{:S(2)}) copy-start(bf16[512]{0:T(512)(128)(2,1)} %param.45) | copy-start | bytes 3076
  295.1 135.5 %all-to-all-start.1 = ((bf16[8,512,768]{2,1,0:T(8,128)(2,1)}), bf16[8,512,768]{2,1,0:T(8,128)(2,1)}, u32[]{:S(2)}, u32[]{:S(2)}) async-start(bf16[8,512,768]{2,1,0:T(8,128)(2,1)} %maximum_bitcast_fusion), calls=%async_computation.1 | async-start | bytes 12582912 | tf_op jit(solution)/shard_map/all_to_all | solution.py:363
  512.5 1.7 copy-start.2
  670.6 4.5 copy-start.1
Sparse Core Ops, SparseCore 0:
  277.3 165.6 all-gather.2

commit v3 on v2

--- a/solution.py
+++ b/solution.py
@@ -22,7 +22,37 @@
     return jnp.where(z > -0.03, series, 1.0 - jnp.exp(z))
 
 
-def lru_kernel(u_ref, y_ref, pos_ref, taps_ref, cbias_ref, gate_w_ref, gate_b_ref, lam_ref, out_ref, u32, a_s, b_s):
+def lru_kernel(u_ref, y_ref, pos_ref, taps_ref, cbias_ref, gate_w_ref, gate_b_ref, lam_ref, w_g_ref, w_u_ref, out_ref, mlp_w_ref, u32, a_s, b_s, own_w, own_sem, ws, wr):
+    ring_x, _, _, wd, core, chip = ring_refs()
+    depth = w_g_ref.shape[0]
+    ff = own_w.shape[2]
+    here = pl.ds(pl.multiple_of(chip * depth, depth), depth)
+
+    def piece(src_ref, k, to_chip):
+        return src_ref.at[:, pl.ds(pl.multiple_of((to_chip * CORES + k) * ff, ff), ff)]
+
+    def exchange(step):
+        to = lax.rem(chip + step, ring_x)
+        return [pltpu.make_async_remote_copy(src_ref=piece(src, k, to), dst_ref=mlp_w_ref.at[k, here, pl.ds(m * ff, ff)],
+                                             send_sem=ws.at[step, 2 * k + m], recv_sem=wr.at[step, 2 * k + m],
+                                             device_id={'wd': to * CORES + core}, device_id_type=MESH)
+                for k in range(CORES) for m, src in enumerate((w_g_ref, w_u_ref))]
+
+    barrier = pltpu.get_barrier_semaphore()
+    for step in range(1, ring_x):
+        pl.semaphore_signal(barrier, inc=1, device_id={'wd': lax.rem(chip + step, ring_x) * CORES + core}, device_id_type=MESH)
+    inward = [pltpu.make_async_copy(piece(src, k, chip), own_w.at[2 * k + m], own_sem.at[2 * k + m]) for k in range(CORES) for m, src in enumerate((w_g_ref, w_u_ref))]
+    for one in inward:
+        one.start()
+    pl.semaphore_wait(barrier, ring_x - 1)
+    for step in range(1, ring_x):
+        for one in exchange(step):
+            one.start()
+    for one in inward:
+        one.wait()
+    outward = [pltpu.make_async_copy(own_w.at[2 * k + m], mlp_w_ref.at[k, here, pl.ds(m * ff, ff)], own_sem.at[2 * k + m]) for k in range(CORES) for m in range(2)]
+    for one in outward:
+        one.start()
     tokens, wide = u_ref.shape
     width = y_ref.shape[1]
     tile = tokens // SEGS
@@ -85,59 +115,30 @@
             rows = slice(seg * tile + q * sub, seg * tile + (q + 1) * sub)
             out_ref[rows, :] = (hidden * y_ref[rows, :].astype(jnp.float32)).astype(jnp.bfloat16)
         entry = hid[seg:seg + 1] + acc[seg:seg + 1] * entry
-
-
-def lru(u_pair, y_rows, pos, taps, cbias, gate_w, gate_b, lam):
+    for one in outward:
+        one.wait()
+    for step in range(1, ring_x):
+        for one in exchange(step):
+            one.wait()
+
+
+def lru(u_pair, y_rows, pos, taps, cbias, gate_w, gate_b, lam, w_g, w_u, ring_x, cid):
     tokens, wide = u_pair.shape
     width = y_rows.shape[1]
     rows = SEGS * (tokens // SEGS + PAD)
+    depth, ff = w_g.shape[0], w_g.shape[1] // (ring_x * CORES)
+    vmem, anywhere = pl.BlockSpec(memory_space=pltpu.VMEM), pl.BlockSpec(memory_space=pl.ANY)
     return pl.pallas_call(
         lru_kernel,
-        out_shape=jax.ShapeDtypeStruct((tokens, width), jnp.bfloat16),
-        in_specs=[pl.BlockSpec(memory_space=pltpu.VMEM)] * 8,
-        out_specs=pl.BlockSpec(memory_space=pltpu.VMEM),
-        scratch_shapes=[pltpu.VMEM((tokens + PAD, wide), jnp.float32), pltpu.VMEM((rows, width), jnp.float32), pltpu.VMEM((rows, width), jnp.float32)],
-        compiler_params=pltpu.CompilerParams(vmem_limit_bytes=48 << 20),
+        out_shape=(jax.ShapeDtypeStruct((tokens, width), jnp.bfloat16), jax.ShapeDtypeStruct((CORES, ring_x * depth, 2 * ff), jnp.bfloat16)),
+        in_specs=[vmem] * 8 + [anywhere] * 2,
+        out_specs=(vmem, anywhere),
+        scratch_shapes=[pltpu.VMEM((tokens + PAD, wide), jnp.float32), pltpu.VMEM((rows, width), jnp.float32), pltpu.VMEM((rows, width), jnp.float32),
+                        pltpu.VMEM((2 * CORES, depth, ff), jnp.bfloat16), pltpu.SemaphoreType.DMA((2 * CORES,)),
+                        pltpu.SemaphoreType.DMA((ring_x, 2 * CORES)), pltpu.SemaphoreType.DMA((ring_x, 2 * CORES))],
+        compiler_params=pltpu.CompilerParams(collective_id=cid, has_side_effects=True, vmem_limit_bytes=48 << 20),
         name='lru',
-    )(u_pair, y_rows, pos, taps, cbias, gate_w, gate_b, lam)
-
-
-def gate_up_kernel(n_ref, w_ref, bias_ref, out_ref, acc):
-    step = pl.program_id(2)
-    half = out_ref.shape[1]
-    part = jnp.dot(n_ref[0, 0], w_ref[0], preferred_element_type=jnp.float32)
-
-    @pl.when(step == 0)
-    def _():
-        acc[...] = part
-
-    @pl.when(step > 0)
-    def _():
-        acc[...] += part
-
-    @pl.when(step == pl.num_programs(2) - 1)
-    def _():
-        bias = bias_ref[...].astype(jnp.float32)
-        total = acc[...] + bias
-        out_ref[...] = (jax.nn.gelu(total[:, :half], approximate=True) * total[:, half:]).astype(jnp.bfloat16)
-
-
-def gate_up(normed, weight, bias):
-    ch, wd, share, depth = normed.shape
-    cols = weight.shape[2]
-    tile = 512
-    return pl.pallas_call(
-        gate_up_kernel,
-        grid=(ch, share // tile, wd),
-        out_shape=jax.ShapeDtypeStruct((ch * share, cols // 2), jnp.bfloat16),
-        in_specs=[pl.BlockSpec((1, 1, tile, depth), lambda c, t, i: (c, i, t, 0)),
-                  pl.BlockSpec((1, depth, cols), lambda c, t, i: (i, 0, 0)),
-                  pl.BlockSpec((1, cols), lambda c, t, i: (0, 0))],
-        out_specs=pl.BlockSpec((tile, cols // 2), lambda c, t, i: (c * (share // tile) + t, 0)),
-        scratch_shapes=[pltpu.VMEM((tile, cols), jnp.float32)],
-        compiler_params=pltpu.CompilerParams(vmem_limit_bytes=40 << 20),
-        name='gate_up',
-    )(normed, weight, bias)
+    )(u_pair, y_rows, pos, taps, cbias, gate_w, gate_b, lam, w_g, w_u)
 
 
 MESH = pl.DeviceIdType.MESH
@@ -331,6 +332,183 @@
     return res.reshape(tokens, cols) if regather else res
 
 
+def ring_refs():
+    ring_x = lax.axis_size('wd') // CORES
+    ring_y = lax.axis_size('ch')
+    ch = lax.axis_index('ch')
+    wd = lax.axis_index('wd')
+    core = lax.rem(wd, CORES)
+    return ring_x, ring_y, ch, wd, core, wd // CORES
+
+
+def mlp_in_kernel(resid_ref, gain_ref, w_ref, bias_ref, out_ref, nbuf, keep, send, got, sums, all_sums, ns, nr, ss, sr):
+    share, width = resid_ref.shape
+    ring_x, ring_y, ch, wd, core, chip = ring_refs()
+    wd_count = ring_x * CORES
+    rr = share // ROUNDS
+    half = rr // 2
+    partner = wd + 1 - 2 * core
+    lanes = sums.shape[1]
+
+    def device(d1, d2):
+        return {'ch': lax.rem(ch + d1 * (1 - core) + d2 * core, ring_y), 'wd': lax.rem(chip + d1 * core + d2 * (1 - core), ring_x) * CORES + core}
+
+    def block(d1, d2, r, part=None):
+        rows = pl.ds(r * rr, rr) if part is None else pl.ds(r * rr + part * half, half)
+        at = lax.rem(chip + d1 * core + d2 * (1 - core), ring_x)
+        return nbuf.at[lax.rem(ch + d1 * (1 - core) + d2 * core, ring_y), rows, pl.ds(pl.multiple_of(at * width, width), width)]
+
+    firsts = (0, 3, 1, 2)
+
+    def route(k, r):
+        if k < 4:
+            src, to, dst = (((0, 0, r), (1, 0), (3, 0, r)), ((0, 0, r), (3, 0), (1, 0, r)),
+                            ((3, 0, r, 0), (1, 0), (2, 0, r, 0)), ((1, 0, r, 1), (3, 0), (2, 0, r, 1)))[k]
+        else:
+            d1 = firsts[(k - 4) // 4]
+            src, to, dst = (((d1, 0, r), (0, 1), (d1, 3, r)), ((d1, 0, r), (0, 3), (d1, 1, r)),
+                            ((d1, 3, r, 0), (0, 1), (d1, 2, r, 0)), ((d1, 1, r, 1), (0, 3), (d1, 2, r, 1)))[k % 4]
+        return block(*src), to, block(*dst)
+
+    def start(r, *ks):
+        for k in ks:
+            src, to, _ = route(k, r)
+            pltpu.make_async_remote_copy(src_ref=src, dst_ref=src, send_sem=ns.at[r, k], recv_sem=nr.at[r, k], device_id=device(*to), device_id_type=MESH).start()
+
+    def wait(r, *ks):
+        for k in ks:
+            ref = route(k, r)[2]
+            pltpu.make_async_remote_copy(src_ref=ref, dst_ref=ref, send_sem=ns.at[r, k], recv_sem=nr.at[r, k], device_id=device(1, 0), device_id_type=MESH).wait_recv()
+
+    def own(r):
+        if r < ROUNDS:
+            start(r, 0, 1, 4, 5)
+
+    def stage1(r):
+        if r < ROUNDS:
+            wait(r, 0, 1)
+            start(r, 2, 3, 8, 9, 12, 13)
+            wait(r, 4, 5)
+            start(r, 6, 7)
+
+    def stage2(r):
+        if r < ROUNDS:
+            wait(r, 2, 3)
+            start(r, 16, 17)
+            wait(r, 8, 9)
+            start(r, 10, 11)
+            wait(r, 12, 13)
+            start(r, 14, 15)
+
+    def stage3(r):
+        if r < ROUNDS:
+            wait(r, 16, 17)
+            start(r, 18, 19)
+
+    def halves(r):
+        return pltpu.make_async_remote_copy(src_ref=send.at[r], dst_ref=got.at[r], send_sem=ns.at[r, 20], recv_sem=nr.at[r, 20], device_id={'wd': partner}, device_id_type=MESH)
+
+    def dots(r, mine):
+        def one(q, carry):
+            block_in = nbuf[q, pl.ds(r * rr, rr), :]
+            if mine:
+                keep[q] = jnp.dot(block_in, w_ref[core], preferred_element_type=jnp.float32)
+            else:
+                send[r, q] = jnp.dot(block_in, w_ref[1 - core], preferred_element_type=jnp.float32).astype(jnp.bfloat16)
+            return carry
+        lax.fori_loop(0, ring_y, one, 0)
+
+    def finish(r):
+        halves(r).wait_recv()
+        mid = out_ref.shape[2]
+
+        def one(q, carry):
+            total = keep[q] + got[r, q].astype(jnp.float32) + bias_ref[...].astype(jnp.float32)
+            out_ref[q, pl.ds(r * rr, rr), :] = (jax.nn.gelu(total[:, :mid], approximate=True) * total[:, mid:]).astype(jnp.bfloat16)
+            return carry
+        lax.fori_loop(0, ring_y, one, 0)
+
+    barrier = pltpu.get_barrier_semaphore()
+    for step in range(1, wd_count):
+        pl.semaphore_signal(barrier, inc=1, device_id={'wd': lax.rem(wd + step, wd_count)}, device_id_type=MESH)
+    for step in (1, 3):
+        pl.semaphore_signal(barrier, inc=1, device_id={'ch': lax.rem(ch + step, ring_y)}, device_id_type=MESH)
+
+    tiles = share // lanes
+    for i in range(tiles):
+        sq = jnp.zeros((lanes, lanes), jnp.float32)
+        for j in range(width // lanes):
+            val = resid_ref[i * lanes:(i + 1) * lanes, j * lanes:(j + 1) * lanes]
+            sq = sq + val * val
+        sums[i:i + 1, :] = jnp.sum(sq.T, axis=0, keepdims=True)
+    all_sums[wd] = sums[...]
+    pl.semaphore_wait(barrier, wd_count + 1)
+    for step in range(1, wd_count):
+        pltpu.make_async_remote_copy(src_ref=sums, dst_ref=all_sums.at[wd], send_sem=ss.at[step], recv_sem=sr.at[step], device_id={'wd': lax.rem(wd + step, wd_count)}, device_id_type=MESH).start()
+    for step in range(1, wd_count):
+        ref = all_sums.at[lax.rem(wd + wd_count - step, wd_count)]
+        pltpu.make_async_remote_copy(src_ref=ref, dst_ref=ref, send_sem=ss.at[step], recv_sem=sr.at[step], device_id={'wd': partner}, device_id_type=MESH).wait_recv()
+    scale = lax.rsqrt(jnp.sum(all_sums[...], axis=0) / (width * wd_count) + EPS)
+    at = pl.ds(pl.multiple_of(chip * width, width), width)
+    gain = 1.0 + gain_ref[...].astype(jnp.float32)
+    for i in range(tiles):
+        factor = jnp.broadcast_to(scale[i:i + 1, :], (lanes, lanes)).T[:, 0:1]
+        rows = slice(i * lanes, (i + 1) * lanes)
+        nbuf[ch, rows, at] = (resid_ref[rows, :] * factor * gain).astype(jnp.bfloat16)
+    own(0)
+    own(1)
+    stage1(0)
+    own(2)
+    stage2(0)
+    stage1(1)
+    stage3(0)
+    stage2(1)
+    for r in range(ROUNDS):
+        wait(r, 6, 7, 10, 11, 14, 15, 18, 19)
+        dots(r, False)
+        halves(r).start()
+        own(r + 3)
+        stage1(r + 2)
+        stage3(r + 1)
+        dots(r, True)
+        stage2(r + 2)
+        finish(r)
+    for step in range(1, wd_count):
+        pltpu.make_async_remote_copy(src_ref=sums, dst_ref=all_sums.at[wd], send_sem=ss.at[step], recv_sem=sr.at[step], device_id={'wd': partner}, device_id_type=MESH).wait_send()
+    for r in range(ROUNDS):
+        halves(r).wait_send()
+        for k in range(20):
+            src, to, _ = route(k, r)
+            pltpu.make_async_remote_copy(src_ref=src, dst_ref=src, send_sem=ns.at[r, k], recv_sem=nr.at[r, k], device_id=device(*to), device_id_type=MESH).wait_send()
+
+
+def mlp_in(resid, gain, weight, bias, ring_x, ring_y, cid):
+    share, width = resid.shape
+    _, depth, cols = weight.shape
+    lanes = 128
+    rr = share // ROUNDS
+    vmem = pl.BlockSpec(memory_space=pltpu.VMEM)
+    out = pl.pallas_call(
+        mlp_in_kernel,
+        out_shape=jax.ShapeDtypeStruct((ring_y, share, cols // 2), jnp.bfloat16),
+        in_specs=[vmem] * 4,
+        out_specs=vmem,
+        scratch_shapes=[
+            pltpu.VMEM((ring_y, share, depth), jnp.bfloat16),
+            pltpu.VMEM((ring_y, rr, cols), jnp.float32),
+            pltpu.VMEM((ROUNDS, ring_y, rr, cols), jnp.bfloat16),
+            pltpu.VMEM((ROUNDS, ring_y, rr, cols), jnp.bfloat16),
+            pltpu.VMEM((share // lanes, lanes), jnp.float32),
+            pltpu.VMEM((ring_x * CORES, share // lanes, lanes), jnp.float32),
+            pltpu.SemaphoreType.DMA((ROUNDS, 21)), pltpu.SemaphoreType.DMA((ROUNDS, 21)),
+            pltpu.SemaphoreType.DMA((ring_x * CORES,)), pltpu.SemaphoreType.DMA((ring_x * CORES,)),
+        ],
+        compiler_params=pltpu.CompilerParams(collective_id=cid, has_side_effects=True, vmem_limit_bytes=60 << 20),
+        name='mlp_in',
+    )(resid, gain, weight, bias)
+    return out.reshape(ring_y * share, cols // 2)
+
+
 def solution(mesh):
     wd_count = mesh.shape['wd']
     ch_count = mesh.shape['ch']
@@ -359,9 +537,6 @@
             return jnp.where(core == 0, pair, jnp.concatenate([pair[..., mine:], pair[..., :mine]], axis=-1))
 
         ff = w_g.shape[1] // wd_count
-        pieces = jnp.concatenate([w_g.reshape(local_width, wd_count, ff), w_u.reshape(local_width, wd_count, ff)], axis=2)
-        mlp_w = lax.all_to_all(pieces.transpose(1, 0, 2), 'wd', 0, 0)
-
         resid32 = resid_in.astype(jnp.float32)
         sum_sq = lax.psum(jnp.sum(resid32 * resid32, axis=1, keepdims=True), 'wd')
         normed = rms_apply(resid32, sum_sq, model_width, gain_temporal)
@@ -381,14 +556,11 @@
         gate_w = lax.dynamic_index_in_dim(gate_w, core, 3, keepdims=False).reshape(CORES, mine, 2 * mine)
         gate_w = jnp.where(core == 0, gate_w, gate_w[::-1]).reshape(CORES * mine, 2 * mine)
         gate_b = jnp.concatenate([own(rgate_b), own(igate_b)])[None]
-        mixed = lru(u_pair, y_own, positions[:, None], both(conv_w), both(conv_bias)[None], gate_w, gate_b, own(lam_param)[None])
+        mixed, mlp_w = lru(u_pair, y_own, positions[:, None], both(conv_w), both(conv_bias)[None], gate_w, gate_b, own(lam_param)[None], w_g, w_u, chips, 3)
         resid_rows = lax.dynamic_slice_in_dim(resid_in, lax.axis_index('ch') * share, share, axis=0)
         resid = ring_layer(mixed, w_o, resid_rows, bias_o[None], ch_count, False, 1)
-        sum_sq2 = lax.psum(jnp.sum(resid * resid, axis=1, keepdims=True), 'wd')
-        normed2 = rms_apply(resid, sum_sq2, model_width, gain_mlp)
-        all2 = lax.all_gather(normed2, ('ch', 'wd'), axis=0).reshape(ch_count, wd_count, share, local_width)
         mlp_b = jnp.concatenate([lax.dynamic_slice_in_dim(b, wd_i * ff, ff) for b in (bias_g, bias_u)])[None]
-        inner = gate_up(all2, mlp_w, mlp_b)
+        inner = mlp_in(resid, gain_mlp[None], mlp_w, mlp_b, chips, ch_count, 4)
         return ring_layer(inner, w_d, resid, bias_d[None], ch_count, True, 2)
 
     return jax.shard_map(local_layer, mesh=mesh, in_specs=specs, out_specs=row_spec, check_vma=False)

time: 684 us -> 590 us (0.86)
  waiting for transfers between devices: 222 us -> 79.8 us
  Pallas kernels: 306 us -> 410 us
  between operations: 13.8 us -> 0.33 us
  local copies, waits for them, and re-layouts: 36.6 us -> 24.1 us
  blocking collectives: 36.2 us -> 24 us
  other arithmetic: 27.1 us -> 17.3 us
  starting transfers between devices: 18.6 us -> 11.2 us
    all_to_all x1 -> x0, waiting for transfers between devices: 126 us -> none  [local_layer(): mlp_w = lax.all_to_all(pieces.transpose(1, 0, 2), 'wd', 0, 0)]
    pallas_call x2, Pallas kernels: 82.6 us -> 186 us  [the longest x1 113 us: mlp_in(): pl.pallas_call(mlp_in_kernel, out_shape=jax.ShapeDtypeStruct((ring_y, sha...]
    all_gather x1 -> x0, waiting for transfers between devices: 12.5 us -> none  [local_layer(): lax.all_gather(normed2, ('ch', 'wd'), axis=0)]
    psum x1 -> x0, blocking collectives: 12.2 us -> none  [local_layer(): sum_sq2 = lax.psum(jnp.sum(resid * resid, axis=1, keepdims=True), 'wd')]
    unnamed x33 -> x27, local copies, waits for them, and re-layouts: 18.4 us -> 10.4 us
    all_to_all x1 -> x0, starting transfers between devices: 7.28 us -> none  [local_layer(): mlp_w = lax.all_to_all(pieces.transpose(1, 0, 2), 'wd', 0, 0)]
  transfers between devices with their start and end apart: 6 -> 4, of which waited for: 3 -> 1; matrix products, arithmetic and copies ran while one was open for 6% -> 5% of each run, Pallas kernels for 0% -> 0%
where the time goes in v3:
time: 590 us; the launch traced here: 589 us
  Pallas kernels  410 us (69%)
  waiting for transfers between devices  79.8 us (14%)
  local copies, waits for them, and re-layouts  24.1 us (4%)
  blocking collectives  24 us (4%)
  matrix products  21.9 us (4%)
  other arithmetic  17.3 us (3%)
  starting transfers between devices  11.2 us (2%)
    pallas_call x2, Pallas kernels, ring_layer(): pl.pallas_call(functools.partial(ring_kernel, regather), out_shape=out, i...  224 us
    pallas_call x1, Pallas kernels, mlp_in(): pl.pallas_call(mlp_in_kernel, out_shape=jax.ShapeDtypeStruct((ring_y, sha...  113 us
    all_to_all x1, waiting for transfers between devices, local_layer(): lax.all_to_all(part.reshape(tokens, chips, CORES * mine).transpose(1, 0,...  79.8 us
    pallas_call x1, Pallas kernels, lru(): pl.pallas_call(lru_kernel, out_shape=(jax.ShapeDtypeStruct((tokens, width...  73.2 us
    psum x1, blocking collectives, local_layer(): sum_sq = lax.psum(jnp.sum(resid32 * resid32, axis=1, keepdims=True), 'wd')  24 us
  transfers between devices with their start and end apart: 4, of which 1 were waited for; matrix products, arithmetic and copies ran while one was open for 5% of the time, Pallas kernels for 0%

profile of v3, /device:TPU:97, one launch (start us, length us, event | category | flops | bytes accessed | tf_op | source)
XLA Modules:
  0.0 589.1 jit_solution(9176218671853620657)
XLA Ops:
  0.0 3.1 fusion
  3.1 24.0 %psum.7 = f32[4096,1]{0,1:T(1,128)S(1)} all-reduce(f32[4096,1]{0,1:T(1,128)S(1)} %bitcast.34), channel_id=1, replica_groups=mesh['dp'=1,'ch'=4,'wd'=8] {'wd'}, use_global_device_ids=true, to_apply=%region_1.2 | all-reduce | flops 4096 | bytes 32768 | tf_op jit(solution)/shard_map/psum | solution.py:541
  27.2 0.0 copy-start.3
  27.2 4.3 fusion.2
  31.5 3.5 collective-permute-start
  35.1 0.5 copy.30
  35.6 0.5 copy.31
  36.2 0.2 fusion.11
  36.4 0.1 collective-permute-start.1
  36.5 10.3 %fusion.16 = f32[4096,1024]{0,1:T(8,128)} fusion(bf16[4096,512]{1,0:T(8,128)(2,1)} %fusion.2, bf16[512,1024]{0,1:T(8,128)(2,1)S(1)} %bitcast.30), kind=kOutput, calls=%fused_computation.44 | convolution fusion | flops 4294967296 | bytes 22020096 | tf_op jit(solution)/shard_map/dot_general | solution.py:548
  46.9 11.5 %add_convert_fusion = bf16[4096,1024]{0,1:T(8,128)(2,1)} fusion(f32[4096,1024]{0,1:T(8,128)} %fusion.16, bf16[4096,512]{1,0:T(8,128)(2,1)} %collective-permute-done, bf16[512,1024]{0,1:T(8,128)(2,1)S(1)} %collective-permute-done.1), kind=kOutput, calls=%fused_computation.1 | convolution fusion | flops 4303355904 | bytes 30408704 | tf_op jit(solution)/shard_map/dot_general | solution.py:548
  58.4 6.0 %all-to-all-start = ((bf16[4,4096,256]{1,2,0:T(8,128)(2,1)}), bf16[4,4096,256]{1,2,0:T(8,128)(2,1)}, u32[]{:S(2)}, u32[]{:S(2)}) async-start(bf16[4,4096,256]{1,2,0:T(8,128)(2,1)} %bitcast.27), calls=%async_computation | async-start | bytes 16777216 | tf_op jit(solution)/shard_map/all_to_all | solution.py:549
  64.4 0.0 copy-start.7
  64.5 1.0 dynamic-slice_bitcast_fusion
  65.5 0.1 reshape.41
  65.6 0.3 constant_dynamic-slice_fusion.1
  65.9 0.1 copy.34
  66.1 0.1 copy.35
  66.2 0.1 dynamic_slice.53
  66.3 0.1 broadcast_select_fusion
  66.4 0.8 dynamic_slice.57
  67.2 0.8 dynamic_slice.58
  67.9 2.0 copy.36.pos_ref
  70.0 0.6 broadcast_in_dim.31.bias_ref
  70.5 0.8 dynamic_slice.61
  71.3 0.8 dynamic_slice.62
  72.1 0.6 broadcast_in_dim.33.bias_ref
  72.7 0.6 broadcast_in_dim.32.gain_ref
  73.3 0.5 broadcast_in_dim.34.bias_ref
  73.8 0.8 dynamic-slice_convert_fusion.1
  74.6 0.8 dynamic-slice_convert_fusion
  75.4 2.3 constant_dynamic-slice_fusion.resid_ref
  77.7 79.8 %all-to-all-done = bf16[4,4096,256]{1,2,0:T(8,128)(2,1)} async-done(((bf16[4,4096,256]{1,2,0:T(8,128)(2,1)}), bf16[4,4096,256]{1,2,0:T(8,128)(2,1)}, u32[]{:S(2)}, u32[]{:S(2)}) %all-to-all-start) | async-done | bytes 8388640 | tf_op jit(solution)/shard_map/all_to_all | solution.py:549
  157.4 5.5 convert_reduce_fusion
  163.0 2.3 fusion.14
  165.3 1.9 copy.37
  167.2 0.1 add_convert_fusion.1
  167.3 1.5 collective-permute-start.2
  168.8 0.1 dynamic-slice_bitcast_fusion.2.lam_ref
  168.9 1.9 copy.38
  170.8 0.8 fusion.10.y_ref
  171.6 1.6 pad_maximum_fusion.u_ref
  173.2 73.2 %lru.1 = (bf16[4096,128]{1,0:T(8,128)(2,1)S(1)}, bf16[2,2048,768]{2,1,0:T(8,128)(2,1)}) custom-call(bf16[4096,256]{1,0:T(8,128)(2,1)S(1)} %pad_maximum_fusion.u_ref, bf16[4096,128]{1,0:T(8,128)(2,1)S(1)} %fusion.10.y_ref, s32[4096,1]{1,0:T(8,128)} %copy.36.pos_ref, bf16[4,256]{1,0:T(4,128)(2,1)S(1)} %fusion.13.taps_ref, ...), custom_call_target="tpu_custom_call" | custom-call | tf_op jit(solution)/shard_map/lru/pallas_call | solution.py:131
  246.4 1.0 copy-done.1
  247.4 68.1 %ring_layer.2.resid_ref = f32[1024,512]{1,0:T(8,128)} custom-call(bf16[4,1024,128]{2,1,0:T(8,128)(2,1)} %bitcast.24, bf16[1024,512]{1,0:T(8,128)(2,1)} %w_ref.2, bf16[1024,512]{1,0:T(8,128)(2,1)} %constant_dynamic-slice_fusion.resid_ref, bf16[1,512]{1,0:T(2,128)(2,1)} %broadcast_in_dim.31.bias_ref), custom_call_target="tpu_custom_call" | custom-call | tf_op jit(solution)/shard_map/ring_layer/pallas_call | solution.py:315
  315.4 113.2 %mlp_in.1.h_ref = bf16[4,1024,384]{2,1,0:T(8,128)(2,1)} custom-call(f32[1024,512]{1,0:T(8,128)} %ring_layer.2.resid_ref, bf16[1,512]{1,0:T(2,128)(2,1)} %broadcast_in_dim.32.gain_ref, bf16[2,2048,768]{2,1,0:T(8,128)(2,1)} %get-tuple-element.8.w_ref, bf16[1,768]{1,0:T(2,128)(2,1)} %broadcast_in_dim.33.bias_ref), custom_call_target="tpu_custom_call" | custom-call | tf_op jit(solution)/shard_map/mlp_in/pallas_call | solution.py:491
  428.6 156.0 %ring_layer.3 = bf16[4,1024,512]{2,1,0:T(8,128)(2,1)} custom-call(bf16[4,1024,384]{2,1,0:T(8,128)(2,1)} %mlp_in.1.h_ref, bf16[3072,512]{1,0:T(8,128)(2,1)} %w_ref.3, f32[1024,512]{1,0:T(8,128)} %ring_layer.2.resid_ref, bf16[1,512]{1,0:T(2,128)(2,1)} %broadcast_in_dim.34.bias_ref), custom_call_target="tpu_custom_call" | custom-call | tf_op jit(solution)/shard_map/ring_layer/pallas_call | solution.py:315
  584.7 4.5 copy.40
  (33 shorter events, 0.2 us)
Async XLA Ops:
  0.0 168.8 %copy-start = (f32[1024]{0:T(1024)S(1)}, f32[1024]{0:T(1024)}, u32[]{:S(2)}) copy-start(f32[1024]{0:T(1024)} %param.32) | copy-start | bytes 12292
  0.0 27.2 %copy-start.6 = (bf16[512]{0:T(512)(128)(2,1)S(1)}, bf16[512]{0:T(512)(128)(2,1)}, u32[]{:S(2)}) copy-start(bf16[512]{0:T(512)(128)(2,1)} %param.25) | copy-start | bytes 3076
  27.2 7.9 %copy-start.2 = (bf16[512,1024]{1,0:T(8,128)(2,1)S(1)}, bf16[512,1024]{1,0:T(8,128)(2,1)}, u32[]{:S(2)}) copy-start(bf16[512,1024]{1,0:T(8,128)(2,1)} %param.26) | copy-start | bytes 3145732
  27.2 8.4 %copy-start.3 = (bf16[512,1024]{1,0:T(8,128)(2,1)S(1)}, bf16[512,1024]{1,0:T(8,128)(2,1)}, u32[]{:S(2)}) copy-start(bf16[512,1024]{1,0:T(8,128)(2,1)} %param.28) | copy-start | bytes 3145732
  31.5 15.4 %collective-permute-start = (bf16[4096,512]{1,0:T(8,128)(2,1)}, bf16[4096,512]{1,0:T(8,128)(2,1)}, u32[]{:S(2)}, u32[]{:S(2)}) collective-permute-start(bf16[4096,512]{1,0:T(8,128)(2,1)} %fusion.2), channel_id=1, source_target_pairs={{0,1},{1,0},{2,3},{3,2},{4,5},{5,4},{6,7},{7,6},{8,9},{9,8},{10,11... | collective-permute-start | bytes 12582920 | tf_op jit(solution)/shard_map/ppermute | solution.py:543
  36.4 10.5 %collective-permute-start.1 = (bf16[512,1024]{0,1:T(8,128)(2,1)S(1)}, bf16[512,1024]{0,1:T(8,128)(2,1)S(1)}, u32[]{:S(2)}, u32[]{:S(2)}) collective-permute-start(bf16[512,1024]{0,1:T(8,128)(2,1)S(1)} %bitcast.31), channel_id=1, source_target_pairs={{0,1},{1,0},{2,3},{3,2},{4,5},{5,4},{6,7},{7,6},{8,9},{9,8},{10,11... | collective-permute-start | bytes 3145736 | tf_op jit(solution)/shard_map/ppermute | solution.py:547
  58.4 7.8 %copy-start.10 = (bf16[1024]{0:T(1024)(128)(2,1)S(1)}, bf16[1024]{0:T(1024)(128)(2,1)}, u32[]{:S(2)}) copy-start(bf16[1024]{0:T(1024)(128)(2,1)} %param.31) | copy-start | bytes 6148
  58.4 9.5 %copy-start.4 = (s32[1,4096]{1,0:T(1,128)S(1)}, s32[1,4096]{1,0:T(1,128)}, u32[]{:S(2)}) copy-start(s32[1,4096]{1,0:T(1,128)} %param.24) | copy-start | bytes 49156
  58.4 99.0 %all-to-all-start = ((bf16[4,4096,256]{1,2,0:T(8,128)(2,1)}), bf16[4,4096,256]{1,2,0:T(8,128)(2,1)}, u32[]{:S(2)}, u32[]{:S(2)}) async-start(bf16[4,4096,256]{1,2,0:T(8,128)(2,1)} %bitcast.27), calls=%async_computation | async-start | bytes 16777216 | tf_op jit(solution)/shard_map/all_to_all | solution.py:549
  64.4 5.5 copy-start.7
  64.5 8.2 %copy-start.8 = (bf16[512]{0:T(512)(128)(2,1)S(1)}, bf16[512]{0:T(512)(128)(2,1)}, u32[]{:S(2)}) copy-start(bf16[512]{0:T(512)(128)(2,1)} %param.39) | copy-start | bytes 3076
  64.5 8.8 %copy-start.9 = (bf16[512]{0:T(512)(128)(2,1)S(1)}, bf16[512]{0:T(512)(128)(2,1)}, u32[]{:S(2)}) copy-start(bf16[512]{0:T(512)(128)(2,1)} %param.45) | copy-start | bytes 3076
  64.5 10.8 %copy-start.5 = (bf16[4,1024]{1,0:T(4,128)(2,1)S(1)}, bf16[4,1024]{1,0:T(4,128)(2,1)}, u32[]{:S(2)}) copy-start(bf16[4,1024]{1,0:T(4,128)(2,1)} %param.30) | copy-start | bytes 24580
  167.3 4.3 collective-permute-start.2
  246.4 1.0 copy-start.1

commit v4 on v3

--- a/solution.py
+++ b/solution.py
@@ -11,10 +11,6 @@
 CORES = 2
 SEGS = 8
 PAD = 8
-
-
-def rms_apply(vals, sum_sq, width, gain):
-    return (vals * lax.rsqrt(sum_sq / width + EPS) * (1.0 + gain.astype(jnp.float32))).astype(jnp.bfloat16)
 
 
 def neg_expm1(z):
@@ -509,6 +505,176 @@
     return out.reshape(ring_y * share, cols // 2)
 
 
+def front_kernel(x_ref, gain_ref, w_x_ref, w_y_ref, bias_ref, u_ref, y_ref, nbuf, wbuf, pbuf, opp_buf, side, sums, all_sums, local_sem, ps, pr, xs, xr, ss, sr):
+    tokens, width = x_ref.shape
+    ring_x, _, _, wd, core, chip = ring_refs()
+    wd_count = ring_x * CORES
+    rr = tokens // ROUNDS
+    half = rr // 2
+    mine = y_ref.shape[1]
+    piece = CORES * mine
+    lanes = sums.shape[1]
+    partner = wd + 1 - 2 * core
+    right, opp, left = (lax.rem(chip + step, ring_x) for step in (1, 2, 3))
+
+    def span(r, part=None):
+        return pl.ds(r * rr, rr) if part is None else pl.ds(r * rr + part * half, half)
+
+    def weight(k, of):
+        j, m = k // 2, k % 2
+        src = (w_x_ref, w_y_ref)[m].at[:, pl.ds(pl.multiple_of((j * CORES + of) * mine, mine), mine)]
+        return src, wbuf.at[pl.ds(pl.multiple_of(core * width, width), width), pl.ds(j * piece + m * mine, mine)]
+
+    def weight_out(k):
+        src, dst = weight(k, 1 - core)
+        return pltpu.make_async_remote_copy(src_ref=src, dst_ref=dst, send_sem=ps.at[ROUNDS, k], recv_sem=pr.at[ROUNDS, k], device_id={'wd': partner}, device_id_type=MESH)
+
+    def weight_own(k):
+        src, dst = weight(k, core)
+        return pltpu.make_async_copy(src, dst, local_sem.at[k])
+
+    def weight_in(k):
+        ref = wbuf.at[pl.ds(pl.multiple_of((1 - core) * width, width), width), pl.ds((k // 2) * piece + (k % 2) * mine, mine)]
+        pltpu.make_async_remote_copy(src_ref=ref, dst_ref=ref, send_sem=ps.at[ROUNDS, k], recv_sem=pr.at[ROUNDS, k], device_id={'wd': partner}, device_id_type=MESH).wait_recv()
+
+    def normed(r, of):
+        ref = nbuf.at[span(r), pl.ds(pl.multiple_of(of * width, width), width)]
+        return pltpu.make_async_remote_copy(src_ref=ref, dst_ref=ref, send_sem=ps.at[r, 0], recv_sem=pr.at[r, 0], device_id={'wd': partner}, device_id_type=MESH)
+
+    def u_copy(r):
+        return pltpu.make_async_remote_copy(src_ref=u_ref.at[span(r), pl.ds(0, mine)], dst_ref=u_ref.at[span(r), pl.ds(mine, mine)],
+                                            send_sem=ps.at[r, 1], recv_sem=pr.at[r, 1], device_id={'wd': partner}, device_id_type=MESH)
+
+    def part_of(dest, r, part):
+        return pbuf.at[span(r, part), pl.ds(pl.multiple_of(dest * piece, piece), piece)]
+
+    def x_send(k, r):
+        rows = pl.ds(r * half, half)
+        src, dst, to = {
+            0: (part_of(opp, r, 0), opp_buf.at[0, rows], right),
+            1: (part_of(opp, r, 1), opp_buf.at[1, rows], left),
+            2: (part_of(right, r, 1), side.at[0, span(r, 1)], right),
+            3: (part_of(left, r, 0), side.at[1, span(r, 0)], left),
+            4: (part_of(right, r, 0), side.at[0, span(r, 0)], right),
+            5: (part_of(left, r, 1), side.at[1, span(r, 1)], left),
+        }[k]
+        return pltpu.make_async_remote_copy(src_ref=src, dst_ref=dst, send_sem=xs.at[r, k], recv_sem=xr.at[r, k], device_id={'wd': to * CORES + core}, device_id_type=MESH)
+
+    def norm(r):
+        for i in range(rr // lanes):
+            tile = r * (rr // lanes) + i
+            factor = jnp.broadcast_to(scale[tile:tile + 1, :], (lanes, lanes)).T[:, 0:1]
+            rows = slice(tile * lanes, (tile + 1) * lanes)
+            nbuf[rows, pl.ds(pl.multiple_of(core * width, width), width)] = (x_ref[rows, :].astype(jnp.float32) * factor * gain).astype(jnp.bfloat16)
+        normed(r, core).start()
+
+    def dots(r):
+        normed(r, 1 - core).wait_recv()
+        step_rows = rr // 4
+
+        def one(i, carry):
+            rows = pl.ds(pl.multiple_of(r * rr + i * step_rows, step_rows), step_rows)
+            pbuf[rows, :] = jnp.dot(nbuf[rows, :], wbuf[...], preferred_element_type=jnp.float32).astype(jnp.bfloat16)
+            return carry
+        lax.fori_loop(0, 4, one, 0)
+        for k in range(4):
+            x_send(k, r).start()
+
+    def combine(r):
+        rows = pl.ds(r * half, half)
+        for k, dest, part, back in ((0, right, 0, 4), (1, left, 1, 5)):
+            x_send(k, r).wait_recv()
+            at = (span(r, part), pl.ds(pl.multiple_of(dest * piece, piece), piece))
+            pbuf[at] = (pbuf[at].astype(jnp.float32) + opp_buf[k, rows, :].astype(jnp.float32)).astype(jnp.bfloat16)
+            x_send(back, r).start()
+
+    def final(r):
+        for k in range(2, 6):
+            x_send(k, r).wait_recv()
+        rows = span(r)
+        total = pbuf[rows, pl.ds(pl.multiple_of(chip * piece, piece), piece)].astype(jnp.float32) + side[0, rows, :].astype(jnp.float32) + side[1, rows, :].astype(jnp.float32)
+        total = total + bias_ref[...].astype(jnp.float32)
+        u_ref[rows, 0:mine] = total[:, :mine].astype(jnp.bfloat16)
+        u_copy(r).start()
+        y_ref[rows, :] = jax.nn.gelu(total[:, mine:], approximate=True).astype(jnp.bfloat16)
+
+    barrier = pltpu.get_barrier_semaphore()
+    for step in range(1, wd_count):
+        pl.semaphore_signal(barrier, inc=1, device_id={'wd': lax.rem(wd + step, wd_count)}, device_id_type=MESH)
+    for k in range(2 * ring_x):
+        weight_own(k).start()
+    for i in range(tokens // lanes):
+        sq = jnp.zeros((lanes, lanes), jnp.float32)
+        for j in range(width // lanes):
+            val = x_ref[i * lanes:(i + 1) * lanes, j * lanes:(j + 1) * lanes].astype(jnp.float32)
+            sq = sq + val * val
+        sums[i:i + 1, :] = jnp.sum(sq.T, axis=0, keepdims=True)
+    all_sums[wd] = sums[...]
+    pl.semaphore_wait(barrier, wd_count - 1)
+    for step in range(1, wd_count):
+        pltpu.make_async_remote_copy(src_ref=sums, dst_ref=all_sums.at[wd], send_sem=ss.at[step], recv_sem=sr.at[step], device_id={'wd': lax.rem(wd + step, wd_count)}, device_id_type=MESH).start()
+    for k in range(2 * ring_x):
+        weight_out(k).start()
+    for step in range(1, wd_count):
+        ref = all_sums.at[lax.rem(wd + wd_count - step, wd_count)]
+        pltpu.make_async_remote_copy(src_ref=ref, dst_ref=ref, send_sem=ss.at[step], recv_sem=sr.at[step], device_id={'wd': partner}, device_id_type=MESH).wait_recv()
+    scale = lax.rsqrt(jnp.sum(all_sums[...], axis=0) / (width * wd_count) + EPS)
+    gain = 1.0 + gain_ref[...].astype(jnp.float32)
+    norm(0)
+    for k in range(2 * ring_x):
+        weight_own(k).wait()
+        weight_in(k)
+    for r in range(ROUNDS):
+        if r + 1 < ROUNDS:
+            norm(r + 1)
+        dots(r)
+        if r >= 1:
+            combine(r - 1)
+        if r >= 2:
+            final(r - 2)
+    combine(ROUNDS - 1)
+    final(ROUNDS - 2)
+    final(ROUNDS - 1)
+    for step in range(1, wd_count):
+        pltpu.make_async_remote_copy(src_ref=sums, dst_ref=all_sums.at[wd], send_sem=ss.at[step], recv_sem=sr.at[step], device_id={'wd': partner}, device_id_type=MESH).wait_send()
+    for k in range(2 * ring_x):
+        weight_out(k).wait_send()
+    for r in range(ROUNDS):
+        normed(r, core).wait_send()
+        u_copy(r).wait()
+        for k in range(6):
+            x_send(k, r).wait_send()
+
+
+def front(x, gain, w_x, w_y, bias, ring_x, cid):
+    tokens, width = x.shape
+    rnn = w_x.shape[1]
+    mine = rnn // (ring_x * CORES)
+    lanes = 128
+    vmem, anywhere = pl.BlockSpec(memory_space=pltpu.VMEM), pl.BlockSpec(memory_space=pl.ANY)
+    return pl.pallas_call(
+        front_kernel,
+        out_shape=(jax.ShapeDtypeStruct((tokens, CORES * mine), jnp.bfloat16), jax.ShapeDtypeStruct((tokens, mine), jnp.bfloat16)),
+        in_specs=[vmem, vmem, anywhere, anywhere, vmem],
+        out_specs=(vmem, vmem),
+        scratch_shapes=[
+            pltpu.VMEM((tokens, CORES * width), jnp.bfloat16),
+            pltpu.VMEM((CORES * width, rnn), jnp.bfloat16),
+            pltpu.VMEM((tokens, rnn), jnp.bfloat16),
+            pltpu.VMEM((2, tokens // 2, CORES * mine), jnp.bfloat16),
+            pltpu.VMEM((2, tokens, CORES * mine), jnp.bfloat16),
+            pltpu.VMEM((tokens // lanes, lanes), jnp.float32),
+            pltpu.VMEM((ring_x * CORES, tokens // lanes, lanes), jnp.float32),
+            pltpu.SemaphoreType.DMA((2 * ring_x,)),
+            pltpu.SemaphoreType.DMA((ROUNDS + 1, 2 * ring_x)), pltpu.SemaphoreType.DMA((ROUNDS + 1, 2 * ring_x)),
+            pltpu.SemaphoreType.DMA((ROUNDS, 6)), pltpu.SemaphoreType.DMA((ROUNDS, 6)),
+            pltpu.SemaphoreType.DMA((ring_x * CORES,)), pltpu.SemaphoreType.DMA((ring_x * CORES,)),
+        ],
+        compiler_params=pltpu.CompilerParams(collective_id=cid, has_side_effects=True, vmem_limit_bytes=56 << 20),
+        name='front',
+    )(x, gain, w_x, w_y, bias)
+
+
 def solution(mesh):
     wd_count = mesh.shape['wd']
     ch_count = mesh.shape['ch']
@@ -537,20 +703,7 @@
             return jnp.where(core == 0, pair, jnp.concatenate([pair[..., mine:], pair[..., :mine]], axis=-1))
 
         ff = w_g.shape[1] // wd_count
-        resid32 = resid_in.astype(jnp.float32)
-        sum_sq = lax.psum(jnp.sum(resid32 * resid32, axis=1, keepdims=True), 'wd')
-        normed = rms_apply(resid32, sum_sq, model_width, gain_temporal)
-        normed_pair = lax.ppermute(normed, 'wd', swap)
-        w_xy = jnp.concatenate([w_x.reshape(local_width, chips, CORES, mine), w_y.reshape(local_width, chips, CORES, mine)], axis=3)
-        w_keep = lax.dynamic_index_in_dim(w_xy, core, 2, keepdims=False).reshape(local_width, rnn)
-        w_send = lax.dynamic_index_in_dim(w_xy, 1 - core, 2, keepdims=False).reshape(local_width, rnn)
-        w_pair = lax.ppermute(w_send, 'wd', swap)
-        part = (jnp.dot(normed, w_keep, preferred_element_type=jnp.float32) + jnp.dot(normed_pair, w_pair, preferred_element_type=jnp.float32)).astype(jnp.bfloat16)
-        got = lax.all_to_all(part.reshape(tokens, chips, CORES * mine).transpose(1, 0, 2), 'wd', 0, 0, axis_index_groups=same_core)
-        uy = jnp.sum(got.astype(jnp.float32), axis=0)
-        u_own = (uy[:, :mine] + own(bias_x).astype(jnp.float32)).astype(jnp.bfloat16)
-        y_own = jax.nn.gelu(uy[:, mine:] + own(bias_y).astype(jnp.float32), approximate=True).astype(jnp.bfloat16)
-        u_pair = jnp.concatenate([u_own, lax.ppermute(u_own, 'wd', swap)], axis=1)
+        u_pair, y_own = front(resid_in, gain_temporal[None], w_x, w_y, jnp.concatenate([own(bias_x), own(bias_y)])[None], chips, 5)
         gate_w = jnp.concatenate([lax.dynamic_index_in_dim(w, block, 0, keepdims=False) for w in (rgate_w, igate_w)], axis=1)
         gate_w = gate_w.reshape(CORES, mine, 2, CORES, mine)
         gate_w = lax.dynamic_index_in_dim(gate_w, core, 3, keepdims=False).reshape(CORES, mine, 2 * mine)

time: 590 us -> 527 us (0.89)
  Pallas kernels: 410 us -> 502 us
  waiting for transfers between devices: 79.8 us -> 0 us
  blocking collectives: 24 us -> 0 us
  matrix products: 21.9 us -> 0 us
  other arithmetic: 17.3 us -> 1.52 us
  starting transfers between devices: 11.2 us -> 0 us
    pallas_call x0 -> x1, Pallas kernels: none -> 91.2 us  [front(): pl.pallas_call(front_kernel, out_shape=(jax.ShapeDtypeStruct((tokens, COR...]
    all_to_all x1 -> x0, waiting for transfers between devices: 79.8 us -> none  [local_layer(): lax.all_to_all(part.reshape(tokens, chips, CORES * mine).transpose(1, 0,...]
    psum x1 -> x0, blocking collectives: 24 us -> none  [local_layer(): sum_sq = lax.psum(jnp.sum(resid32 * resid32, axis=1, keepdims=True), 'wd')]
    dot_general x2 -> x0, matrix products: 21.9 us -> none  [the longest x1 11.5 us: local_layer(): jnp.dot(normed_pair, w_pair, preferred_element_type=jnp.float32)]
    reduce_sum x2 -> x0, other arithmetic: 8.61 us -> none  [the longest x1 5.51 us: local_layer(): uy = jnp.sum(got.astype(jnp.float32), axis=0)]
    convert_element_type x5 -> x0, other arithmetic: 6.67 us -> none  [the longest x1 4.3 us: rms_apply(): (vals * lax.rsqrt(sum_sq / width + EPS) * (1.0 + gain.astype(jnp.float32)...]
    all_to_all x1 -> x0, starting transfers between devices: 6.02 us -> none  [local_layer(): lax.all_to_all(part.reshape(tokens, chips, CORES * mine).transpose(1, 0,...]
  transfers between devices with their start and end apart: 4 -> 0, of which waited for: 1 -> 0; matrix products, arithmetic and copies ran while one was open for 5% -> 0% of each run, Pallas kernels for 0% -> 0%
where the time goes in v4:
time: 527 us; the launch traced here: 526 us
  Pallas kernels  502 us (95%)
  local copies, waits for them, and re-layouts  22.9 us (4%)
    pallas_call x2, Pallas kernels, ring_layer(): pl.pallas_call(functools.partial(ring_kernel, regather), out_shape=out, i...  224 us
    pallas_call x1, Pallas kernels, mlp_in(): pl.pallas_call(mlp_in_kernel, out_shape=jax.ShapeDtypeStruct((ring_y, sha...  113 us
    pallas_call x1, Pallas kernels, front(): pl.pallas_call(front_kernel, out_shape=(jax.ShapeDtypeStruct((tokens, COR...  91.2 us
    pallas_call x1, Pallas kernels, lru(): pl.pallas_call(lru_kernel, out_shape=(jax.ShapeDtypeStruct((tokens, width...  73.1 us

profile of v4, /device:TPU:97, one launch (start us, length us, event | category | flops | bytes accessed | tf_op | source)
XLA Modules:
  0.0 526.2 jit_solution(6687236842435131088)
XLA Ops:
  0.0 0.0 copy-start
  0.0 1.0 dynamic-slice_bitcast_fusion
  1.0 0.1 reshape.16
  1.1 0.3 constant_dynamic-slice_fusion.3
  1.4 0.1 copy.25
  1.6 0.1 copy.26
  1.7 0.7 constant_dynamic-slice_fusion.1
  2.4 0.7 maximum_select_fusion.taps_ref
  3.1 0.8 dynamic_slice.44
  3.9 0.8 broadcast_select_fusion
  4.6 0.8 dynamic_slice.41
  5.4 0.8 dynamic_slice.42
  6.2 0.6 broadcast_in_dim.28.bias_ref
  6.7 1.3 broadcast_in_dim.27.gain_ref
  8.0 0.0 copy-start.4
  8.0 91.2 %front.1 = (bf16[4096,256]{1,0:T(8,128)(2,1)}, bf16[4096,128]{1,0:T(8,128)(2,1)}) custom-call(bf16[4096,512]{1,0:T(8,128)(2,1)} %x_ref.1, bf16[1,512]{1,0:T(2,128)(2,1)} %broadcast_in_dim.27.gain_ref, bf16[512,1024]{1,0:T(8,128)(2,1)} %w_x_ref.1, bf16[512,1024]{1,0:T(8,128)(2,1)} %w_y_ref.1, bf16[1,256]{1,0:T(2,128)(2,1)} %broadcast_in_dim.28.bias_ref), custom_call_target="tpu_custom_call" | custom-call | tf_op jit(solution)/shard_map/front/pallas_call | solution.py:655
  99.2 0.0 copy-start.1
  99.2 0.9 dynamic_slice.48
  100.1 0.8 dynamic_slice.49
  100.9 0.0 copy-done
  100.9 0.1 dynamic-slice_bitcast_fusion.2.lam_ref
  101.0 0.0 copy-done.4
  101.0 2.0 copy.27.pos_ref
  103.0 0.0 copy-done.1
  103.0 0.0 copy-start.3
  103.0 1.2 copy-done.3
  104.2 0.0 copy-start.5
  104.2 73.1 %lru.1 = (bf16[4096,128]{1,0:T(8,128)(2,1)S(1)}, bf16[2,2048,768]{2,1,0:T(8,128)(2,1)}) custom-call(bf16[4096,256]{1,0:T(8,128)(2,1)S(1)} %copy-done.1, bf16[4096,128]{1,0:T(8,128)(2,1)S(1)} %copy-done.3, s32[4096,1]{1,0:T(8,128)} %copy.27.pos_ref, bf16[4,256]{1,0:T(4,128)(2,1)S(1)} %maximum_select_fusion.taps_ref, ...), custom_call_target="tpu_custom_call" | custom-call | tf_op jit(solution)/shard_map/lru/pallas_call | solution.py:127
  177.3 0.0 copy-start.2
  177.3 1.0 copy-done.2
  178.2 2.3 constant_dynamic-slice_fusion.2.resid_ref
  180.5 0.0 copy-done.5
  180.5 0.0 copy-start.6
  180.5 0.6 broadcast_in_dim.32.bias_ref
  181.1 68.3 %ring_layer.2.resid_ref = f32[1024,512]{1,0:T(8,128)} custom-call(bf16[4,1024,128]{2,1,0:T(8,128)(2,1)} %bitcast.11, bf16[1024,512]{1,0:T(8,128)(2,1)} %w_ref.2, bf16[1024,512]{1,0:T(8,128)(2,1)} %constant_dynamic-slice_fusion.2.resid_ref, bf16[1,512]{1,0:T(2,128)(2,1)} %broadcast_in_dim.32.bias_ref), custom_call_target="tpu_custom_call" | custom-call | tf_op jit(solution)/shard_map/ring_layer/pallas_call | solution.py:311
  249.4 0.8 dynamic_slice.52
  250.2 0.8 dynamic_slice.53
  250.9 0.6 broadcast_in_dim.34.bias_ref
  251.5 0.0 copy-done.6
  251.5 0.6 broadcast_in_dim.33.gain_ref
  252.1 0.0 copy-start.7
  252.1 113.0 %mlp_in.1.h_ref = bf16[4,1024,384]{2,1,0:T(8,128)(2,1)} custom-call(f32[1024,512]{1,0:T(8,128)} %ring_layer.2.resid_ref, bf16[1,512]{1,0:T(2,128)(2,1)} %broadcast_in_dim.33.gain_ref, bf16[2,2048,768]{2,1,0:T(8,128)(2,1)} %get-tuple-element.12.w_ref, bf16[1,768]{1,0:T(2,128)(2,1)} %broadcast_in_dim.34.bias_ref), custom_call_target="tpu_custom_call" | custom-call | tf_op jit(solution)/shard_map/mlp_in/pallas_call | solution.py:487
  365.1 0.0 copy-done.7
  365.1 0.6 broadcast_in_dim.35.bias_ref
  365.7 156.0 %ring_layer.3 = bf16[4,1024,512]{2,1,0:T(8,128)(2,1)} custom-call(bf16[4,1024,384]{2,1,0:T(8,128)(2,1)} %mlp_in.1.h_ref, bf16[3072,512]{1,0:T(8,128)(2,1)} %w_ref.3, f32[1024,512]{1,0:T(8,128)} %ring_layer.2.resid_ref, bf16[1,512]{1,0:T(2,128)(2,1)} %broadcast_in_dim.35.bias_ref), custom_call_target="tpu_custom_call" | custom-call | tf_op jit(solution)/shard_map/ring_layer/pallas_call | solution.py:311
  521.7 4.5 copy.29
  (8 shorter events, 0.1 us)
Async XLA Ops:
  0.0 100.9 %copy-start = (f32[1024]{0:T(1024)S(1)}, f32[1024]{0:T(1024)}, u32[]{:S(2)}) copy-start(f32[1024]{0:T(1024)} %param.32) | copy-start | bytes 12292
  8.0 93.0 %copy-start.4 = (s32[1,4096]{1,0:T(1,128)S(1)}, s32[1,4096]{1,0:T(1,128)}, u32[]{:S(2)}) copy-start(s32[1,4096]{1,0:T(1,128)} %param.24) | copy-start | bytes 49156
  99.2 3.8 copy-start.1
  103.0 1.2 copy-start.3
  104.2 76.3 %copy-start.5 = (bf16[512]{0:T(512)(128)(2,1)S(1)}, bf16[512]{0:T(512)(128)(2,1)}, u32[]{:S(2)}) copy-start(bf16[512]{0:T(512)(128)(2,1)} %param.38) | copy-start | bytes 3076
  177.3 1.0 copy-start.2
  180.5 71.0 %copy-start.6 = (bf16[512]{0:T(512)(128)(2,1)S(1)}, bf16[512]{0:T(512)(128)(2,1)}, u32[]{:S(2)}) copy-start(bf16[512]{0:T(512)(128)(2,1)} %param.39) | copy-start | bytes 3076
  252.1 113.0 %copy-start.7 = (bf16[512]{0:T(512)(128)(2,1)S(1)}, bf16[512]{0:T(512)(128)(2,1)}, u32[]{:S(2)}) copy-start(bf16[512]{0:T(512)(128)(2,1)} %param.45) | copy-start | bytes 3076

commit v5 on v0

v5 whole, which is shorter than its diff:
```python
import functools

import jax
import jax.numpy as jnp
from jax import lax
from jax.experimental import pallas as pl
from jax.experimental.pallas import tpu as pltpu
from jax.sharding import PartitionSpec as P

EPS = 1e-6
CORES = 2
SEGS = 8
PAD = 8
LANES = 128
RIGHT, OPP, LEFT = 1, 2, 3
MESH = pl.DeviceIdType.MESH
F32 = jnp.float32
BF16 = jnp.bfloat16
VMEM = pl.BlockSpec(memory_space=pltpu.VMEM)
ANY = pl.BlockSpec(memory_space=pl.ANY)
DMA = pltpu.SemaphoreType.DMA


def neg_expm1(z):
    series = -z * (1.0 + z * (0.5 + z * (1.0 / 6.0 + z * (1.0 / 24.0))))
    return jnp.where(z > -0.03, series, 1.0 - jnp.exp(z))


def where_am_i():
    ring_x = lax.axis_size('wd') // CORES
    wd = lax.axis_index('wd')
    return ring_x, lax.axis_size('ch'), lax.axis_index('ch'), wd, lax.rem(wd, CORES), wd // CORES


def aligned(index, size):
    return pl.ds(pl.multiple_of(index * size, size), size)


def remote(src, dst, send, recv, device):
    return pltpu.make_async_remote_copy(src_ref=src, dst_ref=dst, send_sem=send, recv_sem=recv, device_id=device, device_id_type=MESH)


def greet(devices):
    barrier = pltpu.get_barrier_semaphore()
    for device in devices:
        pl.semaphore_signal(barrier, inc=1, device_id=device, device_id_type=MESH)
    return functools.partial(pl.semaphore_wait, barrier, len(devices))


def chip_peers():
    ring_x, _, _, _, core, chip = where_am_i()
    return [{'wd': lax.rem(chip + step, ring_x) * CORES + core} for step in range(1, ring_x)]


def swaps(src, dst, k, sends, recvs):
    ring_x, _, _, _, core, chip = where_am_i()
    depth, ff = src.shape[0], dst.shape[1]
    return [remote(src.at[:, aligned(lax.rem(chip + step, ring_x) * CORES + k, ff)], dst.at[aligned(chip, depth), :],
                   sends.at[step], recvs.at[step], {'wd': lax.rem(chip + step, ring_x) * CORES + core}) for step in range(1, ring_x)]


def row_sums(x_ref, sums):
    for i in range(x_ref.shape[0] // LANES):
        sq = jnp.zeros((LANES, LANES), F32)
        for j in range(x_ref.shape[1] // LANES):
            val = x_ref[i * LANES:(i + 1) * LANES, j * LANES:(j + 1) * LANES].astype(F32)
            sq = sq + val * val
        sums[i:i + 1, :] = jnp.sum(sq.T, axis=0, keepdims=True)


def sum_copies(sums, all_sums, ss, sr):
    ring_x, _, _, wd, _, _ = where_am_i()
    count = ring_x * CORES
    return [remote(sums, all_sums.at[wd], ss.at[step], sr.at[step], {'wd': lax.rem(wd + step, count)}) for step in range(1, count)]


def as_column(row):
    return jnp.broadcast_to(row, (LANES, LANES)).T


def lru_kernel(offs, u_ref, y_ref, pos_ref, vec_ref, rg_ref, ig_ref, w_ref, out_ref, part_ref, u32, a_s, b_s, gate_w, ws, wr):
    ring_x, _, _, wd, core, chip = where_am_i()
    tokens, wide = u_ref.shape
    width = y_ref.shape[1]
    tile = tokens // SEGS
    pitch = tile + PAD
    per_seg = tile // LANES
    rnn = offs['rnn']
    n_taps = offs['taps']

    def vec(name, index, size):
        return vec_ref[:, pl.ds(pl.multiple_of(offs[name] + index * size, size), size)]

    ready = greet(chip_peers())
    taps = [vec_ref[:, pl.ds(pl.multiple_of(offs['conv_w'] + k * rnn + chip * wide, wide), wide)] for k in range(n_taps)]
    cbias = vec('conv_bias', chip, wide)
    gate_b = jnp.concatenate([vec('rgate_b', wd, width), vec('igate_b', wd, width)], axis=1)
    lam = -vec('lam_param', wd, width)
    soft = -8.0 * (jnp.maximum(lam, 0.0) + jnp.log(1.0 + jnp.exp(-jnp.abs(lam))))
    gate_w[:, :width] = rg_ref[chip, :, aligned(core, width)]
    gate_w[:, width:] = ig_ref[chip, :, aligned(core, width)]
    u32[0:PAD, :] = jnp.zeros((PAD, wide), F32)
    ready()
    moves = swaps(w_ref, part_ref, 0, ws, wr)
    for one in moves:
        one.start()

    def widen(i, carry):
        rows = pl.multiple_of(i * tile, tile)
        u32[pl.ds(rows + PAD, tile), :] = u_ref[pl.ds(rows, tile), :].astype(F32)
        return carry
    lax.fori_loop(0, SEGS, widen, 0)

    def gates(i, carry):
        rows = pl.multiple_of(i * LANES, LANES)
        window = u32[pl.ds(rows, LANES + PAD), :]
        pos = as_column(pos_ref[:, pl.ds(rows, LANES)].astype(F32))
        pair = jnp.concatenate([pos, pos], axis=1)
        total = cbias + window[PAD:] * taps[0]
        for k in range(1, n_taps):
            total = total + jnp.where(pair >= k, window[PAD - k:PAD - k + LANES], 0.0) * taps[k]
        conv = total.astype(BF16)
        both = jax.nn.sigmoid(jnp.dot(conv, gate_w[...], preferred_element_type=F32) + gate_b)
        log_a = both[:, :width] * soft
        reset = pos == 0
        decay = jnp.where(reset, 0.0, jnp.exp(log_a))
        scale = jnp.where(reset, 1.0, jnp.sqrt(neg_expm1(2.0 * log_a)))
        mine = conv.astype(F32)
        drive = scale * both[:, width:] * jnp.where(core == 0, mine[:, :width], mine[:, width:])
        seg = i // per_seg
        at = pl.multiple_of(seg * pitch + (i - seg * per_seg) * LANES, PAD)
        a_s[pl.ds(at, LANES), :] = decay
        b_s[pl.ds(at, LANES), :] = drive
        return carry
    lax.fori_loop(0, tokens // LANES, gates, 0)

    def steps(i, carry):
        hid, acc = carry
        for j in range(8):
            at = pl.ds(i * 8 + j, SEGS, stride=pitch)
            a = a_s[at, :]
            hid = a * hid + b_s[at, :]
            acc = a * acc
            b_s[at, :] = hid
            a_s[at, :] = acc
        return hid, acc
    hid, acc = lax.fori_loop(0, tile // 8, steps, (jnp.zeros((SEGS, width), F32), jnp.ones((SEGS, width), F32)))

    entry = jnp.zeros((1, width), F32)
    for seg in range(SEGS):
        for q in range(per_seg):
            at = seg * pitch + q * LANES
            hidden = b_s[at:at + LANES, :] + a_s[at:at + LANES, :] * entry
            rows = slice(seg * tile + q * LANES, seg * tile + (q + 1) * LANES)
            out_ref[rows, :] = (hidden * y_ref[rows, :].astype(F32)).astype(BF16)
        entry = hid[seg:seg + 1] + acc[seg:seg + 1] * entry
    for one in moves:
        one.wait()


def lru(offs, u_pair, y_rows, pos, vec, rgate_w, igate_w, weight, part, ring_x, cid):
    tokens, wide = u_pair.shape
    width = y_rows.shape[1]
    rows = SEGS * (tokens // SEGS + PAD)
    return pl.pallas_call(
        functools.partial(lru_kernel, offs),
        out_shape=(jax.ShapeDtypeStruct((tokens, width), BF16), part),
        in_specs=[VMEM] * 6 + [ANY],
        out_specs=(VMEM, ANY),
        scratch_shapes=[pltpu.VMEM((tokens + PAD, wide), F32), pltpu.VMEM((rows, width), F32), pltpu.VMEM((rows, width), F32),
                        pltpu.VMEM((wide, 2 * width), BF16), DMA((ring_x,)), DMA((ring_x,))],
        compiler_params=pltpu.CompilerParams(collective_id=cid, has_side_effects=True, vmem_limit_bytes=48 << 20),
        name='lru',
    )(u_pair, y_rows, pos, vec, rgate_w, igate_w, weight)


def ring_kernel(rounds, regather, bias_at, h_ref, w_ref, resid_ref, vec_ref, *refs):
    if regather:
        out_ref, hbuf, pbuf, opp_buf, side, resid, xs, xr, ys, yr, local_sem = refs
    else:
        wg_ref, wu_ref, out_ref, part_g, part_u, hbuf, pbuf, opp_buf, side, resid, xs, xr, ys, yr, local_sem, ws, wr = refs
    share, depth = h_ref.shape[1:]
    cols_out = w_ref.shape[1]
    rr = share // rounds
    half = rr // 2
    ring_x, ring_y, ch, wd, core, chip = where_am_i()
    other = 1 - 2 * core
    partner = wd + other
    x_at = [lax.rem(chip + step, ring_x) * CORES + core for step in range(ring_x)]
    y_at = [lax.rem(ch + step, ring_y) for step in range(ring_y)]
    first, second, whole = 0, 1, None

    def span(r, part=None):
        return pl.ds(r * rr, rr) if part is None else pl.ds(r * rr + part * half, half)

    def cols(owner, r, part=None):
        return hbuf.at[:, span(r, part), aligned(owner, depth)]

    x_plan = [(wd, whole, x_at[RIGHT], x_at[LEFT]), (wd, whole, x_at[LEFT], x_at[RIGHT]),
              (x_at[LEFT], first, x_at[RIGHT], x_at[OPP]), (x_at[RIGHT], second, x_at[LEFT], x_at[OPP]),
              (wd, whole, partner, partner), (x_at[LEFT], whole, partner, x_at[LEFT] + other), (x_at[RIGHT], whole, partner, x_at[RIGHT] + other),
              (x_at[OPP], first, partner, x_at[OPP] + other), (x_at[OPP], second, partner, x_at[OPP] + other)]
    own_both, own_side, relay_both, side_both, opp_both, core_in = (0, 1), (4,), (2, 3), (5, 6), (7, 8), (4, 5, 6, 7, 8)

    def x_copy(k, r):
        owner, part, to, _ = x_plan[k]
        dst = cols(owner, r, part)
        src = h_ref.at[:, span(r), :] if k in own_both + own_side else dst
        return remote(src, dst, xs.at[r, k], xr.at[r, k], {'wd': to})

    def x_start(r, *ks):
        for k in ks:
            x_copy(k, r).start()

    def x_wait(r, *ks):
        for k in ks:
            ref = cols(x_plan[k][-1], r, x_plan[k][1])
            remote(ref, ref, xs.at[r, k], xr.at[r, k], {'wd': partner}).wait_recv()

    def y_refs(k, r):
        rows = pl.ds(r * half, half)
        sums = [(OPP, first, opp_buf.at[0, rows], RIGHT), (OPP, second, opp_buf.at[1, rows], LEFT),
                (RIGHT, second, side.at[0, span(r, second)], RIGHT), (LEFT, first, side.at[1, span(r, first)], LEFT),
                (RIGHT, first, side.at[0, span(r, first)], RIGHT), (LEFT, second, side.at[1, span(r, second)], LEFT)]
        if k < len(sums):
            piece, part, dst, to = sums[k]
            return pbuf.at[y_at[piece], span(r, part)], dst, to, dst
        owner, part, to, got = [(0, whole, RIGHT, LEFT), (0, whole, LEFT, RIGHT), (LEFT, first, RIGHT, OPP), (RIGHT, second, LEFT, OPP)][k - len(sums)]
        src = out_ref.at[y_at[owner], span(r, part)]
        return src, src, to, out_ref.at[y_at[got], span(r, part)]

    to_opp, to_side, relayed, out_own, out_relay = (0, 1), (2, 3), (4, 5), (6, 7), (8, 9)

    def y_start(r, *ks):
        for k in ks:
            src, dst, to, _ = y_refs(k, r)
            remote(src, dst, ys.at[r, k], yr.at[r, k], {'ch': y_at[to]}).start()

    def y_wait(r, *ks):
        for k in ks:
            ref = y_refs(k, r)[-1]
            remote(ref, ref, ys.at[r, k], yr.at[r, k], {'ch': y_at[RIGHT]}).wait_recv()

    def own(r):
        if r < rounds:
            x_start(r, *own_both, *own_side)

    def stage1(r):
        if r < rounds:
            for side_in, on in zip(own_both, relay_both):
                x_wait(r, side_in)
                x_start(r, on)
            x_start(r, *side_both)
            own(r + 2)
            if not regather and r == rounds - 1:
                for one in moves:
                    one.start()

    def stage2(r):
        for side_in, on in zip(relay_both, opp_both):
            x_wait(r, side_in)
            x_start(r, on)

    def dots(r):
        x_wait(r, *core_in)
        each = max(1, 256 // rr)

        def one(i, carry):
            at = pl.ds(i * each, each)
            block = hbuf[at, pl.ds(r * rr, rr), :].reshape(each * rr, hbuf.shape[2])
            part = jnp.dot(block, w_ref[...], preferred_element_type=F32)
            pbuf[at, pl.ds(r * rr, rr), :] = part.astype(BF16).reshape(each, rr, cols_out)
            return carry
        lax.fori_loop(0, ring_y // each, one, 0)
        y_start(r, *to_opp, *to_side)

    def combine(r):
        for k, piece, part in zip(to_opp, (RIGHT, LEFT), (first, second)):
            y_wait(r, k)
            at = y_at[piece], span(r, part)
            pbuf[at] = (pbuf[at].astype(F32) + opp_buf[k, pl.ds(r * half, half), :].astype(F32)).astype(BF16)
            y_start(r, relayed[k])

    def final(r):
        y_wait(r, *to_side, *relayed)
        rows = span(r)
        total = pbuf[ch, rows, :].astype(F32) + side[0, rows, :].astype(F32) + side[1, rows, :].astype(F32)
        total = resid[rows, :].astype(F32) + total + vec_ref[:, bias_at:bias_at + cols_out]
        if regather:
            out_ref[ch, rows, :] = total.astype(out_ref.dtype)
            y_start(r, *out_own)
        else:
            out_ref[rows, :] = total.astype(out_ref.dtype)

    def relay(r):
        if regather:
            y_wait(r, *out_own)
            y_start(r, *out_relay)

    peers = [{'wd': partner}, {'ch': y_at[LEFT]}, {'ch': y_at[RIGHT]}]
    if regather:
        ready = greet(peers + [{'wd': x_at[LEFT]}, {'wd': x_at[RIGHT]}])
        resid_rows = resid_ref
    else:
        ready = greet(peers + chip_peers())
        moves = swaps(wg_ref, part_g, 1, ws.at[0], wr.at[0]) + swaps(wu_ref, part_u, 1, ws.at[1], wr.at[1])
        resid_rows = resid_ref.at[aligned(ch, share), :]
    local = [pltpu.make_async_copy(h_ref, hbuf.at[:, :, aligned(wd, depth)], local_sem.at[0]), pltpu.make_async_copy(resid_rows, resid, local_sem.at[1])]
    for one in local:
        one.start()
    ready()
    own(0)
    own(1)
    for one in local:
        one.wait()
    stage1(0)
    for r in range(rounds):
        stage1(r + 1)
        stage2(r)
        if r >= 1:
            combine(r - 1)
        dots(r)
        if r >= 1:
            final(r - 1)
        if r >= 2:
            relay(r - 2)
    combine(rounds - 1)
    relay(rounds - 2)
    final(rounds - 1)
    relay(rounds - 1)
    for r in range(rounds):
        if regather:
            y_wait(r, *out_relay)
        for k in range(len(x_plan)):
            x_copy(k, r).wait_send()
        for k in range(10 if regather else 6):
            src, dst, to, _ = y_refs(k, r)
            remote(src, dst, ys.at[r, k], yr.at[r, k], {'ch': y_at[to]}).wait_send()
    if not regather:
        for one in moves:
            one.wait()


def ring_layer(h, w, resid, vec, bias_at, weights, part, ring_x, ring_y, rounds, cid):
    tokens, depth = h.shape
    share = tokens // ring_y
    wide, cols = w.shape
    regather = not weights
    out = jax.ShapeDtypeStruct((ring_y, share, cols), BF16) if regather else (jax.ShapeDtypeStruct((share, cols), F32), part, part)
    res = pl.pallas_call(
        functools.partial(ring_kernel, rounds, regather, bias_at),
        out_shape=out,
        in_specs=[ANY, VMEM, ANY, VMEM] + [ANY] * len(weights),
        out_specs=VMEM if regather else (VMEM, ANY, ANY),
        scratch_shapes=[
            pltpu.VMEM((ring_y, share, wide), BF16),
            pltpu.VMEM((ring_y, share, cols), BF16),
            pltpu.VMEM((2, share // 2, cols), BF16),
            pltpu.VMEM((2, share, cols), BF16),
            pltpu.VMEM((share, cols), resid.dtype),
            DMA((rounds, 9)), DMA((rounds, 9)), DMA((rounds, 10)), DMA((rounds, 10)), DMA((2,)),
        ] + ([] if regather else [DMA((2, ring_x)), DMA((2, ring_x))]),
        compiler_params=pltpu.CompilerParams(collective_id=cid, has_side_effects=True, vmem_limit_bytes=60 << 20),
        name='ring_layer',
    )(h.reshape(ring_y, share, depth), w, resid, vec, *weights)
    return res.reshape(tokens, cols) if regather else res


def mlp_in_kernel(rounds, offs, resid_ref, vec_ref, wg_ref, wu_ref, g0_ref, u0_ref, g1_ref, u1_ref, out_ref, nbuf, w_ref, keep, send, got, sums, all_sums, ns, nr, ss, sr, local_sem):
    share, width = resid_ref.shape
    ring_x, ring_y, ch, wd, core, chip = where_am_i()
    wd_count = ring_x * CORES
    rr = share // rounds
    half = rr // 2
    partner = wd + 1 - 2 * core
    ff = out_ref.shape[2]

    def device(d1, d2):
        return {'ch': lax.rem(ch + d1 * (1 - core) + d2 * core, ring_y), 'wd': lax.rem(chip + d1 * core + d2 * (1 - core), ring_x) * CORES + core}

    def block(d1, d2, r, part=None):
        rows = pl.ds(r * rr, rr) if part is None else pl.ds(r * rr + part * half, half)
        at = lax.rem(chip + d1 * core + d2 * (1 - core), ring_x)
        return nbuf.at[lax.rem(ch + d1 * (1 - core) + d2 * core, ring_y), rows, aligned(at, width)]

    whole = None
    plan = [((0, 0), (RIGHT, 0), (LEFT, 0), whole), ((0, 0), (LEFT, 0), (RIGHT, 0), whole),
            ((LEFT, 0), (RIGHT, 0), (OPP, 0), 0), ((RIGHT, 0), (LEFT, 0), (OPP, 0), 1)]
    for d1 in (0, LEFT, RIGHT, OPP):
        plan += [((d1, 0), (0, RIGHT), (d1, LEFT), whole), ((d1, 0), (0, LEFT), (d1, RIGHT), whole),
                 ((d1, LEFT), (0, RIGHT), (d1, OPP), 0), ((d1, RIGHT), (0, LEFT), (d1, OPP), 1)]
    core_step = len(plan)

    def copy(k, r):
        src, to, _, part = plan[k]
        ref = block(*src, r, part)
        return remote(ref, ref, ns.at[r, k], nr.at[r, k], device(*to))

    def start(r, *ks):
        for k in ks:
            copy(k, r).start()

    def wait(r, *ks):
        for k in ks:
            ref = block(*plan[k][2], r, plan[k][3])
            remote(ref, ref, ns.at[r, k], nr.at[r, k], device(RIGHT, 0)).wait_recv()

    def own(r):
        if r < rounds:
            start(r, 0, 1, 4, 5)

    def stage1(r):
        if r < rounds:
            wait(r, 0, 1)
            start(r, 2, 3, 8, 9, 12, 13)
            wait(r, 4, 5)
            start(r, 6, 7)

    def stage2(r):
        if r < rounds:
            wait(r, 2, 3)
            start(r, 16, 17)
            wait(r, 8, 9)
            start(r, 10, 11)
            wait(r, 12, 13)
            start(r, 14, 15)

    def stage3(r):
        if r < rounds:
            wait(r, 16, 17)
            start(r, 18, 19)

    def halves(r):
        return remote(send.at[r], got.at[r], ns.at[r, core_step], nr.at[r, core_step], {'wd': partner})

    each = max(1, 256 // rr)

    def dots(r, mine):
        def one(i, carry):
            at = pl.ds(i * each, each)
            rows = nbuf[at, pl.ds(r * rr, rr), :].reshape(each * rr, nbuf.shape[2])
            if mine:
                keep[at] = jnp.dot(rows, w_ref[core], preferred_element_type=F32).reshape(each, rr, 2 * ff)
            else:
                send[r, at] = jnp.dot(rows, w_ref[1 - core], preferred_element_type=F32).astype(BF16).reshape(each, rr, 2 * ff)
            return carry
        lax.fori_loop(0, ring_y // each, one, 0)

    def finish(r):
        halves(r).wait_recv()
        b_g, b_u = (vec_ref[:, pl.ds(pl.multiple_of(offs[name] + wd * ff, LANES), ff)] for name in ('bias_g', 'bias_u'))

        def one(q, carry):
            total = keep[q] + got[r, q].astype(F32)
            out_ref[q, pl.ds(r * rr, rr), :] = (jax.nn.gelu(total[:, :ff] + b_g, approximate=True) * (total[:, ff:] + b_u)).astype(BF16)
            return carry
        lax.fori_loop(0, ring_y, one, 0)

    ready = greet([{'wd': lax.rem(wd + step, wd_count)} for step in range(1, wd_count)] + [{'ch': lax.rem(ch + step, ring_y)} for step in (RIGHT, LEFT)])
    loads = []
    for k, (g_part, u_part) in enumerate(((g0_ref, u0_ref), (g1_ref, u1_ref))):
        for m, (full, part) in enumerate(((wg_ref, g_part), (wu_ref, u_part))):
            sems = local_sem.at[k, m]
            for step in range(ring_x):
                rows = aligned(lax.rem(chip + step, ring_x), width)
                src = part.at[rows, :] if step else full.at[:, aligned(chip * CORES + k, ff)]
                loads.append(pltpu.make_async_copy(src, w_ref.at[k, rows, pl.ds(m * ff, ff)], sems.at[step]))
    for one in loads:
        one.start()
    row_sums(resid_ref, sums)
    all_sums[wd] = sums[...]
    ready()
    for one in sum_copies(sums, all_sums, ss, sr):
        one.start()
    for one in sum_copies(sums, all_sums, ss, sr):
        one.wait()
    scale = lax.rsqrt(jnp.sum(all_sums[...], axis=0) / (width * wd_count) + EPS)
    gain = 1.0 + vec_ref[:, offs['gain_mlp']:offs['gain_mlp'] + width]

    def norm(r):
        for i in range(r * rr // LANES, (r + 1) * rr // LANES):
            factor = as_column(scale[i:i + 1, :])[:, 0:1]
            rows = slice(i * LANES, (i + 1) * LANES)
            nbuf[ch, rows, aligned(chip, width)] = (resid_ref[rows, :] * factor * gain).astype(BF16)

    for r in range(rounds):
        norm(r)
        if r < 3:
            own(r)
    stage1(0)
    stage2(0)
    stage1(1)
    stage3(0)
    stage2(1)
    for one in loads:
        one.wait()
    for r in range(rounds):
        wait(r, 6, 7, 10, 11, 14, 15, 18, 19)
        dots(r, False)
        halves(r).start()
        own(r + 3)
        stage1(r + 2)
        stage3(r + 1)
        dots(r, True)
        stage2(r + 2)
        finish(r)
    for r in range(rounds):
        halves(r).wait_send()
        for k in range(core_step):
            copy(k, r).wait_send()


def mlp_in(offs, resid, vec, w_g, w_u, parts, ring_x, ring_y, rounds, cid):
    share, width = resid.shape
    depth, ff = parts[0].shape
    cols = 2 * ff
    rr = share // rounds
    out = pl.pallas_call(
        functools.partial(mlp_in_kernel, rounds, offs),
        out_shape=jax.ShapeDtypeStruct((ring_y, share, ff), BF16),
        in_specs=[VMEM] * 2 + [ANY] * 6,
        out_specs=VMEM,
        scratch_shapes=[
            pltpu.VMEM((ring_y, share, depth), BF16),
            pltpu.VMEM((CORES, depth, cols), BF16),
            pltpu.VMEM((ring_y, rr, cols), F32),
            pltpu.VMEM((rounds, ring_y, rr, cols), BF16),
            pltpu.VMEM((rounds, ring_y, rr, cols), BF16),
            pltpu.VMEM((share // LANES, LANES), F32),
            pltpu.VMEM((ring_x * CORES, share // LANES, LANES), F32),
            DMA((rounds, 21)), DMA((rounds, 21)), DMA((ring_x * CORES,)), DMA((ring_x * CORES,)), DMA((CORES, 2, ring_x)),
        ],
        compiler_params=pltpu.CompilerParams(collective_id=cid, has_side_effects=True, vmem_limit_bytes=60 << 20),
        name='mlp_in',
    )(resid, vec, w_g, w_u, *parts)
    return out.reshape(ring_y * share, ff)


def front_kernel(rounds, offs, x_ref, vec_ref, w_x_ref, w_y_ref, w_ref, u_ref, y_ref, part_ref, nbuf, wbuf, pbuf, opp_buf, side, sums, all_sums, local_sem, ps, pr, xs, xr, ss, sr, ws, wr):
    tokens, width = x_ref.shape
    ring_x, _, _, wd, core, chip = where_am_i()
    wd_count = ring_x * CORES
    rr = tokens // rounds
    half = rr // 2
    mine = y_ref.shape[1]
    piece = CORES * mine
    partner = wd + 1 - 2 * core
    right, opp, left = (lax.rem(chip + step, ring_x) for step in (RIGHT, OPP, LEFT))
    first, second = 0, 1

    def span(r, part=None):
        return pl.ds(r * rr, rr) if part is None else pl.ds(r * rr + part * half, half)

    def weight(k, of):
        j, m = k // 2, k % 2
        src = (w_x_ref, w_y_ref)[m].at[:, pl.ds(pl.multiple_of((j * CORES + of) * mine, mine), mine)]
        return src, wbuf.at[aligned(core, width), pl.ds(j * piece + m * mine, mine)]

    def weight_out(k):
        src, dst = weight(k, 1 - core)
        return pltpu.make_async_remote_copy(src_ref=src, dst_ref=dst, send_sem=ps.at[rounds, k], recv_sem=pr.at[rounds, k], device_id={'wd': partner}, device_id_type=MESH)

    def weight_own(k):
        src, dst = weight(k, core)
        return pltpu.make_async_copy(src, dst, local_sem.at[k])

    def weight_in(k):
        ref = wbuf.at[aligned(1 - core, width), pl.ds((k // 2) * piece + (k % 2) * mine, mine)]
        pltpu.make_async_remote_copy(src_ref=ref, dst_ref=ref, send_sem=ps.at[rounds, k], recv_sem=pr.at[rounds, k], device_id={'wd': partner}, device_id_type=MESH).wait_recv()

    def normed(r, of):
        ref = nbuf.at[span(r), aligned(of, width)]
        return pltpu.make_async_remote_copy(src_ref=ref, dst_ref=ref, send_sem=ps.at[r, 0], recv_sem=pr.at[r, 0], device_id={'wd': partner}, device_id_type=MESH)

    def u_copy(r, of):
        ref = u_ref.at[span(r), aligned(of, mine)]
        return remote(ref, ref, ps.at[r, 1], pr.at[r, 1], {'wd': partner})

    def part_of(dest, r, part):
        return pbuf.at[span(r, part), aligned(dest, piece)]

    def x_send(k, r):
        rows = pl.ds(r * half, half)
        dest, part, dst, to = [
            (opp, first, opp_buf.at[0, rows], right), (opp, second, opp_buf.at[1, rows], left),
            (right, second, side.at[0, span(r, second)], right), (left, first, side.at[1, span(r, first)], left),
            (right, first, side.at[0, span(r, first)], right), (left, second, side.at[1, span(r, second)], left)][k]
        return remote(part_of(dest, r, part), dst, xs.at[r, k], xr.at[r, k], {'wd': to * CORES + core})

    def norm(r):
        for i in range(rr // LANES):
            tile = r * (rr // LANES) + i
            factor = as_column(scale[tile:tile + 1, :])[:, 0:1]
            rows = slice(tile * LANES, (tile + 1) * LANES)
            nbuf[rows, aligned(core, width)] = (x_ref[rows, :].astype(F32) * factor * gain).astype(BF16)
        normed(r, core).start()

    def dots(r):
        normed(r, 1 - core).wait_recv()
        step_rows = rr // 4

        def one(i, carry):
            rows = pl.ds(pl.multiple_of(r * rr + i * step_rows, step_rows), step_rows)
            pbuf[rows, :] = jnp.dot(nbuf[rows, :], wbuf[...], preferred_element_type=F32).astype(BF16)
            return carry
        lax.fori_loop(0, 4, one, 0)
        for k in range(4):
            x_send(k, r).start()

    def combine(r):
        rows = pl.ds(r * half, half)
        for k, dest, part, back in ((0, right, first, 4), (1, left, second, 5)):
            x_send(k, r).wait_recv()
            at = (span(r, part), aligned(dest, piece))
            pbuf[at] = (pbuf[at].astype(F32) + opp_buf[k, rows, :].astype(F32)).astype(BF16)
            x_send(back, r).start()

    def final(r):
        for k in range(2, 6):
            x_send(k, r).wait_recv()
        rows = span(r)
        total = pbuf[rows, aligned(chip, piece)].astype(F32) + side[0, rows, :].astype(F32) + side[1, rows, :].astype(F32)
        b_x, b_y = (vec_ref[:, pl.ds(pl.multiple_of(offs[name] + wd * mine, mine), mine)] for name in ('bias_x', 'bias_y'))
        u_ref[rows, aligned(core, mine)] = (total[:, :mine] + b_x).astype(BF16)
        u_copy(r, core).start()
        y_ref[rows, :] = jax.nn.gelu(total[:, mine:] + b_y, approximate=True).astype(BF16)

    ready = greet([{'wd': lax.rem(wd + step, wd_count)} for step in range(1, wd_count)])
    for k in range(2 * ring_x):
        weight_own(k).start()
    row_sums(x_ref, sums)
    all_sums[wd] = sums[...]
    ready()
    for one in sum_copies(sums, all_sums, ss, sr):
        one.start()
    for k in range(2 * ring_x):
        weight_out(k).start()
    moves = swaps(w_ref, part_ref, 0, ws, wr)
    for one in moves:
        one.start()
    for one in sum_copies(sums, all_sums, ss, sr):
        one.wait()
    scale = lax.rsqrt(jnp.sum(all_sums[...], axis=0) / (width * wd_count) + EPS)
    gain = 1.0 + vec_ref[:, offs['gain_temporal']:offs['gain_temporal'] + width]
    norm(0)
    for k in range(2 * ring_x):
        weight_own(k).wait()
        weight_in(k)
    for r in range(rounds):
        if r + 1 < rounds:
            norm(r + 1)
        dots(r)
        if r >= 1:
            combine(r - 1)
        if r >= 2:
            final(r - 2)
    combine(rounds - 1)
    final(rounds - 2)
    final(rounds - 1)
    for k in range(2 * ring_x):
        weight_out(k).wait_send()
    for r in range(rounds):
        normed(r, core).wait_send()
        u_copy(r, core).wait_send()
        u_copy(r, 1 - core).wait_recv()
        for k in range(6):
            x_send(k, r).wait_send()
    for one in moves:
        one.wait()


def front(offs, x, vec, w_x, w_y, weight, part, ring_x, rounds, cid):
    tokens, width = x.shape
    rnn = w_x.shape[1]
    mine = rnn // (ring_x * CORES)
    return pl.pallas_call(
        functools.partial(front_kernel, rounds, offs),
        out_shape=(jax.ShapeDtypeStruct((tokens, CORES * mine), BF16), jax.ShapeDtypeStruct((tokens, mine), BF16), part),
        in_specs=[VMEM, VMEM, ANY, ANY, ANY],
        out_specs=(VMEM, VMEM, ANY),
        scratch_shapes=[
            pltpu.VMEM((tokens, CORES * width), BF16),
            pltpu.VMEM((CORES * width, rnn), BF16),
            pltpu.VMEM((tokens, rnn), BF16),
            pltpu.VMEM((2, tokens // 2, CORES * mine), BF16),
            pltpu.VMEM((2, tokens, CORES * mine), BF16),
            pltpu.VMEM((tokens // LANES, LANES), F32),
            pltpu.VMEM((ring_x * CORES, tokens // LANES, LANES), F32),
            DMA((2 * ring_x,)), DMA((rounds + 1, 2 * ring_x)), DMA((rounds + 1, 2 * ring_x)), DMA((rounds, 6)), DMA((rounds, 6)),
            DMA((ring_x * CORES,)), DMA((ring_x * CORES,)), DMA((ring_x,)), DMA((ring_x,)),
        ],
        compiler_params=pltpu.CompilerParams(collective_id=cid, has_side_effects=True, vmem_limit_bytes=56 << 20),
        name='front',
    )(x, vec, w_x, w_y, weight)


def solution(mesh):
    wd_count = mesh.shape['wd']
    ch_count = mesh.shape['ch']
    chips = wd_count // CORES
    row_spec = P('dp', 'wd')
    specs = (row_spec, P('dp', None), P('wd'), P('wd', 'ch'), P('ch'), P('wd', 'ch'), P('ch'), P(None, 'ch'), P('ch'), P('ch'), P('ch', None, None), P('ch'), P('ch', None, None), P('ch'), P('ch', 'wd'), P('wd'), P('wd'), P('wd', 'ch'), P('ch'), P('wd', 'ch'), P('ch'), P('ch', 'wd'), P('wd'))

    def local_layer(resid_in, seg_pos, gain_temporal, w_x, bias_x, w_y, bias_y, conv_w, conv_bias, lam_param, rgate_w, rgate_b, igate_w, igate_b, w_o, bias_o, gain_mlp, w_g, bias_g, w_u, bias_u, w_d, bias_d):
        small = {'gain_temporal': gain_temporal, 'bias_x': bias_x, 'bias_y': bias_y, 'conv_w': conv_w, 'conv_bias': conv_bias, 'lam_param': lam_param, 'rgate_b': rgate_b,
                 'igate_b': igate_b, 'bias_o': bias_o, 'gain_mlp': gain_mlp, 'bias_g': bias_g, 'bias_u': bias_u, 'bias_d': bias_d}
        offs = {'rnn': w_x.shape[1], 'taps': conv_w.shape[0]}
        end = 0
        for name, val in sorted(small.items(), key=lambda item: -item[1].size):
            offs[name] = end
            end += val.size
        order = sorted(small, key=lambda name: offs[name])
        vec = jnp.concatenate([small[name].astype(F32).reshape(-1) for name in order]).reshape(1, end)
        tokens = resid_in.shape[0]
        part = jax.ShapeDtypeStruct((chips * w_g.shape[0], w_g.shape[1] // wd_count), BF16)
        u_pair, y_own, g0 = front(offs, resid_in, vec, w_x, w_y, w_g, part, chips, 4, 1)
        mixed, u0 = lru(offs, u_pair, y_own, seg_pos.reshape(1, tokens), vec, rgate_w, igate_w, w_u, part, chips, 2)
        resid, g1, u1 = ring_layer(mixed, w_o, resid_in, vec, offs['bias_o'], (w_g, w_u), part, chips, ch_count, 4, 3)
        inner = mlp_in(offs, resid, vec, w_g, w_u, (g0, u0, g1, u1), chips, ch_count, 4, 4)
        return ring_layer(inner, w_d, resid, vec, offs['bias_d'], (), part, chips, ch_count, 8, 5)

    return jax.shard_map(local_layer, mesh=mesh, in_specs=specs, out_specs=row_spec, check_vma=False)
```

time: 2390 us -> 470 us (0.20)
  waiting for transfers between devices: 1020 us -> 0 us
  local copies, waits for them, and re-layouts: 859 us -> 10 us
  Pallas kernels: 0 us -> 451 us
  other arithmetic: 276 us -> 8.24 us
  matrix products: 122 us -> 0 us
  starting transfers between devices: 40 us -> 0 us
  blocking collectives: 37.4 us -> 0 us
    all_to_all x6 -> x0, waiting for transfers between devices: 812 us -> none  [token_sum(): received = lax.all_to_all(pieces, axis_name, 0, 0)]
    slice x78 -> x0, local copies, waits for them, and re-layouts: 530 us -> none  [the longest x74 496 us: rg_lru(): lax.associative_scan(combine, (decay.reshape(seqs, steps, width), drive.r...]
    pallas_call x0 -> x5, Pallas kernels: none -> 451 us  [the longest x2 217 us: ring_layer(): pl.pallas_call(functools.partial(ring_kernel, rounds, regather, bias_at),...]
    pad x22 -> x0, local copies, waits for them, and re-layouts: 261 us -> none  [rg_lru(): lax.associative_scan(combine, (decay.reshape(seqs, steps, width), drive.r...]
    all_gather x5 -> x0, waiting for transfers between devices: 205 us -> none  [the longest x1 118 us: local_layer(): inner = lax.all_gather(inner_rows, 'wd', axis=0, tiled=True)]
    dot_general x8 -> x0, matrix products: 122 us -> none  [the longest x1 20.7 us: local_layer(): jnp.dot(normed2, w_g, preferred_element_type=jnp.float32)]
    add x24 -> x0, other arithmetic: 63.8 us -> none  [the longest x11 32.2 us: combine(): return (left[0] * right[0], right[0] * left[1] + right[1])]
    reduce_sum x8 -> x0, other arithmetic: 57.3 us -> none  [the longest x6 50.9 us: token_sum(): return jnp.sum(received.astype(jnp.float32), axis=0)]
  transfers between devices with their start and end apart: 11 -> 0, of which waited for: 9 -> 0; matrix products, arithmetic and copies ran while one was open for 48% -> 0% of each run, Pallas kernels for 0% -> 0%
where the time goes in v5:
time: 470 us
  Pallas kernels  451 us (96%)
  local copies, waits for them, and re-layouts  10 us (2%)
  other arithmetic  8.24 us (2%)
    pallas_call x2, Pallas kernels, ring_layer(): pl.pallas_call(functools.partial(ring_kernel, rounds, regather, bias_at),...  217 us
    pallas_call x1, Pallas kernels, mlp_in(): pl.pallas_call(functools.partial(mlp_in_kernel, rounds, offs), out_shape=...  112 us
    pallas_call x1, Pallas kernels, front(): pl.pallas_call(functools.partial(front_kernel, rounds, offs), out_shape=(...  99.4 us
    pallas_call x1, Pallas kernels, lru(): pl.pallas_call(functools.partial(lru_kernel, offs), out_shape=(jax.ShapeD...  22.1 us
    unnamed x19, local copies, waits for them, and re-layouts  10 us

profile of v5, /device:TPU:97, one launch (start us, length us, event | category | flops | bytes accessed | tf_op | source)
XLA Modules:
  0.0 469.7 jit_solution(3953785588110005351)
XLA Ops:
  0.0 0.7 convert_bitcast_fusion
  0.7 0.7 convert_dynamic-update-slice_fusion.1
  1.4 0.7 convert_dynamic-update-slice_fusion
  2.1 0.7 constant_dynamic-update-slice_fusion.9
  2.8 0.7 constant_dynamic-update-slice_fusion.8
  3.5 0.7 constant_dynamic-update-slice_fusion.7
  4.1 0.7 constant_dynamic-update-slice_fusion.6
  4.8 0.7 constant_dynamic-update-slice_fusion.5
  5.5 0.7 constant_dynamic-update-slice_fusion.4
  6.2 0.7 constant_dynamic-update-slice_fusion.3
  6.9 0.7 constant_dynamic-update-slice_fusion.2
  7.6 0.7 constant_dynamic-update-slice_fusion.1
  8.3 0.7 constant_dynamic-update-slice_fusion
  8.9 0.0 copy-start
  8.9 0.6 copy-done
  9.6 0.0 copy-start.5
  9.6 0.0 copy-start.6
  9.6 0.0 copy-start.7
  9.6 99.4 %front.1 = (bf16[4096,256]{1,0:T(8,128)(2,1)}, bf16[4096,128]{1,0:T(8,128)(2,1)}, bf16[2048,384]{1,0:T(8,128)(2,1)}) custom-call(bf16[4096,512]{1,0:T(8,128)(2,1)} %resid_ref.1, f32[1,18432]{1,0:T(1,128)} %bitcast.7, bf16[512,1024]{1,0:T(8,128)(2,1)} %w_x_ref.1, bf16[512,1024]{1,0:T(8,128)(2,1)} %w_y_ref.1, bf16[512,3072]{1,0:T(8,128)(2,1)} %wg_ref.1), custom_call_target="tpu_custom_call" | custom-call | tf_op jit(solution)/shard_map/front/pallas_call | solution.py:676
  109.0 0.0 copy-done.5
  109.0 0.0 copy-done.6
  109.0 0.0 copy-done.7
  109.0 0.0 copy-start.1
  109.0 0.9 copy-done.1
  109.9 0.0 copy-start.3
  109.9 1.2 copy-done.3
  111.1 22.1 %lru.1 = (bf16[4096,128]{1,0:T(8,128)(2,1)S(1)}, bf16[2048,384]{1,0:T(8,128)(2,1)S(1)}) custom-call(bf16[4096,256]{1,0:T(8,128)(2,1)} %get-tuple-element.13.u_ref, bf16[4096,128]{1,0:T(8,128)(2,1)S(1)} %copy-done.3, s32[1,4096]{1,0:T(1,128)S(1)} %copy-done.7, f32[1,18432]{1,0:T(1,128)S(1)} %bitcast.11, bf16[4,256,256]{2,1,0:T(8,128)(2,1)S(1)} %copy-done.5, ...), custom_call_target="tpu_custom_call" | custom-call | tf_op jit(solution)/shard_map/lru/pallas_call | solution.py:165
  133.2 0.0 copy-start.2
  133.3 1.1 copy-done.2
  134.4 0.0 copy-start.4
  134.4 1.0 copy-done.4
  135.4 77.9 %ring_layer.2 = (f32[1024,512]{1,0:T(8,128)}, bf16[2048,384]{1,0:T(8,128)(2,1)}, bf16[2048,384]{1,0:T(8,128)(2,1)}) custom-call(bf16[4,1024,128]{2,1,0:T(8,128)(2,1)} %bitcast.12, bf16[1024,512]{1,0:T(8,128)(2,1)} %w_ref.6, bf16[4096,512]{1,0:T(8,128)(2,1)} %resid_ref.1, f32[1,18432]{1,0:T(1,128)} %bitcast.8, bf16[512,3072]{1,0:T(8,128)(2,1)} %wg_ref.1, ...), custom_call_target="tpu_custom_call" | custom-call | tf_op jit(solution)/shard_map/ring_layer/pallas_call | solution.py:350
  213.3 112.4 %mlp_in.1.h_ref = bf16[4,1024,384]{2,1,0:T(8,128)(2,1)} custom-call(f32[1024,512]{1,0:T(8,128)} %get-tuple-element.16.resid_ref, f32[1,18432]{1,0:T(1,128)} %bitcast.9, bf16[512,3072]{1,0:T(8,128)(2,1)} %wg_ref.1, bf16[512,3072]{1,0:T(8,128)(2,1)} %wu_ref.1, bf16[2048,384]{1,0:T(8,128)(2,1)} %get-tuple-element.17.g0_ref, bf16[2048,384]{1,0:T(8,128)(2,1)} %copy-done.2, ...), custom_call_target="tpu_custom_call" | custom-call | tf_op jit(solution)/shard_map/mlp_in/pallas_call | solution.py:518
  325.7 139.5 %ring_layer.3 = bf16[4,1024,512]{2,1,0:T(8,128)(2,1)} custom-call(bf16[4,1024,384]{2,1,0:T(8,128)(2,1)} %mlp_in.1.h_ref, bf16[3072,512]{1,0:T(8,128)(2,1)} %w_ref.7, f32[1024,512]{1,0:T(8,128)} %get-tuple-element.16.resid_ref, f32[1,18432]{1,0:T(1,128)} %bitcast.10), custom_call_target="tpu_custom_call" | custom-call | tf_op jit(solution)/shard_map/ring_layer/pallas_call | solution.py:350
  465.2 4.5 copy.39
  (1 shorter events, 0.0 us)
Async XLA Ops:
  8.9 0.6 copy-start
  9.6 99.4 %copy-start.5 = (bf16[4,256,256]{2,1,0:T(8,128)(2,1)S(1)}, bf16[4,256,256]{2,1,0:T(8,128)(2,1)}, u32[]{:S(2)}) copy-start(bf16[4,256,256]{2,1,0:T(8,128)(2,1)} %rg_ref.1) | copy-start | bytes 1572868
  9.6 99.4 %copy-start.6 = (bf16[4,256,256]{2,1,0:T(8,128)(2,1)S(1)}, bf16[4,256,256]{2,1,0:T(8,128)(2,1)}, u32[]{:S(2)}) copy-start(bf16[4,256,256]{2,1,0:T(8,128)(2,1)} %ig_ref.1) | copy-start | bytes 1572868
  9.6 99.4 %copy-start.7 = (s32[1,4096]{1,0:T(1,128)S(1)}, s32[1,4096]{1,0:T(1,128)}, u32[]{:S(2)}) copy-start(s32[1,4096]{1,0:T(1,128)} %pos_ref.1) | copy-start | bytes 49156
  109.0 0.9 copy-start.1
  109.9 1.2 copy-start.3
  133.2 1.1 copy-start.2
  134.4 1.0 copy-start.4

commit v6 on v5

v6 whole, which is shorter than its diff:
```python
import functools

import jax
import jax.numpy as jnp
from jax import lax
from jax.experimental import pallas as pl
from jax.experimental.pallas import tpu as pltpu
from jax.sharding import PartitionSpec as P

EPS = 1e-6
CORES = 2
SEGS = 8
PAD = 8
LANES = 128
RIGHT, OPP, LEFT = 1, 2, 3
MESH = pl.DeviceIdType.MESH
F32 = jnp.float32
BF16 = jnp.bfloat16
VMEM = pl.BlockSpec(memory_space=pltpu.VMEM)
ANY = pl.BlockSpec(memory_space=pl.ANY)
DMA = pltpu.SemaphoreType.DMA
GRANT = 67043328


def neg_expm1(z):
    series = -z * (1.0 + z * (0.5 + z * (1.0 / 6.0 + z * (1.0 / 24.0))))
    return jnp.where(z > -0.03, series, 1.0 - jnp.exp(z))


def where_am_i():
    ring_x = lax.axis_size('wd') // CORES
    wd = lax.axis_index('wd')
    return ring_x, lax.axis_size('ch'), lax.axis_index('ch'), wd, lax.rem(wd, CORES), wd // CORES


def aligned(index, size):
    return pl.ds(pl.multiple_of(index * size, size), size)


def remote(src, dst, send, recv, device):
    return pltpu.make_async_remote_copy(src_ref=src, dst_ref=dst, send_sem=send, recv_sem=recv, device_id=device, device_id_type=MESH)


def greet(devices):
    barrier = pltpu.get_barrier_semaphore()
    for device in devices:
        pl.semaphore_signal(barrier, inc=1, device_id=device, device_id_type=MESH)
    return functools.partial(pl.semaphore_wait, barrier, len(devices))


def swaps(src, dst, k, sends, recvs):
    ring_x, _, _, _, core, chip = where_am_i()
    depth, ff = src.shape[0], dst.shape[1]
    return [remote(src.at[:, aligned(lax.rem(chip + step, ring_x) * CORES + k, ff)], dst.at[aligned(chip, depth), :],
                   sends.at[step], recvs.at[step], {'wd': lax.rem(chip + step, ring_x) * CORES + core}) for step in range(1, ring_x)]


def row_sums(x_ref, sums):
    for i in range(x_ref.shape[0] // LANES):
        sq = jnp.zeros((LANES, LANES), F32)
        for j in range(x_ref.shape[1] // LANES):
            val = x_ref[i * LANES:(i + 1) * LANES, j * LANES:(j + 1) * LANES].astype(F32)
            sq = sq + val * val
        sums[i:i + 1, :] = jnp.sum(sq.T, axis=0, keepdims=True)


def sum_copies(sums, all_sums, ss, sr):
    ring_x, _, _, wd, _, _ = where_am_i()
    count = ring_x * CORES
    return [remote(sums, all_sums.at[wd], ss.at[step], sr.at[step], {'wd': lax.rem(wd + step, count)}) for step in range(1, count)]


def as_column(row):
    return jnp.broadcast_to(row, (LANES, LANES)).T


def ring_body(rounds, bias_at, h_ref, w_ref, resid, vec_ref, out_ref, obuf, hbuf, pbuf, side, opp_buf, xs, xr, ys, yr, own_sem, ready, loads, after):
    share, depth = h_ref.shape[1:]
    cols_out = w_ref.shape[1]
    rr = share // rounds
    ring_x, ring_y, ch, wd, core, chip = where_am_i()
    regather = obuf is not None
    other = 1 - 2 * core
    partner = wd + other
    x_at = [lax.rem(chip + step, ring_x) * CORES + core for step in range(ring_x)]
    y_at = [lax.rem(ch + step, ring_y) for step in range(ring_y)]
    first, second, whole = 0, 1, None
    steps = (RIGHT, LEFT, OPP)

    def span(r, part=None):
        return aligned(r, rr) if part is None else aligned(2 * r + part, rr // 2)

    def cols(owner, r, part=None):
        return hbuf.at[:, span(r, part), aligned(owner, depth)]

    x_plan = [(wd, whole, x_at[RIGHT], x_at[LEFT]), (wd, whole, x_at[LEFT], x_at[RIGHT]),
              (x_at[LEFT], first, x_at[RIGHT], x_at[OPP]), (x_at[RIGHT], second, x_at[LEFT], x_at[OPP]),
              (wd, whole, partner, partner), (x_at[LEFT], whole, partner, x_at[LEFT] + other), (x_at[RIGHT], whole, partner, x_at[RIGHT] + other),
              (x_at[OPP], first, partner, x_at[OPP] + other), (x_at[OPP], second, partner, x_at[OPP] + other)]
    own_both, own_side, relay_both, side_both, opp_both, core_in = (0, 1), (4,), (2, 3), (5, 6), (7, 8), (4, 5, 6, 7, 8)

    def x_copy(k, r):
        owner, part, to, _ = x_plan[k]
        dst = cols(owner, r, part)
        src = h_ref.at[:, span(r), :] if k in own_both + own_side else dst
        return remote(src, dst, xs.at[r, k], xr.at[r, k], {'wd': to})

    def x_start(r, *ks):
        for k in ks:
            x_copy(k, r).start()

    def x_wait(r, *ks):
        for k in ks:
            ref = cols(x_plan[k][-1], r, x_plan[k][1])
            remote(ref, ref, xs.at[r, k], xr.at[r, k], {'wd': partner}).wait_recv()

    def sum_copy(step, r):
        return remote(pbuf.at[y_at[step], span(r), :], side.at[step - 1, span(r), :], ys.at[r, step], yr.at[r, step], {'ch': y_at[step]})

    def out_copy(step, r, owner):
        return remote(obuf.at[span(r), :], out_ref.at[y_at[owner], span(r), :], ys.at[r, ring_y + step], yr.at[r, ring_y + step], {'ch': y_at[step]})

    def keep_copy(r):
        return pltpu.make_async_copy(obuf.at[span(r), :], out_ref.at[ch, span(r), :], ys.at[r, 0])

    to_opp, to_side, relayed = (0, 1), (2, 3), (4, 5)

    def y_copy(k, r):
        piece, part, dst, to = [
            (OPP, first, opp_buf.at[0, span(r, first)], RIGHT), (OPP, second, opp_buf.at[1, span(r, second)], LEFT),
            (RIGHT, second, side.at[0, span(r, second)], RIGHT), (LEFT, first, side.at[1, span(r, first)], LEFT),
            (RIGHT, first, side.at[0, span(r, first)], RIGHT), (LEFT, second, side.at[1, span(r, second)], LEFT)][k]
        return remote(pbuf.at[y_at[piece], span(r, part)], dst, ys.at[r, k], yr.at[r, k], {'ch': y_at[to]})

    def known(r, bound):
        return not isinstance(r, int) or r < bound

    def own(r):
        if known(r, rounds):
            x_start(r, *own_both, *own_side)

    def stage1(r):
        if known(r, rounds):
            for side_in, on in zip(own_both, relay_both):
                x_wait(r, side_in)
                x_start(r, on)
            x_start(r, *side_both)
            own(r + 2)
            if isinstance(r, int) and r == rounds - 1:
                after()

    def stage2(r):
        for side_in, on in zip(relay_both, opp_both):
            x_wait(r, side_in)
            x_start(r, on)

    def dots(r):
        x_wait(r, *core_in)
        each = max(1, 256 // rr)

        def one(i, carry):
            at = pl.ds(i * each, each)
            block = hbuf[at, span(r), :].reshape(each * rr, hbuf.shape[2])
            part = jnp.dot(block, w_ref[...], preferred_element_type=F32)
            pbuf[at, span(r), :] = part.astype(BF16).reshape(each, rr, cols_out)
            return carry
        lax.fori_loop(0, ring_y // each, one, 0)
        if regather:
            for step in steps:
                sum_copy(step, r).start()
        else:
            for k in to_opp + to_side:
                y_copy(k, r).start()

    def combine(r):
        for k, piece, part in zip(to_opp, (RIGHT, LEFT), (first, second)):
            y_copy(k, r).wait_recv()
            at = y_at[piece], span(r, part)
            pbuf[at] = (pbuf[at].astype(F32) + opp_buf[k, span(r, part), :].astype(F32)).astype(BF16)
            y_copy(relayed[k], r).start()

    def final(r):
        rows = span(r)
        if regather:
            for step in steps:
                sum_copy(step, r).wait_recv()
        else:
            for k in to_side + relayed:
                y_copy(k, r).wait_recv()
        total = pbuf[ch, rows, :].astype(F32)
        for slot in range(side.shape[0]):
            total = total + side[slot, rows, :].astype(F32)
        total = resid[rows, :].astype(F32) + total + vec_ref[:, bias_at:bias_at + cols_out]
        if regather:
            obuf[rows, :] = total.astype(obuf.dtype)
            for step in steps:
                out_copy(step, r, 0).start()
            keep_copy(r).start()
        else:
            out_ref[rows, :] = total

    def turn(r):
        stage1(r + 1)
        stage2(r)
        later = not isinstance(r, int) or r >= 1
        if later and not regather:
            combine(r - 1)
        dots(r)
        if later:
            final(r - 1)

    mine = pltpu.make_async_copy(h_ref, hbuf.at[:, :, aligned(wd, depth)], own_sem)
    mine.start()
    ready()
    own(0)
    own(1)
    mine.wait()
    for one in loads:
        one.wait()
    stage1(0)
    turn(0)

    def middle(r, carry):
        turn(r)
        return carry
    lax.fori_loop(1, rounds - 3, middle, 0)
    for r in range(max(1, rounds - 3), rounds):
        turn(r)
    if not regather:
        combine(rounds - 1)
    final(rounds - 1)

    def finish():
        def drain(r, carry):
            for k in range(len(x_plan)):
                x_copy(k, r).wait_send()
            if regather:
                for step in steps:
                    sum_copy(step, r).wait_send()
                    out_copy(step, r, ring_y - step).wait_recv()
                    out_copy(step, r, 0).wait_send()
                keep_copy(r).wait()
            else:
                for k in to_opp + to_side + relayed:
                    y_copy(k, r).wait_send()
            return carry
        lax.fori_loop(0, rounds, drain, 0)
    return finish


def ring_peers():
    ring_x, ring_y, ch, wd, core, chip = where_am_i()
    return [{'wd': wd + 1 - 2 * core}] + [{'wd': lax.rem(chip + step, ring_x) * CORES + core} for step in (RIGHT, LEFT)] + [{'ch': lax.rem(ch + step, ring_y)} for step in range(1, ring_y)]


def mlp_out_kernel(rounds, bias_at, h_ref, w_in_ref, resid_ref, vec_ref, out_ref, w_ref, resid, obuf, hbuf, pbuf, side, xs, xr, ys, yr, local_sem):
    ready = greet(ring_peers())
    loads = [pltpu.make_async_copy(w_in_ref, w_ref, local_sem.at[1]), pltpu.make_async_copy(resid_ref, resid, local_sem.at[2])]
    for one in loads:
        one.start()
    ring_body(rounds, bias_at, h_ref, w_ref, resid, vec_ref, out_ref, obuf, hbuf, pbuf, side, None, xs, xr, ys, yr, local_sem.at[0], ready, loads, lambda: None)()


def ring_scratch(ring_y, share, wide, cols, rounds, regather):
    return [pltpu.VMEM((ring_y, share, wide), BF16), pltpu.VMEM((ring_y, share, cols), BF16),
            pltpu.VMEM((ring_y - 1 if regather else 2, share, cols), BF16)]


def ring_sems(rounds, ring_y):
    return [DMA((rounds, 9)), DMA((rounds, 9)), DMA((rounds, 2 * ring_y)), DMA((rounds, 2 * ring_y))]


def mlp_out(h, w, resid, vec, bias_at, ring_y, rounds, cid):
    share, cols = resid.shape
    return pl.pallas_call(
        functools.partial(mlp_out_kernel, rounds, bias_at),
        out_shape=jax.ShapeDtypeStruct((ring_y, share, cols), BF16),
        in_specs=[ANY, ANY, ANY, VMEM],
        out_specs=ANY,
        scratch_shapes=[pltpu.VMEM(w.shape, BF16), pltpu.VMEM(resid.shape, F32), pltpu.VMEM(resid.shape, BF16)]
        + ring_scratch(ring_y, share, w.shape[0], cols, rounds, True) + ring_sems(rounds, ring_y) + [DMA((3,))],
        compiler_params=pltpu.CompilerParams(collective_id=cid, has_side_effects=True, vmem_limit_bytes=GRANT),
        name='mlp_out',
    )(h, w, resid, vec).reshape(ring_y * share, cols)


def mid_kernel(rounds, offs, h_ref, w_o_ref, x_ref, vec_ref, wg_ref, wu_ref, g0_ref, u0_ref, inner_ref, resid_out, resid_ref, x_rows, hbuf, pbuf, side, opp_buf, out_ref, nbuf, w_ref, keep, send, got, sums, all_sums,
               xs, xr, ys, yr, ns, nr, ss, sr, load_sem, local_sem, ws, wr, io_sem):
    share, width = resid_ref.shape
    ring_x, ring_y, ch, wd, core, chip = where_am_i()
    wd_count = ring_x * CORES
    rr = share // rounds
    half = rr // 2
    partner = wd + 1 - 2 * core
    ff = out_ref.shape[2]

    def device(d1, d2):
        return {'ch': lax.rem(ch + d1 * (1 - core) + d2 * core, ring_y), 'wd': lax.rem(chip + d1 * core + d2 * (1 - core), ring_x) * CORES + core}

    def block(d1, d2, r, part=None):
        rows = pl.ds(r * rr, rr) if part is None else pl.ds(r * rr + part * half, half)
        at = lax.rem(chip + d1 * core + d2 * (1 - core), ring_x)
        return nbuf.at[lax.rem(ch + d1 * (1 - core) + d2 * core, ring_y), rows, aligned(at, width)]

    whole = None
    plan = [((0, 0), (RIGHT, 0), (LEFT, 0), whole), ((0, 0), (LEFT, 0), (RIGHT, 0), whole),
            ((LEFT, 0), (RIGHT, 0), (OPP, 0), 0), ((RIGHT, 0), (LEFT, 0), (OPP, 0), 1)]
    for d1 in (0, LEFT, RIGHT, OPP):
        plan += [((d1, 0), (0, RIGHT), (d1, LEFT), whole), ((d1, 0), (0, LEFT), (d1, RIGHT), whole),
                 ((d1, LEFT), (0, RIGHT), (d1, OPP), 0), ((d1, RIGHT), (0, LEFT), (d1, OPP), 1)]
    core_step = len(plan)

    def copy(k, r):
        src, to, _, part = plan[k]
        ref = block(*src, r, part)
        return remote(ref, ref, ns.at[r, k], nr.at[r, k], device(*to))

    def start(r, *ks):
        for k in ks:
            copy(k, r).start()

    def wait(r, *ks):
        for k in ks:
            ref = block(*plan[k][2], r, plan[k][3])
            remote(ref, ref, ns.at[r, k], nr.at[r, k], device(RIGHT, 0)).wait_recv()

    def own(r):
        if r < rounds:
            start(r, 0, 1, 4, 5)

    def stage1(r):
        if r < rounds:
            wait(r, 0, 1)
            start(r, 2, 3, 8, 9, 12, 13)
            wait(r, 4, 5)
            start(r, 6, 7)

    def stage2(r):
        if r < rounds:
            wait(r, 2, 3)
            start(r, 16, 17)
            wait(r, 8, 9)
            start(r, 10, 11)
            wait(r, 12, 13)
            start(r, 14, 15)

    def stage3(r):
        if r < rounds:
            wait(r, 16, 17)
            start(r, 18, 19)

    def halves(r):
        return remote(send.at[r], got.at[r], ns.at[r, core_step], nr.at[r, core_step], {'wd': partner})

    each = max(1, 256 // rr)

    def dots(r, mine):
        def one(i, carry):
            at = pl.ds(i * each, each)
            rows = nbuf[at, pl.ds(r * rr, rr), :].reshape(each * rr, nbuf.shape[2])
            if mine:
                keep[at] = jnp.dot(rows, w_ref[core], preferred_element_type=F32).reshape(each, rr, 2 * ff)
            else:
                send[r, at] = jnp.dot(rows, w_ref[1 - core], preferred_element_type=F32).astype(BF16).reshape(each, rr, 2 * ff)
            return carry
        lax.fori_loop(0, ring_y // each, one, 0)

    def inner_copy(r):
        at = pl.ds(r * rr, rr)
        return pltpu.make_async_copy(out_ref.at[:, at, :], inner_ref.at[:, at, :], io_sem.at[r])

    def finish(r):
        halves(r).wait_recv()
        b_g, b_u = (vec_ref[:, pl.ds(pl.multiple_of(offs[name] + wd * ff, LANES), ff)] for name in ('bias_g', 'bias_u'))

        def one(q, carry):
            total = keep[q] + got[r, q].astype(F32)
            out_ref[q, pl.ds(r * rr, rr), :] = (jax.nn.gelu(total[:, :ff] + b_g, approximate=True) * (total[:, ff:] + b_u)).astype(BF16)
            return carry
        lax.fori_loop(0, ring_y, one, 0)
        inner_copy(r).start()

    ready = greet([{'wd': lax.rem(wd + step, wd_count)} for step in range(1, wd_count)] + [{'ch': lax.rem(ch + step, ring_y)} for step in range(1, ring_y)])
    loads = []
    for m, (full, part) in enumerate(((wg_ref, g0_ref), (wu_ref, u0_ref))):
        for k in range(CORES):
            for step in range(1 if k else ring_x):
                rows = aligned(lax.rem(chip + step, ring_x), width)
                src = part.at[rows, :] if step else full.at[:, aligned(chip * CORES + k, ff)]
                loads.append(pltpu.make_async_copy(src, w_ref.at[k, rows, pl.ds(m * ff, ff)], load_sem.at[k, m, step]))
    moves = [one for m, full in enumerate((wg_ref, wu_ref)) for one in swaps(full, w_ref.at[1, :, pl.ds(m * ff, ff)], 1, ws.at[m], wr.at[m])]
    first_load = pltpu.make_async_copy(x_ref.at[aligned(ch, share), :], x_rows, local_sem.at[1])
    first_load.start()

    def after():
        for one in moves + loads:
            one.start()

    ring_done = ring_body(rounds, offs['bias_o'], h_ref, w_o_ref, x_rows, vec_ref, resid_ref, None, hbuf, pbuf, side, opp_buf, xs, xr, ys, yr, local_sem.at[0], ready, [first_load], after)
    keep_resid = pltpu.make_async_copy(resid_ref, resid_out, local_sem.at[2])
    keep_resid.start()
    row_sums(resid_ref, sums)
    all_sums[wd] = sums[...]
    for one in sum_copies(sums, all_sums, ss, sr):
        one.start()
    for one in sum_copies(sums, all_sums, ss, sr):
        one.wait()
    scale = lax.rsqrt(jnp.sum(all_sums[...], axis=0) / (width * wd_count) + EPS)
    gain = 1.0 + vec_ref[:, offs['gain_mlp']:offs['gain_mlp'] + width]

    def norm(r):
        for i in range(r * rr // LANES, (r + 1) * rr // LANES):
            factor = as_column(scale[i:i + 1, :])[:, 0:1]
            rows = slice(i * LANES, (i + 1) * LANES)
            nbuf[ch, rows, aligned(chip, width)] = (resid_ref[rows, :] * factor * gain).astype(BF16)

    for r in range(rounds):
        norm(r)
        if r < 3:
            own(r)
    stage1(0)
    stage2(0)
    stage1(1)
    stage3(0)
    stage2(1)
    for one in loads + moves:
        one.wait()
    for r in range(rounds):
        wait(r, 6, 7, 10, 11, 14, 15, 18, 19)
        dots(r, False)
        halves(r).start()
        own(r + 3)
        stage1(r + 2)
        stage3(r + 1)
        dots(r, True)
        stage2(r + 2)
        finish(r)
    for r in range(rounds):
        inner_copy(r).wait()
        halves(r).wait_send()
        for k in range(core_step):
            copy(k, r).wait_send()
    keep_resid.wait()
    ring_done()


def mid(offs, h, w_o, x, vec, w_g, w_u, parts, ring_x, ring_y, rounds, cid):
    tokens, width = x.shape
    share = tokens // ring_y
    depth, ff = parts[0].shape
    cols = 2 * ff
    rr = share // rounds
    return pl.pallas_call(
        functools.partial(mid_kernel, rounds, offs),
        out_shape=(jax.ShapeDtypeStruct((ring_y, share, ff), BF16), jax.ShapeDtypeStruct((share, width), F32)),
        in_specs=[ANY, VMEM, ANY, VMEM] + [ANY] * 4,
        out_specs=(ANY, ANY),
        scratch_shapes=[pltpu.VMEM((share, width), F32), pltpu.VMEM((share, width), BF16)] + ring_scratch(ring_y, share, w_o.shape[0], width, rounds, False) + [
            pltpu.VMEM((2, share, width), BF16),
            pltpu.VMEM((ring_y, share, ff), BF16),
            pltpu.VMEM((ring_y, share, depth), BF16),
            pltpu.VMEM((CORES, depth, cols), BF16),
            pltpu.VMEM((ring_y, rr, cols), F32),
            pltpu.VMEM((rounds, ring_y, rr, cols), BF16),
            pltpu.VMEM((rounds, ring_y, rr, cols), BF16),
            pltpu.VMEM((share // LANES, LANES), F32),
            pltpu.VMEM((ring_x * CORES, share // LANES, LANES), F32),
        ] + ring_sems(rounds, ring_y) + [
            DMA((rounds, 21)), DMA((rounds, 21)), DMA((ring_x * CORES,)), DMA((ring_x * CORES,)),
            DMA((CORES, 2, ring_x)), DMA((3,)), DMA((2, ring_x)), DMA((2, ring_x)), DMA((rounds,)),
        ],
        compiler_params=pltpu.CompilerParams(collective_id=cid, has_side_effects=True, vmem_limit_bytes=GRANT),
        name='mid',
    )(h.reshape(ring_y, share, h.shape[1]), w_o, x, vec, w_g, w_u, *parts)


def front_kernel(rounds, offs, x_ref, vec_ref, pos_ref, rg_ref, ig_ref, w_x_ref, w_y_ref, wg_ref, wu_ref, out_ref, part_g, part_u, nbuf, wbuf, pbuf, opp_buf, side, u_ref, y_ref, u32, a_s, b_s, gate_w, sums, all_sums, local_sem, ps, pr, xs, xr, ss, sr, ws, wr):
    tokens, width = x_ref.shape
    ring_x, _, _, wd, core, chip = where_am_i()
    wd_count = ring_x * CORES
    rr = tokens // rounds
    half = rr // 2
    mine = y_ref.shape[1]
    piece = CORES * mine
    partner = wd + 1 - 2 * core
    right, opp, left = (lax.rem(chip + step, ring_x) for step in (RIGHT, OPP, LEFT))
    first, second = 0, 1

    def span(r, part=None):
        return pl.ds(r * rr, rr) if part is None else pl.ds(r * rr + part * half, half)

    def weight(k, of):
        j, m = k // 2, k % 2
        src = (w_x_ref, w_y_ref)[m].at[:, pl.ds(pl.multiple_of((j * CORES + of) * mine, mine), mine)]
        return src, wbuf.at[aligned(core, width), pl.ds(j * piece + m * mine, mine)]

    def weight_out(k):
        src, dst = weight(k, 1 - core)
        return pltpu.make_async_remote_copy(src_ref=src, dst_ref=dst, send_sem=ps.at[rounds, k], recv_sem=pr.at[rounds, k], device_id={'wd': partner}, device_id_type=MESH)

    def weight_own(k):
        src, dst = weight(k, core)
        return pltpu.make_async_copy(src, dst, local_sem.at[k])

    def weight_in(k):
        ref = wbuf.at[aligned(1 - core, width), pl.ds((k // 2) * piece + (k % 2) * mine, mine)]
        pltpu.make_async_remote_copy(src_ref=ref, dst_ref=ref, send_sem=ps.at[rounds, k], recv_sem=pr.at[rounds, k], device_id={'wd': partner}, device_id_type=MESH).wait_recv()

    def normed(r, of):
        ref = nbuf.at[span(r), aligned(of, width)]
        return pltpu.make_async_remote_copy(src_ref=ref, dst_ref=ref, send_sem=ps.at[r, 0], recv_sem=pr.at[r, 0], device_id={'wd': partner}, device_id_type=MESH)

    def u_copy(r, of):
        ref = u_ref.at[span(r), aligned(of, mine)]
        return remote(ref, ref, ps.at[r, 1], pr.at[r, 1], {'wd': partner})

    def part_of(dest, r, part):
        return pbuf.at[span(r, part), aligned(dest, piece)]

    def x_send(k, r):
        rows = pl.ds(r * half, half)
        dest, part, dst, to = [
            (opp, first, opp_buf.at[0, rows], right), (opp, second, opp_buf.at[1, rows], left),
            (right, second, side.at[0, span(r, second)], right), (left, first, side.at[1, span(r, first)], left),
            (right, first, side.at[0, span(r, first)], right), (left, second, side.at[1, span(r, second)], left)][k]
        return remote(part_of(dest, r, part), dst, xs.at[r, k], xr.at[r, k], {'wd': to * CORES + core})

    def norm(r):
        for i in range(rr // LANES):
            tile = r * (rr // LANES) + i
            factor = as_column(scale[tile:tile + 1, :])[:, 0:1]
            rows = slice(tile * LANES, (tile + 1) * LANES)
            nbuf[rows, aligned(core, width)] = (x_ref[rows, :].astype(F32) * factor * gain).astype(BF16)
        normed(r, core).start()

    def dots(r):
        normed(r, 1 - core).wait_recv()
        step_rows = rr // 4

        def one(i, carry):
            rows = pl.ds(pl.multiple_of(r * rr + i * step_rows, step_rows), step_rows)
            pbuf[rows, :] = jnp.dot(nbuf[rows, :], wbuf[...], preferred_element_type=F32).astype(BF16)
            return carry
        lax.fori_loop(0, 4, one, 0)
        for k in range(4):
            x_send(k, r).start()

    def combine(r):
        rows = pl.ds(r * half, half)
        for k, dest, part, back in ((0, right, first, 4), (1, left, second, 5)):
            x_send(k, r).wait_recv()
            at = (span(r, part), aligned(dest, piece))
            pbuf[at] = (pbuf[at].astype(F32) + opp_buf[k, rows, :].astype(F32)).astype(BF16)
            x_send(back, r).start()

    def final(r):
        for k in range(2, 6):
            x_send(k, r).wait_recv()
        rows = span(r)
        total = pbuf[rows, aligned(chip, piece)].astype(F32) + side[0, rows, :].astype(F32) + side[1, rows, :].astype(F32)
        b_x, b_y = (vec_ref[:, pl.ds(pl.multiple_of(offs[name] + wd * mine, mine), mine)] for name in ('bias_x', 'bias_y'))
        u_ref[rows, aligned(core, mine)] = (total[:, :mine] + b_x).astype(BF16)
        u_copy(r, core).start()
        y_ref[rows, :] = jax.nn.gelu(total[:, mine:] + b_y, approximate=True).astype(BF16)

    wide = CORES * mine
    tile = tokens // SEGS
    pitch = tile + PAD
    per_seg = tile // LANES
    per_round = rr // LANES
    n_taps = offs['taps']

    def vec(name, index, size):
        return vec_ref[:, pl.ds(pl.multiple_of(offs[name] + index * size, size), size)]

    taps = [vec_ref[:, pl.ds(pl.multiple_of(offs['conv_w'] + k * offs['rnn'] + chip * wide, wide), wide)] for k in range(n_taps)]
    cbias = vec('conv_bias', chip, wide)
    gate_b = jnp.concatenate([vec('rgate_b', wd, mine), vec('igate_b', wd, mine)], axis=1)
    lam = -vec('lam_param', wd, mine)
    soft = -8.0 * (jnp.maximum(lam, 0.0) + jnp.log(1.0 + jnp.exp(-jnp.abs(lam))))

    def gates(r):
        u_copy(r, 1 - core).wait_recv()

        def widen(i, carry):
            rows = pl.multiple_of(i * LANES, LANES)
            u32[pl.ds(rows + PAD, LANES), :] = u_ref[pl.ds(rows, LANES), :].astype(F32)
            return carry
        lax.fori_loop(r * per_round, (r + 1) * per_round, widen, 0)

        def one(i, carry):
            rows = pl.multiple_of(i * LANES, LANES)
            window = u32[pl.ds(rows, LANES + PAD), :]
            pos = as_column(pos_ref[:, pl.ds(rows, LANES)].astype(F32))
            pair = jnp.concatenate([pos, pos], axis=1)
            total = cbias + window[PAD:] * taps[0]
            for k in range(1, n_taps):
                total = total + jnp.where(pair >= k, window[PAD - k:PAD - k + LANES], 0.0) * taps[k]
            conv = total.astype(BF16)
            both = jax.nn.sigmoid(jnp.dot(conv, gate_w[...], preferred_element_type=F32) + gate_b)
            log_a = both[:, :mine] * soft
            reset = pos == 0
            decay = jnp.where(reset, 0.0, jnp.exp(log_a))
            scale = jnp.where(reset, 1.0, jnp.sqrt(neg_expm1(2.0 * log_a)))
            held = conv.astype(F32)
            drive = scale * both[:, mine:] * jnp.where(core == 0, held[:, :mine], held[:, mine:])
            seg = i // per_seg
            at = pl.multiple_of(seg * pitch + (i - seg * per_seg) * LANES, PAD)
            a_s[pl.ds(at, LANES), :] = decay
            b_s[pl.ds(at, LANES), :] = drive
            return carry
        lax.fori_loop(r * per_round, (r + 1) * per_round, one, 0)

    def scan():
        def steps(i, carry):
            hid, acc = carry
            for j in range(8):
                at = pl.ds(i * 8 + j, SEGS, stride=pitch)
                a = a_s[at, :]
                hid = a * hid + b_s[at, :]
                acc = a * acc
                b_s[at, :] = hid
                a_s[at, :] = acc
            return hid, acc
        hid, acc = lax.fori_loop(0, tile // 8, steps, (jnp.zeros((SEGS, mine), F32), jnp.ones((SEGS, mine), F32)))
        entry = jnp.zeros((1, mine), F32)
        for seg in range(SEGS):
            for q in range(per_seg):
                at = seg * pitch + q * LANES
                hidden = b_s[at:at + LANES, :] + a_s[at:at + LANES, :] * entry
                rows = slice(seg * tile + q * LANES, seg * tile + (q + 1) * LANES)
                out_ref[rows, :] = (hidden * y_ref[rows, :].astype(F32)).astype(BF16)
            entry = hid[seg:seg + 1] + acc[seg:seg + 1] * entry

    ready = greet([{'wd': lax.rem(wd + step, wd_count)} for step in range(1, wd_count)])
    for k in range(2 * ring_x):
        weight_own(k).start()
    row_sums(x_ref, sums)
    all_sums[wd] = sums[...]
    ready()
    for one in sum_copies(sums, all_sums, ss, sr):
        one.start()
    for k in range(2 * ring_x):
        weight_out(k).start()
    moves, later = swaps(wg_ref, part_g, 0, ws.at[0], wr.at[0]), swaps(wu_ref, part_u, 0, ws.at[1], wr.at[1])
    for one in moves:
        one.start()
    gate_w[:, :mine] = rg_ref[chip, :, aligned(core, mine)]
    gate_w[:, mine:] = ig_ref[chip, :, aligned(core, mine)]
    u32[0:PAD, :] = jnp.zeros((PAD, wide), F32)
    for one in sum_copies(sums, all_sums, ss, sr):
        one.wait()
    scale = lax.rsqrt(jnp.sum(all_sums[...], axis=0) / (width * wd_count) + EPS)
    gain = 1.0 + vec_ref[:, offs['gain_temporal']:offs['gain_temporal'] + width]
    norm(0)
    for k in range(2 * ring_x):
        weight_own(k).wait()
        weight_in(k)
    for r in range(rounds):
        if r + 1 < rounds:
            norm(r + 1)
        dots(r)
        if r >= 1:
            combine(r - 1)
        if r >= 2:
            final(r - 2)
        if r >= 3:
            gates(r - 3)
    combine(rounds - 1)
    for one in later:
        one.start()
    final(rounds - 2)
    gates(rounds - 3)
    final(rounds - 1)
    gates(rounds - 2)
    gates(rounds - 1)
    scan()
    for k in range(2 * ring_x):
        weight_out(k).wait_send()
    for r in range(rounds):
        normed(r, core).wait_send()
        u_copy(r, core).wait_send()
        for k in range(6):
            x_send(k, r).wait_send()
    for one in moves + later:
        one.wait()


def front(offs, x, vec, pos, rgate_w, igate_w, w_x, w_y, w_g, w_u, part, ring_x, rounds, cid):
    tokens, width = x.shape
    rnn = w_x.shape[1]
    mine = rnn // (ring_x * CORES)
    wide = CORES * mine
    seg_rows = SEGS * (tokens // SEGS + PAD)
    return pl.pallas_call(
        functools.partial(front_kernel, rounds, offs),
        out_shape=(jax.ShapeDtypeStruct((tokens, mine), BF16), part, part),
        in_specs=[VMEM] * 5 + [ANY] * 4,
        out_specs=(VMEM, ANY, ANY),
        scratch_shapes=[
            pltpu.VMEM((tokens, CORES * width), BF16),
            pltpu.VMEM((CORES * width, rnn), BF16),
            pltpu.VMEM((tokens, rnn), BF16),
            pltpu.VMEM((2, tokens // 2, wide), BF16),
            pltpu.VMEM((2, tokens, wide), BF16),
            pltpu.VMEM((tokens, wide), BF16),
            pltpu.VMEM((tokens, mine), BF16),
            pltpu.VMEM((tokens + PAD, wide), F32),
            pltpu.VMEM((seg_rows, mine), F32),
            pltpu.VMEM((seg_rows, mine), F32),
            pltpu.VMEM((wide, wide), BF16),
            pltpu.VMEM((tokens // LANES, LANES), F32),
            pltpu.VMEM((ring_x * CORES, tokens // LANES, LANES), F32),
            DMA((2 * ring_x,)), DMA((rounds + 1, 2 * ring_x)), DMA((rounds + 1, 2 * ring_x)), DMA((rounds, 6)), DMA((rounds, 6)),
            DMA((ring_x * CORES,)), DMA((ring_x * CORES,)), DMA((2, ring_x)), DMA((2, ring_x)),
        ],
        compiler_params=pltpu.CompilerParams(collective_id=cid, has_side_effects=True, vmem_limit_bytes=GRANT),
        name='front',
    )(x, vec, pos, rgate_w, igate_w, w_x, w_y, w_g, w_u)


def solution(mesh):
    wd_count = mesh.shape['wd']
    ch_count = mesh.shape['ch']
    chips = wd_count // CORES
    row_spec = P('dp', 'wd')
    specs = (row_spec, P('dp', None), P('wd'), P('wd', 'ch'), P('ch'), P('wd', 'ch'), P('ch'), P(None, 'ch'), P('ch'), P('ch'), P('ch', None, None), P('ch'), P('ch', None, None), P('ch'), P('ch', 'wd'), P('wd'), P('wd'), P('wd', 'ch'), P('ch'), P('wd', 'ch'), P('ch'), P('ch', 'wd'), P('wd'))

    def local_layer(resid_in, seg_pos, gain_temporal, w_x, bias_x, w_y, bias_y, conv_w, conv_bias, lam_param, rgate_w, rgate_b, igate_w, igate_b, w_o, bias_o, gain_mlp, w_g, bias_g, w_u, bias_u, w_d, bias_d):
        small = {'gain_temporal': gain_temporal, 'bias_x': bias_x, 'bias_y': bias_y, 'conv_w': conv_w, 'conv_bias': conv_bias, 'lam_param': lam_param, 'rgate_b': rgate_b,
                 'igate_b': igate_b, 'bias_o': bias_o, 'gain_mlp': gain_mlp, 'bias_g': bias_g, 'bias_u': bias_u, 'bias_d': bias_d}
        offs = {'rnn': w_x.shape[1], 'taps': conv_w.shape[0]}
        end = 0
        for name, val in sorted(small.items(), key=lambda item: -item[1].size):
            offs[name] = end
            end += val.size
        spread = [lax.pad(small[name].astype(F32).reshape(-1), jnp.zeros((), F32), [(offs[name], end - offs[name] - small[name].size, 0)]) for name in small]
        vec = functools.reduce(jnp.add, spread).reshape(1, end)
        tokens = resid_in.shape[0]
        part = jax.ShapeDtypeStruct((chips * w_g.shape[0], w_g.shape[1] // wd_count), BF16)
        mixed, g0, u0 = front(offs, resid_in, vec, seg_pos.reshape(1, tokens), rgate_w, igate_w, w_x, w_y, w_g, w_u, part, chips, 8, 1)
        inner, resid = mid(offs, mixed, w_o, resid_in, vec, w_g, w_u, (g0, u0), chips, ch_count, 4, 2)
        return mlp_out(inner, w_d, resid, vec, offs['bias_d'], ch_count, 16, 3)

    return jax.shard_map(local_layer, mesh=mesh, in_specs=specs, out_specs=row_spec, check_vma=False)
```

time: 470 us -> 431 us (0.917)
  Pallas kernels: 451 us -> 424 us
  other arithmetic: 8.24 us -> 1.46 us
  local copies, waits for them, and re-layouts: 10 us -> 5.17 us
    pallas_call x4 -> x2, Pallas kernels: 352 us -> 309 us  [the longest x1 180 us: mid(): pl.pallas_call(functools.partial(mid_kernel, rounds, offs), out_shape=(ja...]
    pallas_call x1, Pallas kernels: 99.4 us -> 115 us  [front(): pl.pallas_call(functools.partial(front_kernel, rounds, offs), out_shape=(...]
    unnamed x11 -> x0, other arithmetic: 7.56 us -> none
    unnamed x19 -> x2, local copies, waits for them, and re-layouts: 10 us -> 5.17 us
where the time goes in v6:
time: 431 us
  Pallas kernels  424 us (98%)
  local copies, waits for them, and re-layouts  5.17 us (1%)
    pallas_call x1, Pallas kernels, mid(): pl.pallas_call(functools.partial(mid_kernel, rounds, offs), out_shape=(ja...  180 us
    pallas_call x1, Pallas kernels, mlp_out(): pl.pallas_call(functools.partial(mlp_out_kernel, rounds, bias_at), out_sh...  129 us
    pallas_call x1, Pallas kernels, front(): pl.pallas_call(functools.partial(front_kernel, rounds, offs), out_shape=(...  115 us

profile of v6, /device:TPU:97, one launch (start us, length us, event | category | flops | bytes accessed | tf_op | source)
XLA Modules:
  0.0 430.5 jit_solution(10808801537952370093)
XLA Ops:
  0.0 0.7 copy.26
  0.7 1.5 convert_add_fusion
  2.2 114.8 %front.1 = (bf16[4096,128]{1,0:T(8,128)(2,1)}, bf16[2048,384]{1,0:T(8,128)(2,1)}, bf16[2048,384]{1,0:T(8,128)(2,1)}) custom-call(bf16[4096,512]{1,0:T(8,128)(2,1)} %x_ref.3, f32[1,18432]{1,0:T(1,128)} %bitcast.8, s32[1,4096]{1,0:T(1,128)} %pos_ref.1, bf16[4,256,256]{2,1,0:T(8,128)(2,1)} %rg_ref.1, bf16[4,256,256]{2,1,0:T(8,128)(2,1)} %ig_ref.1, ...), custom_call_target="tpu_custom_call" | custom-call | tf_op jit(solution)/shard_map/front/pallas_call | solution.py:695
  117.0 180.5 %mid.1 = (bf16[4,1024,384]{2,1,0:T(8,128)(2,1)}, f32[1024,512]{1,0:T(8,128)}) custom-call(bf16[4,1024,128]{2,1,0:T(8,128)(2,1)} %bitcast.11, bf16[1024,512]{1,0:T(8,128)(2,1)} %w_o_ref.1, bf16[4096,512]{1,0:T(8,128)(2,1)} %x_ref.3, f32[1,18432]{1,0:T(1,128)} %bitcast.9, bf16[512,3072]{1,0:T(8,128)(2,1)} %wg_ref.3, bf16[512,3072]{1,0:T(8,128)(2,1)} %wu_ref.3, ...), custom_call_target="tpu_custom_call" | custom-call | tf_op jit(solution)/shard_map/mid/pallas_call | solution.py:453
  297.5 128.5 %mlp_out.1 = bf16[4,1024,512]{2,1,0:T(8,128)(2,1)} custom-call(bf16[4,1024,384]{2,1,0:T(8,128)(2,1)} %get-tuple-element.13.h_ref, bf16[3072,512]{1,0:T(8,128)(2,1)} %w_in_ref.1, f32[1024,512]{1,0:T(8,128)} %get-tuple-element.14.resid_ref, f32[1,18432]{1,0:T(1,128)} %bitcast.10), custom_call_target="tpu_custom_call" | custom-call | tf_op jit(solution)/shard_map/mlp_out/pallas_call | solution.py:275
  426.0 4.5 %copy.28 = bf16[4096,512]{1,0:T(8,128)(2,1)} copy(bf16[4096,512]{1,0:T(8,128)(2,1)} %bitcast.7) | data formatting | bytes 8388608

commit v7 on v6

--- a/solution.py
+++ b/solution.py
@@ -474,7 +474,7 @@
     )(h.reshape(ring_y, share, h.shape[1]), w_o, x, vec, w_g, w_u, *parts)
 
 
-def front_kernel(rounds, offs, x_ref, vec_ref, pos_ref, rg_ref, ig_ref, w_x_ref, w_y_ref, wg_ref, wu_ref, out_ref, part_g, part_u, nbuf, wbuf, pbuf, opp_buf, side, u_ref, y_ref, u32, a_s, b_s, gate_w, sums, all_sums, local_sem, ps, pr, xs, xr, ss, sr, ws, wr):
+def front_kernel(rounds, offs, x_in_ref, vec_ref, pos_ref, rg_ref, ig_ref, w_x_ref, w_y_ref, wg_ref, wu_ref, out_ref, part_g, part_u, x_ref, nbuf, wbuf, pbuf, opp_buf, side, u_ref, y_ref, u32, a_s, b_s, gate_w, sums, all_sums, local_sem, ps, pr, xs, xr, ss, sr, ws, wr, in_sem):
     tokens, width = x_ref.shape
     ring_x, _, _, wd, core, chip = where_am_i()
     wd_count = ring_x * CORES
@@ -632,21 +632,28 @@
                 out_ref[rows, :] = (hidden * y_ref[rows, :].astype(F32)).astype(BF16)
             entry = hid[seg:seg + 1] + acc[seg:seg + 1] * entry
 
+    x_load = pltpu.make_async_copy(x_in_ref, x_ref, in_sem.at[0])
+    x_load.start()
     ready = greet([{'wd': lax.rem(wd + step, wd_count)} for step in range(1, wd_count)])
+    gate_loads = [pltpu.make_async_copy(w.at[chip, :, aligned(core, mine)], gate_w.at[:, pl.ds(m * mine, mine)], in_sem.at[m + 1]) for m, w in enumerate((rg_ref, ig_ref))]
+    for one in gate_loads:
+        one.start()
     for k in range(2 * ring_x):
         weight_own(k).start()
+    moves, later = swaps(wg_ref, part_g, 0, ws.at[0], wr.at[0]), swaps(wu_ref, part_u, 0, ws.at[1], wr.at[1])
+    ready()
+    moves[RIGHT - 1].start()
+    moves[LEFT - 1].start()
+    x_load.wait()
     row_sums(x_ref, sums)
     all_sums[wd] = sums[...]
-    ready()
     for one in sum_copies(sums, all_sums, ss, sr):
         one.start()
     for k in range(2 * ring_x):
         weight_out(k).start()
-    moves, later = swaps(wg_ref, part_g, 0, ws.at[0], wr.at[0]), swaps(wu_ref, part_u, 0, ws.at[1], wr.at[1])
-    for one in moves:
-        one.start()
-    gate_w[:, :mine] = rg_ref[chip, :, aligned(core, mine)]
-    gate_w[:, mine:] = ig_ref[chip, :, aligned(core, mine)]
+    moves[OPP - 1].start()
+    for one in gate_loads:
+        one.wait()
     u32[0:PAD, :] = jnp.zeros((PAD, wide), F32)
     for one in sum_copies(sums, all_sums, ss, sr):
         one.wait()
@@ -695,9 +702,10 @@
     return pl.pallas_call(
         functools.partial(front_kernel, rounds, offs),
         out_shape=(jax.ShapeDtypeStruct((tokens, mine), BF16), part, part),
-        in_specs=[VMEM] * 5 + [ANY] * 4,
+        in_specs=[ANY, VMEM, VMEM] + [ANY] * 6,
         out_specs=(VMEM, ANY, ANY),
         scratch_shapes=[
+            pltpu.VMEM((tokens, width), BF16),
             pltpu.VMEM((tokens, CORES * width), BF16),
             pltpu.VMEM((CORES * width, rnn), BF16),
             pltpu.VMEM((tokens, rnn), BF16),
@@ -712,11 +720,37 @@
             pltpu.VMEM((tokens // LANES, LANES), F32),
             pltpu.VMEM((ring_x * CORES, tokens // LANES, LANES), F32),
             DMA((2 * ring_x,)), DMA((rounds + 1, 2 * ring_x)), DMA((rounds + 1, 2 * ring_x)), DMA((rounds, 6)), DMA((rounds, 6)),
-            DMA((ring_x * CORES,)), DMA((ring_x * CORES,)), DMA((2, ring_x)), DMA((2, ring_x)),
+            DMA((ring_x * CORES,)), DMA((ring_x * CORES,)), DMA((2, ring_x)), DMA((2, ring_x)), DMA((3,)),
         ],
         compiler_params=pltpu.CompilerParams(collective_id=cid, has_side_effects=True, vmem_limit_bytes=GRANT),
         name='front',
     )(x, vec, pos, rgate_w, igate_w, w_x, w_y, w_g, w_u)
+
+
+def place_kernel(in_ref, out_ref, held, sems):
+    parts = held.shape[0]
+    ins = [pltpu.make_async_copy(in_ref.at[i], held.at[i], sems.at[0, i]) for i in range(parts)]
+    outs = [pltpu.make_async_copy(held.at[i], out_ref.at[i], sems.at[1, i]) for i in range(parts)]
+    for one in ins:
+        one.start()
+    for i in range(parts):
+        ins[i].wait()
+        outs[i].start()
+    for one in outs:
+        one.wait()
+
+
+def place(val, parts):
+    shape = (parts, val.shape[0] // parts, val.shape[1])
+    return pl.pallas_call(
+        place_kernel,
+        out_shape=jax.ShapeDtypeStruct(shape, val.dtype),
+        in_specs=[ANY],
+        out_specs=ANY,
+        scratch_shapes=[pltpu.VMEM(shape, val.dtype), DMA((2, parts))],
+        compiler_params=pltpu.CompilerParams(vmem_limit_bytes=GRANT),
+        name='place',
+    )(val.reshape(shape)).reshape(val.shape)
 
 
 def solution(mesh):
@@ -740,6 +774,6 @@
         part = jax.ShapeDtypeStruct((chips * w_g.shape[0], w_g.shape[1] // wd_count), BF16)
         mixed, g0, u0 = front(offs, resid_in, vec, seg_pos.reshape(1, tokens), rgate_w, igate_w, w_x, w_y, w_g, w_u, part, chips, 8, 1)
         inner, resid = mid(offs, mixed, w_o, resid_in, vec, w_g, w_u, (g0, u0), chips, ch_count, 4, 2)
-        return mlp_out(inner, w_d, resid, vec, offs['bias_d'], ch_count, 16, 3)
+        return place(mlp_out(inner, w_d, resid, vec, offs['bias_d'], ch_count, 16, 3), 8)
 
     return jax.shard_map(local_layer, mesh=mesh, in_specs=specs, out_specs=row_spec, check_vma=False)

time: 431 us -> 429 us (level)
  local copies, waits for them, and re-layouts: 5.17 us -> 0.7 us
    unnamed x2 -> x1, local copies, waits for them, and re-layouts: 5.17 us -> 0.7 us
where the time goes in v7:
time: 429 us; the launch traced here: 428 us
  Pallas kernels  426 us (99%)
    pallas_call x1, Pallas kernels, mid(): pl.pallas_call(functools.partial(mid_kernel, rounds, offs), out_shape=(ja...  181 us
    pallas_call x1, Pallas kernels, mlp_out(): pl.pallas_call(functools.partial(mlp_out_kernel, rounds, bias_at), out_sh...  128 us
    pallas_call x1, Pallas kernels, front(): pl.pallas_call(functools.partial(front_kernel, rounds, offs), out_shape=(...  113 us

profile of v7, /device:TPU:97, one launch (start us, length us, event | category | flops | bytes accessed | tf_op | source)
XLA Modules:
  0.0 428.5 jit_solution(4272858171461075856)
XLA Ops:
  0.0 0.7 copy.26
  0.7 1.5 convert_add_fusion
  2.2 113.2 %front.1 = (bf16[4096,128]{1,0:T(8,128)(2,1)}, bf16[2048,384]{1,0:T(8,128)(2,1)}, bf16[2048,384]{1,0:T(8,128)(2,1)}) custom-call(bf16[4096,512]{1,0:T(8,128)(2,1)} %x_ref.1, f32[1,18432]{1,0:T(1,128)} %bitcast.9, s32[1,4096]{1,0:T(1,128)} %pos_ref.1, bf16[4,256,256]{2,1,0:T(8,128)(2,1)} %rg_ref.1, bf16[4,256,256]{2,1,0:T(8,128)(2,1)} %ig_ref.1, ...), custom_call_target="tpu_custom_call" | custom-call | tf_op jit(solution)/shard_map/front/pallas_call | solution.py:702
  115.4 180.9 %mid.1 = (bf16[4,1024,384]{2,1,0:T(8,128)(2,1)}, f32[1024,512]{1,0:T(8,128)}) custom-call(bf16[4,1024,128]{2,1,0:T(8,128)(2,1)} %bitcast.12, bf16[1024,512]{1,0:T(8,128)(2,1)} %w_o_ref.1, bf16[4096,512]{1,0:T(8,128)(2,1)} %x_ref.1, f32[1,18432]{1,0:T(1,128)} %bitcast.10, bf16[512,3072]{1,0:T(8,128)(2,1)} %wg_ref.3, bf16[512,3072]{1,0:T(8,128)(2,1)} %wu_ref.3, ...), custom_call_target="tpu_custom_call" | custom-call | tf_op jit(solution)/shard_map/mid/pallas_call | solution.py:453
  296.3 128.4 %mlp_out.1 = bf16[4,1024,512]{2,1,0:T(8,128)(2,1)} custom-call(bf16[4,1024,384]{2,1,0:T(8,128)(2,1)} %get-tuple-element.13.h_ref, bf16[3072,512]{1,0:T(8,128)(2,1)} %w_in_ref.1, f32[1024,512]{1,0:T(8,128)} %get-tuple-element.14.resid_ref, f32[1,18432]{1,0:T(1,128)} %bitcast.11), custom_call_target="tpu_custom_call" | custom-call | tf_op jit(solution)/shard_map/mlp_out/pallas_call | solution.py:275
  424.7 3.6 place.1

commit v8 on v7

--- a/solution.py
+++ b/solution.py
@@ -294,13 +294,18 @@
     partner = wd + 1 - 2 * core
     ff = out_ref.shape[2]
 
-    def device(d1, d2):
-        return {'ch': lax.rem(ch + d1 * (1 - core) + d2 * core, ring_y), 'wd': lax.rem(chip + d1 * core + d2 * (1 - core), ring_x) * CORES + core}
+    def turned(r, d1, d2):
+        flip = core if r % 2 == 0 else 1 - core
+        return lax.rem(ch + d1 * (1 - flip) + d2 * flip, ring_y), lax.rem(chip + d1 * flip + d2 * (1 - flip), ring_x)
+
+    def device(r, d1, d2):
+        at_y, at_x = turned(r, d1, d2)
+        return {'ch': at_y, 'wd': at_x * CORES + core}
 
     def block(d1, d2, r, part=None):
         rows = pl.ds(r * rr, rr) if part is None else pl.ds(r * rr + part * half, half)
-        at = lax.rem(chip + d1 * core + d2 * (1 - core), ring_x)
-        return nbuf.at[lax.rem(ch + d1 * (1 - core) + d2 * core, ring_y), rows, aligned(at, width)]
+        at_y, at_x = turned(r, d1, d2)
+        return nbuf.at[at_y, rows, aligned(at_x, width)]
 
     whole = None
     plan = [((0, 0), (RIGHT, 0), (LEFT, 0), whole), ((0, 0), (LEFT, 0), (RIGHT, 0), whole),
@@ -313,7 +318,7 @@
     def copy(k, r):
         src, to, _, part = plan[k]
         ref = block(*src, r, part)
-        return remote(ref, ref, ns.at[r, k], nr.at[r, k], device(*to))
+        return remote(ref, ref, ns.at[r, k], nr.at[r, k], device(r, *to))
 
     def start(r, *ks):
         for k in ks:
@@ -322,7 +327,7 @@
     def wait(r, *ks):
         for k in ks:
             ref = block(*plan[k][2], r, plan[k][3])
-            remote(ref, ref, ns.at[r, k], nr.at[r, k], device(RIGHT, 0)).wait_recv()
+            remote(ref, ref, ns.at[r, k], nr.at[r, k], device(r, RIGHT, 0)).wait_recv()
 
     def own(r):
         if r < rounds:

time: 429 us -> 427 us (level)
  no operation moved by 1% of the time
where the time goes in v8:
time: 427 us
  Pallas kernels  425 us (100%)
    pallas_call x1, Pallas kernels, mid(): pl.pallas_call(functools.partial(mid_kernel, rounds, offs), out_shape=(ja...  180 us
    pallas_call x1, Pallas kernels, mlp_out(): pl.pallas_call(functools.partial(mlp_out_kernel, rounds, bias_at), out_sh...  127 us
    pallas_call x1, Pallas kernels, front(): pl.pallas_call(functools.partial(front_kernel, rounds, offs), out_shape=(...  113 us

profile of v8, /device:TPU:97, one launch (start us, length us, event | category | flops | bytes accessed | tf_op | source)
XLA Modules:
  0.0 427.2 jit_solution(6888328900998077309)
XLA Ops:
  0.0 0.7 copy.26
  0.7 1.5 convert_add_fusion
  2.2 113.2 %front.1 = (bf16[4096,128]{1,0:T(8,128)(2,1)}, bf16[2048,384]{1,0:T(8,128)(2,1)}, bf16[2048,384]{1,0:T(8,128)(2,1)}) custom-call(bf16[4096,512]{1,0:T(8,128)(2,1)} %x_ref.1, f32[1,18432]{1,0:T(1,128)} %bitcast.9, s32[1,4096]{1,0:T(1,128)} %pos_ref.1, bf16[4,256,256]{2,1,0:T(8,128)(2,1)} %rg_ref.1, bf16[4,256,256]{2,1,0:T(8,128)(2,1)} %ig_ref.1, ...), custom_call_target="tpu_custom_call" | custom-call | tf_op jit(solution)/shard_map/front/pallas_call | solution.py:707
  115.4 180.5 %mid.1 = (bf16[4,1024,384]{2,1,0:T(8,128)(2,1)}, f32[1024,512]{1,0:T(8,128)}) custom-call(bf16[4,1024,128]{2,1,0:T(8,128)(2,1)} %bitcast.12, bf16[1024,512]{1,0:T(8,128)(2,1)} %w_o_ref.1, bf16[4096,512]{1,0:T(8,128)(2,1)} %x_ref.1, f32[1,18432]{1,0:T(1,128)} %bitcast.10, bf16[512,3072]{1,0:T(8,128)(2,1)} %wg_ref.3, bf16[512,3072]{1,0:T(8,128)(2,1)} %wu_ref.3, ...), custom_call_target="tpu_custom_call" | custom-call | tf_op jit(solution)/shard_map/mid/pallas_call | solution.py:458
  295.9 127.5 %mlp_out.1 = bf16[4,1024,512]{2,1,0:T(8,128)(2,1)} custom-call(bf16[4,1024,384]{2,1,0:T(8,128)(2,1)} %get-tuple-element.13.h_ref, bf16[3072,512]{1,0:T(8,128)(2,1)} %w_in_ref.1, f32[1024,512]{1,0:T(8,128)} %get-tuple-element.14.resid_ref, f32[1,18432]{1,0:T(1,128)} %bitcast.11), custom_call_target="tpu_custom_call" | custom-call | tf_op jit(solution)/shard_map/mlp_out/pallas_call | solution.py:275
  423.4 3.6 place.1
